TPU v7x, 256 devices: a whole 4x4x8 slice. The times are simulated.
256 devices in a mesh: stage: 4 (over x), expert: 64 (over z, y, core).
Axes of the slice: x: 4, y: 4, z: 8, core: 2. Of those that a mesh axis runs over, the one named last changes fastest.
Arguments:
- x_acts: bfloat16 [2, 4, 32768, 512], P(None, 'stage', 'expert')
- expert_ids: int32 [2, 4, 32768, 8], P(None, 'stage', 'expert')
- gate_wts: float32 [2, 4, 32768, 8], P(None, 'stage', 'expert')
- w_in: bfloat16 [4, 64, 512, 256], P('stage', 'expert')
- w_up: bfloat16 [4, 64, 512, 256], P('stage', 'expert')
- w_out: bfloat16 [4, 64, 256, 512], P('stage', 'expert')
- d_out: bfloat16 [4, 32768, 512], P('stage', 'expert')
Outputs:
- output 1: bfloat16 [4, 32768, 512], P('stage', 'expert')
- output 2: bfloat16 [4, 32768, 512], P('stage', 'expert')
- output 3: bfloat16 [4, 64, 512, 256], P('stage', 'expert')
- output 4: bfloat16 [4, 64, 512, 256], P('stage', 'expert')
- output 5: bfloat16 [4, 64, 256, 512], P('stage', 'expert')
All inputs are finite; a program needn't handle non-finite values.
Results may differ from a plain program's by a relative error of at most 0.001.
Values are sent between devices in bfloat16 or wider.
A program may use at most 768 MiB of HBM per device.

v0:
```python
import jax
import jax.numpy as jnp
from jax import lax
from jax.sharding import PartitionSpec as P


def slot_onehot(expert_ids, gate_wts, num_experts, capacity):
    chosen = expert_ids[..., None] == jnp.arange(num_experts, dtype=jnp.int32)
    taken = jnp.any(chosen, axis=-2)
    gate_tok = jnp.sum(jnp.where(chosen, gate_wts[..., None], 0.0), axis=-2)
    slot_rank = jnp.cumsum(taken.astype(jnp.int32), axis=-2) - 1
    slot_hit = taken[..., None] & (slot_rank[..., None] == jnp.arange(capacity, dtype=jnp.int32))
    gate_slot = jnp.sum(jnp.where(slot_hit, gate_tok[..., None], 0.0), axis=-3)
    return slot_hit.astype(jnp.bfloat16), gate_slot


def expert_forward(x_rows, gate_rows, w_in, w_up, w_out):
    pre_in = jnp.einsum('ecd,edf->ecf', x_rows, w_in, preferred_element_type=jnp.float32)
    pre_up = jnp.einsum('ecd,edf->ecf', x_rows, w_up, preferred_element_type=jnp.float32)
    hidden = (jax.nn.silu(pre_in) * pre_up).astype(jnp.bfloat16)
    expert_out = jnp.einsum('ecf,efd->ecd', hidden, w_out, preferred_element_type=jnp.float32)
    return (gate_rows[..., None] * expert_out).astype(jnp.bfloat16)


def expert_backward(x_rows, dy_rows, gate_rows, w_in, w_up, w_out):
    pre_in = jnp.einsum('ecd,edf->ecf', x_rows, w_in, preferred_element_type=jnp.float32)
    pre_up = jnp.einsum('ecd,edf->ecf', x_rows, w_up, preferred_element_type=jnp.float32)
    sig_in = jax.nn.sigmoid(pre_in)
    act_in = pre_in * sig_in
    hidden = (act_in * pre_up).astype(jnp.bfloat16)
    gated_dy = (gate_rows[..., None] * dy_rows).astype(jnp.bfloat16)
    d_hidden = jnp.einsum('ecd,efd->ecf', gated_dy, w_out, preferred_element_type=jnp.float32)
    d_pre_in = (d_hidden * pre_up * sig_in * (1.0 + pre_in * (1.0 - sig_in))).astype(jnp.bfloat16)
    d_pre_up = (d_hidden * act_in).astype(jnp.bfloat16)
    dw_out = jnp.einsum('ecf,ecd->efd', hidden, gated_dy, preferred_element_type=jnp.float32)
    dw_in = jnp.einsum('ecd,ecf->edf', x_rows, d_pre_in, preferred_element_type=jnp.float32)
    dw_up = jnp.einsum('ecd,ecf->edf', x_rows, d_pre_up, preferred_element_type=jnp.float32)
    dx_rows = (jnp.einsum('ecf,edf->ecd', d_pre_in, w_in, preferred_element_type=jnp.float32)
               + jnp.einsum('ecf,edf->ecd', d_pre_up, w_up, preferred_element_type=jnp.float32))
    return (dx_rows.astype(jnp.bfloat16), dw_in.astype(jnp.bfloat16),
            dw_up.astype(jnp.bfloat16), dw_out.astype(jnp.bfloat16))


def solution(mesh):
    group_size = mesh.shape['expert']
    num_stages = mesh.shape['stage']
    to_next = [(src_idx, (src_idx + 1) % num_stages) for src_idx in range(num_stages)]
    to_prev = [((src_idx + 1) % num_stages, src_idx) for src_idx in range(num_stages)]

    def device_fn(x_acts, expert_ids, gate_wts, w_in, w_up, w_out, d_out):
        local_experts = w_in.shape[1]
        num_experts = local_experts * group_size
        tokens = x_acts.shape[2]
        top_k = expert_ids.shape[3]
        capacity = 3 * top_k * tokens // (2 * num_experts)
        w_in_loc, w_up_loc, w_out_loc = w_in[0], w_up[0], w_out[0]

        def dispatch(slot_buf):
            row_tail = slot_buf.shape[2:]
            split_buf = slot_buf.reshape((group_size, local_experts, capacity) + row_tail)
            received = lax.all_to_all(split_buf, 'expert', 0, 2, tiled=True)
            return received.reshape((local_experts, group_size * capacity) + row_tail)

        def collect(slot_buf):
            row_tail = slot_buf.shape[2:]
            split_buf = slot_buf.reshape((1, local_experts, group_size * capacity) + row_tail)
            received = lax.all_to_all(split_buf, 'expert', 2, 0, tiled=True)
            return received.reshape((num_experts, capacity) + row_tail)

        def to_slots(slot_hit, tok_rows):
            slot_buf = jnp.einsum('uec,ud->ecd', slot_hit, tok_rows, preferred_element_type=jnp.float32)
            return slot_buf.astype(jnp.bfloat16)

        def to_tokens(slot_hit, slot_buf):
            tok_rows = jnp.einsum('uec,ecd->ud', slot_hit, slot_buf, preferred_element_type=jnp.float32)
            return tok_rows.astype(jnp.bfloat16)

        x_fwd = lax.ppermute(x_acts[1, 0], 'stage', to_next)
        ids_fwd = lax.ppermute(expert_ids[1, 0], 'stage', to_next)
        gate_fwd = lax.ppermute(gate_wts[1, 0], 'stage', to_next)
        hit_fwd, gslot_fwd = slot_onehot(ids_fwd, gate_fwd, num_experts, capacity)
        x_recv = dispatch(to_slots(hit_fwd, x_fwd))
        gate_recv = dispatch(gslot_fwd)
        y_back = collect(expert_forward(x_recv, gate_recv, w_in_loc, w_up_loc, w_out_loc))
        y_dev = to_tokens(hit_fwd, y_back)

        x_bwd = lax.ppermute(x_acts[0, 0], 'stage', to_next)
        ids_bwd = lax.ppermute(expert_ids[0, 0], 'stage', to_next)
        gate_bwd = lax.ppermute(gate_wts[0, 0], 'stage', to_next)
        hit_bwd, gslot_bwd = slot_onehot(ids_bwd, gate_bwd, num_experts, capacity)
        x_recv_b = dispatch(to_slots(hit_bwd, x_bwd))
        dy_recv = dispatch(to_slots(hit_bwd, d_out[0]))
        gate_recv_b = dispatch(gslot_bwd)
        dx_rows, dw_in, dw_up, dw_out = expert_backward(
            x_recv_b, dy_recv, gate_recv_b, w_in_loc, w_up_loc, w_out_loc)
        dx_here = to_tokens(hit_bwd, collect(dx_rows))
        dx_dev = lax.ppermute(dx_here, 'stage', to_prev)
        return y_dev[None], dx_dev[None], dw_in[None], dw_up[None], dw_out[None]

    tok_spec = P(None, 'stage', 'expert', None)
    w_spec = P('stage', 'expert', None, None)
    row_spec = P('stage', 'expert', None)
    return jax.shard_map(device_fn, mesh=mesh,
                         in_specs=(tok_spec, tok_spec, tok_spec, w_spec, w_spec, w_spec, row_spec),
                         out_specs=(row_spec, row_spec, w_spec, w_spec, w_spec), check_vma=False)
```

profile of v0, /device:TPU:1, one launch (start us, length us, event | category | flops | bytes accessed | tf_op | source)
XLA Modules:
  0.0 871.4 jit_solution(6775999961160183844)
XLA Ops:
  13.8 14.3 %all-to-all-start = ((f32[64,1,96]{2,1,0:T(1,128)}), f32[64,1,96]{2,1,0:T(1,128)S(1)}, u32[]{:S(2)}, u32[]{:S(2)}) async-start(f32[64,1,96]{2,1,0:T(1,128)} %bitcast.4), calls=%async_computation | async-start | bytes 65536 | tf_op jit(solution)/shard_map/all_to_all | solution.py:61
  60.1 14.3 %collective-permute-done.2 = bf16[512,512]{1,0:T(8,128)(2,1)S(1)} collective-permute-done((bf16[512,512]{1,0:T(8,128)(2,1)S(1)}, bf16[512,512]{1,0:T(8,128)(2,1)S(1)}, u32[]{:S(2)}, u32[]{:S(2)}) %collective-permute-start.2) | collective-permute-done | bytes 524320 | tf_op jit(solution)/shard_map/ppermute | solution.py:78
  79.8 124.2 %all-to-all-done.4 = bf16[64,1,96,512]{3,2,1,0:T(8,128)(2,1)} async-done(((bf16[64,1,96,512]{3,2,1,0:T(8,128)(2,1)}), bf16[64,1,96,512]{3,2,1,0:T(8,128)(2,1)}, u32[]{:S(2)}, u32[]{:S(2)}) %all-to-all-start.4) | async-done | bytes 6291488 | tf_op jit(solution)/shard_map/all_to_all | solution.py:61
  210.4 14.3 %collective-permute-done.5 = bf16[512,512]{1,0:T(8,128)(2,1)S(1)} collective-permute-done((bf16[512,512]{1,0:T(8,128)(2,1)S(1)}, bf16[512,512]{1,0:T(8,128)(2,1)S(1)}, u32[]{:S(2)}, u32[]{:S(2)}) %collective-permute-start.5) | collective-permute-done | bytes 524320 | tf_op jit(solution)/shard_map/ppermute | solution.py:87
  230.1 124.2 %all-to-all-done.1 = bf16[64,1,96,512]{3,2,1,0:T(8,128)(2,1)} async-done(((bf16[64,1,96,512]{3,2,1,0:T(8,128)(2,1)}), bf16[64,1,96,512]{3,2,1,0:T(8,128)(2,1)}, u32[]{:S(2)}, u32[]{:S(2)}) %all-to-all-start.1) | async-done | bytes 6291488 | tf_op jit(solution)/shard_map/all_to_all | solution.py:61
  362.6 7.3 fusion.74
  369.9 10.2 %fusion.14 = bf16[1,1,6144,512]{3,2,1,0:T(8,128)(2,1)} fusion(f32[6144]{0:T(1024)S(1)} %mul.80, bf16[6144,512]{1,0:T(8,128)(2,1)} %bitcast.9, f32[6144,256]{1,0:T(8,128)} %fusion.74, bf16[1,1,256,512]{3,2,1,0:T(8,128)(2,1)S(1)} %copy-done.15, bf16[1,1,512,256]{3,2,1,0:T(8,128)(2,1)S(1)} %copy-done.9), kind=kOutput, calls=%fused_computation.17 | convolution fusion | flops 3236954112 | bytes 19423232 | tf_op jit(solution)/shard_map/ecf,efd->ecd/dot_general | solution.py:21
  380.1 12.0 %copy.72 = bf16[1,1,6144,512]{3,1,0,2:T(2,128)(2,1)} copy(bf16[1,1,6144,512]{3,2,1,0:T(8,128)(2,1)} %fusion.14) | data formatting | bytes 12582912 | tf_op jit(solution)/shard_map/reshape | solution.py:66
  392.7 41.7 %reduce.12 = bf16[6144,512]{1,0:T(8,128)(2,1)} reduce(bf16[6144,1,1,512]{3,2,1,0:T(2,128)(2,1)} %bitcast.145, bf16[]{:T(256)} %broadcast.80), dimensions={1,2}, to_apply=%bitcast.142.reduce_sub_computation | reduce | bytes 12582914
  434.3 15.4 %reshape.324 = bf16[64,2,24576]{2,1,0:T(2,128)(2,1)} reshape(bf16[6144,512]{1,0:T(8,128)(2,1)} %reduce.12) | data formatting | bytes 12582912
  449.8 52.8 %all-to-all-done.5 = bf16[64,1,96,512]{3,2,1,0:T(8,128)(2,1)} async-done(((bf16[64,1,96,512]{3,2,1,0:T(8,128)(2,1)}), bf16[64,1,96,512]{3,2,1,0:T(8,128)(2,1)}, u32[]{:S(2)}, u32[]{:S(2)}) %all-to-all-start.5) | async-done | bytes 6291488 | tf_op jit(solution)/shard_map/all_to_all | solution.py:61
  502.5 8.6 all-to-all-start.2
  523.5 8.6 multiply_convert_fusion.3
  539.1 12.0 %copy.71 = bf16[1,1,6144,512]{3,1,0,2:T(2,128)(2,1)} copy(bf16[1,1,6144,512]{3,2,1,0:T(8,128)(2,1)} %fusion.13) | data formatting | bytes 12582912 | tf_op jit(solution)/shard_map/reshape | solution.py:66
  551.2 41.8 %reduce.13 = bf16[6144,512]{1,0:T(8,128)(2,1)} reduce(bf16[6144,1,1,512]{3,2,1,0:T(2,128)(2,1)} %bitcast.146, bf16[]{:T(256)} %broadcast.80), dimensions={1,2}, to_apply=%bitcast.141.reduce_sub_computation | reduce | bytes 12582914
  592.9 15.4 %reshape.326 = bf16[64,2,24576]{2,1,0:T(2,128)(2,1)} reshape(bf16[6144,512]{1,0:T(8,128)(2,1)} %reduce.13) | data formatting | bytes 12582912
  608.4 44.1 %all-to-all-done.2 = bf16[64,2,24576]{2,1,0:T(2,128)(2,1)} async-done(((bf16[64,2,24576]{2,1,0:T(2,128)(2,1)}), bf16[64,2,24576]{2,1,0:T(2,128)(2,1)}, u32[]{:S(2)}, u32[]{:S(2)}) %all-to-all-start.2) | async-done | bytes 6291488 | tf_op jit(solution)/shard_map/all_to_all | solution.py:67
  652.4 8.3 all-to-all-start.6
  679.5 36.7 %reshape.325 = bf16[6144,1,1,512]{3,2,1,0:T(2,128)(2,1)} reshape(bf16[64,2,24576]{2,1,0:T(2,128)(2,1)} %all-to-all-done.2) | data formatting | bytes 12582912
  716.2 9.0 %copy.59 = bf16[1,1,6144,512]{3,2,0,1:T(8,128)(2,1)} copy(bf16[1,1,6144,512]{3,1,0,2:T(2,128)(2,1)} %bitcast.143) | data formatting | bytes 12582912
  725.2 79.6 %all-to-all-done.6 = bf16[64,2,24576]{2,1,0:T(2,128)(2,1)} async-done(((bf16[64,2,24576]{2,1,0:T(2,128)(2,1)}), bf16[64,2,24576]{2,1,0:T(2,128)(2,1)}, u32[]{:S(2)}, u32[]{:S(2)}) %all-to-all-start.6) | async-done | bytes 6291488 | tf_op jit(solution)/shard_map/all_to_all | solution.py:67
  804.9 36.7 %reshape.327 = bf16[6144,1,1,512]{3,2,1,0:T(2,128)(2,1)} reshape(bf16[64,2,24576]{2,1,0:T(2,128)(2,1)} %all-to-all-done.6) | data formatting | bytes 12582912
  841.6 9.2 %copy.60 = bf16[1,1,6144,512]{3,2,0,1:T(8,128)(2,1)} copy(bf16[1,1,6144,512]{3,1,0,2:T(2,128)(2,1)} %bitcast.144) | data formatting | bytes 12582912
  861.8 8.3 collective-permute-done.6
  (105 shorter events, 120.6 us)
Async XLA Ops:
  0.6 43.1 %copy-start = (bf16[1,512,512]{2,1,0:T(8,128)(2,1)S(1)}, bf16[1,512,512]{2,1,0:T(8,128)(2,1)}, u32[]{:S(2)}) copy-start(bf16[1,512,512]{2,1,0:T(8,128)(2,1)} %param.13) | copy-start | bytes 1572868
  1.4 26.6 %collective-permute-start.3 = (s32[512,8]{0,1:T(8,128)S(1)}, s32[512,8]{0,1:T(8,128)S(1)}, u32[]{:S(2)}, u32[]{:S(2)}) collective-permute-start(s32[512,8]{0,1:T(8,128)S(1)} %get-tuple-element.11), channel_id=1, source_target_pairs={{0,64},{64,128},{128,192},{192,0},{1,65},{65,129},{129,193},{193,1... | collective-permute-start | bytes 49160 | tf_op jit(solution)/shard_map/ppermute | solution.py:88
  3.5 3.8 collective-permute-start
  5.4 24.4 %collective-permute-start.4 = (f32[512,8]{0,1:T(8,128)S(1)}, f32[512,8]{0,1:T(8,128)S(1)}, u32[]{:S(2)}, u32[]{:S(2)}) collective-permute-start(f32[512,8]{0,1:T(8,128)S(1)} %get-tuple-element.9), channel_id=1, source_target_pairs={{0,64},{64,128},{128,192},{192,0},{1,65},{65,129},{129,193},{193,1... | collective-permute-start | bytes 49160 | tf_op jit(solution)/shard_map/ppermute | solution.py:89
  6.3 3.8 collective-permute-start.1
  7.4 66.9 %copy-start.13 = (pred[512,64]{0,1:T(8,128)(4,1)}, pred[512,64]{0,1:T(8,128)(4,1)S(1)}, u32[]{:S(2)}) copy-start(pred[512,64]{0,1:T(8,128)(4,1)S(1)} %fusion.59) | copy-start | bytes 98308
  9.0 65.3 %copy-start.11 = (s32[512,64]{0,1:T(8,128)}, s32[512,64]{0,1:T(8,128)S(1)}, u32[]{:S(2)}) copy-start(s32[512,64]{0,1:T(8,128)S(1)} %bitcast_bitcast_fusion.1) | copy-start | bytes 393220
  13.8 24.0 %all-to-all-start = ((f32[64,1,96]{2,1,0:T(1,128)}), f32[64,1,96]{2,1,0:T(1,128)S(1)}, u32[]{:S(2)}, u32[]{:S(2)}) async-start(f32[64,1,96]{2,1,0:T(1,128)} %bitcast.4), calls=%async_computation | async-start | bytes 65536 | tf_op jit(solution)/shard_map/all_to_all | solution.py:61
  37.8 15.7 %all-to-all-start.3 = ((f32[64,1,96]{2,1,0:T(1,128)}), f32[64,1,96]{2,1,0:T(1,128)S(1)}, u32[]{:S(2)}, u32[]{:S(2)}) async-start(f32[64,1,96]{2,1,0:T(1,128)} %bitcast.20), calls=%async_computation.3 | async-start | bytes 65536 | tf_op jit(solution)/shard_map/all_to_all | solution.py:61
  49.3 10.6 %copy-start.10 = (bf16[2,1,512,512]{3,2,1,0:T(8,128)(2,1)S(1)}, bf16[2,1,512,512]{3,2,1,0:T(8,128)(2,1)}, u32[]{:S(2)}) copy-start(bf16[2,1,512,512]{3,2,1,0:T(8,128)(2,1)} %param.7) | copy-start | bytes 3145732
  53.5 150.5 %all-to-all-start.4 = ((bf16[64,1,96,512]{3,2,1,0:T(8,128)(2,1)}), bf16[64,1,96,512]{3,2,1,0:T(8,128)(2,1)}, u32[]{:S(2)}, u32[]{:S(2)}) async-start(bf16[64,1,96,512]{3,2,1,0:T(8,128)(2,1)} %convert_bitcast_fusion.1), calls=%async_computation.4 | async-start | bytes 12582912 | tf_op jit(solution)/shard_map/all_to_all | solution.py:61
  60.0 14.4 %collective-permute-start.2 = (bf16[512,512]{1,0:T(8,128)(2,1)S(1)}, bf16[512,512]{1,0:T(8,128)(2,1)S(1)}, u32[]{:S(2)}, u32[]{:S(2)}) collective-permute-start(bf16[512,512]{1,0:T(8,128)(2,1)S(1)} %get-tuple-element.8), channel_id=1, source_target_pairs={{0,64},{64,128},{128,192},{192,0},{1,65},{65,129},{129,193},{193,1... | collective-permute-start | bytes 1572872 | tf_op jit(solution)/shard_map/ppermute | solution.py:78
  204.0 150.4 %all-to-all-start.1 = ((bf16[64,1,96,512]{3,2,1,0:T(8,128)(2,1)}), bf16[64,1,96,512]{3,2,1,0:T(8,128)(2,1)}, u32[]{:S(2)}, u32[]{:S(2)}) async-start(bf16[64,1,96,512]{3,2,1,0:T(8,128)(2,1)} %convert_bitcast_fusion.2), calls=%async_computation.1 | async-start | bytes 12582912 | tf_op jit(solution)/shard_map/all_to_all | solution.py:61
  210.3 14.4 %collective-permute-start.5 = (bf16[512,512]{1,0:T(8,128)(2,1)S(1)}, bf16[512,512]{1,0:T(8,128)(2,1)S(1)}, u32[]{:S(2)}, u32[]{:S(2)}) collective-permute-start(bf16[512,512]{1,0:T(8,128)(2,1)S(1)} %get-tuple-element.7), channel_id=1, source_target_pairs={{0,64},{64,128},{128,192},{192,0},{1,65},{65,129},{129,193},{193,1... | collective-permute-start | bytes 1572872 | tf_op jit(solution)/shard_map/ppermute | solution.py:87
  230.1 132.4 %copy-start.8 = (bf16[1,1,512,256]{3,2,1,0:T(8,128)(2,1)S(1)}, bf16[1,1,512,256]{3,2,1,0:T(8,128)(2,1)}, u32[]{:S(2)}) copy-start(bf16[1,1,512,256]{3,2,1,0:T(8,128)(2,1)} %param.10) | copy-start | bytes 786436
  354.4 148.1 %all-to-all-start.5 = ((bf16[64,1,96,512]{3,2,1,0:T(8,128)(2,1)}), bf16[64,1,96,512]{3,2,1,0:T(8,128)(2,1)}, u32[]{:S(2)}, u32[]{:S(2)}) async-start(bf16[64,1,96,512]{3,2,1,0:T(8,128)(2,1)} %convert_bitcast_fusion), calls=%async_computation.5 | async-start | bytes 12582912 | tf_op jit(solution)/shard_map/all_to_all | solution.py:61
  502.5 149.9 %all-to-all-start.2 = ((bf16[64,2,24576]{2,1,0:T(2,128)(2,1)}), bf16[64,2,24576]{2,1,0:T(2,128)(2,1)}, u32[]{:S(2)}, u32[]{:S(2)}) async-start(bf16[64,2,24576]{2,1,0:T(2,128)(2,1)} %reshape.324), calls=%async_computation.2 | async-start | bytes 12582912 | tf_op jit(solution)/shard_map/all_to_all | solution.py:67
  523.4 8.7 copy-start.7
  652.4 152.4 %all-to-all-start.6 = ((bf16[64,2,24576]{2,1,0:T(2,128)(2,1)}), bf16[64,2,24576]{2,1,0:T(2,128)(2,1)}, u32[]{:S(2)}, u32[]{:S(2)}) async-start(bf16[64,2,24576]{2,1,0:T(2,128)(2,1)} %reshape.326), calls=%async_computation.6 | async-start | bytes 12582912 | tf_op jit(solution)/shard_map/all_to_all | solution.py:67
  665.9 11.0 %slice-start = ((s8[6291456]{0:T(1024)(128)(4,1)}), s8[4194304]{0:T(1024)(128)(4,1)S(1)}, s32[]{:S(2)}) async-start(s8[6291456]{0:T(1024)(128)(4,1)} %bitcast.147), calls=%async_computation.7 | async-start | bytes 8388608
  665.9 11.0 %slice-start.2 = ((s8[6291456]{0:T(1024)(128)(4,1)}), s8[4194304]{0:T(1024)(128)(4,1)S(1)}, s32[]{:S(2)}) async-start(s8[6291456]{0:T(1024)(128)(4,1)} %bitcast.149), calls=%async_computation.9 | async-start | bytes 8388608
  841.6 15.9 %slice-start.4 = ((s8[6291456]{0:T(1024)(128)(4,1)}), s8[2097152]{0:T(1024)(128)(4,1)S(1)}, s32[]{:S(2)}) async-start(s8[6291456]{0:T(1024)(128)(4,1)} %bitcast.151), calls=%async_computation.11 | async-start | bytes 4194304
  856.9 13.3 %collective-permute-start.6 = (bf16[512,512]{1,0:T(8,128)(2,1)S(1)}, bf16[512,512]{1,0:T(8,128)(2,1)S(1)}, u32[]{:S(2)}, u32[]{:S(2)}) collective-permute-start(bf16[512,512]{1,0:T(8,128)(2,1)S(1)} %fusion.47), channel_id=1, source_target_pairs={{64,0},{128,64},{192,128},{0,192},{65,1},{129,65},{193,129},{1,193... | collective-permute-start | bytes 1572872 | tf_op jit(solution)/shard_map/ppermute | solution.py:97
  857.5 13.4 %copy-start.1 = (bf16[1,512,512]{2,1,0:T(8,128)(2,1)S(1)}, bf16[1,512,512]{2,1,0:T(8,128)(2,1)}, u32[]{:S(2)}) copy-start(bf16[1,512,512]{2,1,0:T(8,128)(2,1)} %param.13) | copy-start | bytes 1572868
  (12 other events, 67.8 us)
where the time goes:
time: 884 us; the launch traced here: 871 us
  waiting for transfers between devices  472 us (53%)
  local copies, waits for them, and re-layouts  152 us (17%)
  other arithmetic  100 us (11%)
  matrix products  84.1 us (10%)
  starting transfers between devices  61.7 us (7%)
    all_to_all x5, waiting for transfers between devices, dispatch(): received = lax.all_to_all(split_buf, 'expert', 0, 2, tiled=True)  310 us
    unnamed x52, local copies, waits for them, and re-layouts  125 us
    all_to_all x2, waiting for transfers between devices, collect(): received = lax.all_to_all(split_buf, 'expert', 2, 0, tiled=True)  124 us
    unnamed x5, other arithmetic  83.4 us
    all_to_all x5, starting transfers between devices, dispatch(): received = lax.all_to_all(split_buf, 'expert', 0, 2, tiled=True)  39.8 us
    reshape x2, local copies, waits for them, and re-layouts, collect(): slot_buf.reshape((1, local_experts, group_size * capacity) + row_tail)  24.1 us
  transfers between devices with their start and end apart: 14, of which 12 were waited for; matrix products, arithmetic and copies ran while one was open for 32% of the time, Pallas kernels for 0%

commit v1 on v0

v1 whole, which is shorter than its diff:
```python
import functools

import jax
import jax.numpy as jnp
from jax import lax
from jax.experimental import pallas as pl
from jax.experimental.pallas import tpu as pltpu
from jax.sharding import PartitionSpec as P

TG = 8
F32 = jnp.float32
BF16 = jnp.bfloat16


def routing_rows(route, group_rank, num_local):
    gates, ids = route[0:8], route[8:16]
    tokens = route.shape[1]
    taken, gate = [], []
    for k in range(num_local):
        hit = ids == (group_rank + k * TG).astype(F32)
        taken.append(jnp.sum(jnp.where(hit, 1.0, 0.0), axis=0, keepdims=True))
        gate.append(jnp.sum(jnp.where(hit, gates, 0.0), axis=0, keepdims=True))
    taken, gate = jnp.concatenate(taken, axis=0), jnp.concatenate(gate, axis=0)
    lane = lax.broadcasted_iota(jnp.int32, taken.shape, 1)
    count, shift = taken, 1
    while shift < tokens:
        count = count + jnp.where(lane >= shift, pltpu.roll(count, shift, 1), 0.0)
        shift *= 2
    return jnp.where(taken > 0.0, count - 1.0, -1.0), gate


def slot_mask(rank_row, capacity):
    slot = lax.broadcasted_iota(jnp.int32, (capacity, rank_row.shape[1]), 0).astype(F32)
    return slot == rank_row


def fill_onehot(hot_ref, rank, capacity):
    for k in range(rank.shape[0]):
        hit = slot_mask(rank[k:k + 1], capacity)
        hot_ref[k * capacity:(k + 1) * capacity, :] = jnp.where(hit, 1.0, 0.0).astype(BF16)


def gate_column(rank_row, gate_row, capacity):
    hit = slot_mask(rank_row, capacity)
    return jnp.sum(jnp.where(hit, gate_row, 0.0), axis=1, keepdims=True)


def gather_kernel(capacity, with_dy, *refs):
    if with_dy:
        route_ref, x_ref, dy_ref, xs_ref, q_ref, rg_ref, hot_ref = refs
    else:
        route_ref, x_ref, xs_ref, rg_ref, hot_ref = refs
    group_rank = lax.rem(lax.axis_index('expert'), TG)
    num_local = xs_ref.shape[0]
    rank, gate = routing_rows(route_ref[0], group_rank, num_local)
    rg_ref[0, 0:8] = rank
    rg_ref[0, 8:16] = gate
    fill_onehot(hot_ref, rank, capacity)
    rows = jnp.dot(hot_ref[...], x_ref[0], preferred_element_type=F32)
    xs_ref[...] = rows.astype(BF16).reshape(xs_ref.shape)
    if with_dy:
        rows = jnp.dot(hot_ref[...], dy_ref[0], preferred_element_type=F32)
        for k in range(num_local):
            col = gate_column(rank[k:k + 1], gate[k:k + 1], capacity)
            q_ref[k] = (col * rows[k * capacity:(k + 1) * capacity]).astype(BF16)


def gather_rows(route, x_all, dy_all, capacity):
    groups, tokens, width = x_all.shape
    num_local = 8
    tok_block = pl.BlockSpec((1, tokens, width), lambda s: (s, 0, 0))
    slot_block = pl.BlockSpec((num_local, capacity, width), lambda s: (0, s, 0))
    rg_block = pl.BlockSpec((1, 16, tokens), lambda s: (s, 0, 0))
    slot_shape = jax.ShapeDtypeStruct((num_local, groups * capacity, width), BF16)
    with_dy = dy_all is not None
    args = (route, x_all, dy_all) if with_dy else (route, x_all)
    flops = 2 * groups * num_local * capacity * tokens * width * (2 if with_dy else 1)
    return pl.pallas_call(
        functools.partial(gather_kernel, capacity, with_dy),
        grid=(groups,),
        in_specs=[rg_block] + [tok_block] * (len(args) - 1),
        out_specs=[slot_block] * (len(args) - 1) + [rg_block],
        out_shape=[slot_shape] * (len(args) - 1) + [jax.ShapeDtypeStruct((groups, 16, tokens), F32)],
        scratch_shapes=[pltpu.VMEM((num_local * capacity, tokens), BF16)],
        cost_estimate=pl.CostEstimate(flops=flops, bytes_accessed=16 << 20, transcendentals=0),
        name='gather_rows_b' if with_dy else 'gather_rows_f',
    )(*args)


def backward_kernel(x_ref, q_ref, wcat_ref, wout_ref, dwcat_ref, dwout_ref, dx_ref, dab_ref):
    x, q, wcat, wout = x_ref[0], q_ref[0], wcat_ref[0], wout_ref[0]
    hid = wout.shape[0]
    pre = jnp.dot(x, wcat, preferred_element_type=F32)
    a, b = pre[:, :hid], pre[:, hid:]
    sig = jax.nn.sigmoid(a)
    act = a * sig
    h = (act * b).astype(BF16)
    dwout_ref[0] = lax.dot_general(h, q, (((0,), (0,)), ((), ())), preferred_element_type=F32)
    u = lax.dot_general(q, wout, (((1,), (1,)), ((), ())), preferred_element_type=F32)
    dab_ref[:, :hid] = (u * b * sig * (1.0 + a * (1.0 - sig))).astype(BF16)
    dab_ref[:, hid:] = (u * act).astype(BF16)
    dab = dab_ref[...]
    dwcat_ref[0] = lax.dot_general(x, dab, (((0,), (0,)), ((), ())), preferred_element_type=F32)
    dx = lax.dot_general(dab, wcat, (((1,), (1,)), ((), ())), preferred_element_type=F32)
    dx_ref[0] = dx.astype(BF16)


def expert_backward(xs, q, wcat, wout):
    num_local, rows, width = xs.shape
    hid = wout.shape[1]
    row_block = pl.BlockSpec((1, rows, width), lambda e: (e, 0, 0))
    cat_block = pl.BlockSpec((1, width, 2 * hid), lambda e: (e, 0, 0))
    out_block = pl.BlockSpec((1, hid, width), lambda e: (e, 0, 0))
    return pl.pallas_call(
        backward_kernel,
        grid=(num_local,),
        in_specs=[row_block, row_block, cat_block, out_block],
        out_specs=[cat_block, out_block, row_block],
        out_shape=[jax.ShapeDtypeStruct(wcat.shape, F32), jax.ShapeDtypeStruct(wout.shape, F32),
                   jax.ShapeDtypeStruct(xs.shape, BF16)],
        scratch_shapes=[pltpu.VMEM((rows, 2 * hid), BF16)],
        cost_estimate=pl.CostEstimate(flops=16 * num_local * rows * width * hid, bytes_accessed=38 << 20,
                                      transcendentals=num_local * rows * hid),
        name='expert_backward',
    )(xs, q, wcat, wout)


def forward_kernel(capacity, rg_ref, x_ref, wcat_ref, wout_ref, c_ref):
    e = pl.program_id(0)
    x, wcat, wout = x_ref[0], wcat_ref[0], wout_ref[0]
    hid = wout.shape[0]
    pre = jnp.dot(x, wcat, preferred_element_type=F32)
    a, b = pre[:, :hid], pre[:, hid:]
    h = (a * jax.nn.sigmoid(a) * b).astype(BF16)
    o = jnp.dot(h, wout, preferred_element_type=F32)
    for s in range(rg_ref.shape[0]):
        col = gate_column(rg_ref[s, pl.ds(e, 1)], rg_ref[s, pl.ds(8 + e, 1)], capacity)
        c_ref[0, s * capacity:(s + 1) * capacity] = (col * o[s * capacity:(s + 1) * capacity]).astype(BF16)


def expert_forward(rg, xs, wcat, wout, capacity):
    num_local, rows, width = xs.shape
    hid = wout.shape[1]
    row_block = pl.BlockSpec((1, rows, width), lambda e: (e, 0, 0))
    return pl.pallas_call(
        functools.partial(forward_kernel, capacity),
        grid=(num_local,),
        in_specs=[pl.BlockSpec(rg.shape, lambda e: (0, 0, 0)), row_block,
                  pl.BlockSpec((1, width, 2 * hid), lambda e: (e, 0, 0)),
                  pl.BlockSpec((1, hid, width), lambda e: (e, 0, 0))],
        out_specs=row_block,
        out_shape=jax.ShapeDtypeStruct(xs.shape, BF16),
        cost_estimate=pl.CostEstimate(flops=6 * num_local * rows * width * hid, bytes_accessed=20 << 20,
                                      transcendentals=num_local * rows * hid),
        name='expert_forward',
    )(rg, xs, wcat, wout)


def scatter_kernel(capacity, rg_ref, c_ref, out_ref, hot_ref):
    fill_onehot(hot_ref, rg_ref[0, 0:8], capacity)
    rows = c_ref[...].reshape(hot_ref.shape[0], c_ref.shape[2])
    out_ref[0] = lax.dot_general(hot_ref[...], rows, (((0,), (0,)), ((), ())), preferred_element_type=F32)


def scatter_rows(rg, slots, capacity):
    num_local, _, width = slots.shape
    groups, _, tokens = rg.shape
    return pl.pallas_call(
        functools.partial(scatter_kernel, capacity),
        grid=(groups,),
        in_specs=[pl.BlockSpec((1, 16, tokens), lambda s: (s, 0, 0)),
                  pl.BlockSpec((num_local, capacity, width), lambda s: (0, s, 0))],
        out_specs=pl.BlockSpec((1, tokens, width), lambda s: (s, 0, 0)),
        out_shape=jax.ShapeDtypeStruct((groups, tokens, width), F32),
        scratch_shapes=[pltpu.VMEM((num_local * capacity, tokens), BF16)],
        cost_estimate=pl.CostEstimate(flops=2 * groups * num_local * capacity * tokens * width,
                                      bytes_accessed=16 << 20, transcendentals=0),
        name='scatter_rows',
    )(rg, slots)


def solution(mesh):
    group_size = mesh.shape['expert']
    num_stages = mesh.shape['stage']
    to_next = [(i, (i + 1) % num_stages) for i in range(num_stages)]
    to_prev = [((i + 1) % num_stages, i) for i in range(num_stages)]
    rows_of = group_size // TG
    tok_groups = [[z * TG + r for r in range(TG)] for z in range(rows_of)]
    wgt_groups = [[z * TG + r for z in range(rows_of)] for r in range(TG)]

    def device_fn(x_acts, expert_ids, gate_wts, w_in, w_up, w_out, d_out):
        tokens, width = x_acts.shape[2], x_acts.shape[3]
        hid = w_in.shape[3]
        capacity = 96

        def gather_tok(arr):
            return lax.all_gather(arr, 'expert', axis_index_groups=tok_groups, axis=0)

        def gather_wgt(arr):
            return lax.all_gather(arr, 'expert', axis_index_groups=wgt_groups, axis=0)

        def reduce_tok(arr):
            return lax.psum_scatter(arr, 'expert', axis_index_groups=tok_groups, scatter_dimension=0, tiled=False)

        def reduce_wgt(arr):
            return lax.psum_scatter(arr, 'expert', axis_index_groups=wgt_groups, scatter_dimension=0, tiled=False)

        wcat = gather_wgt(jnp.concatenate([w_in[0, 0], w_up[0, 0]], axis=1))
        wout = gather_wgt(w_out[0, 0])
        route = jnp.concatenate([gate_wts[0, 0].T, expert_ids[0, 0].T.astype(F32),
                                 gate_wts[1, 0].T, expert_ids[1, 0].T.astype(F32)], axis=0)
        x_bwd = lax.ppermute(x_acts[0, 0], 'stage', to_next)
        route = gather_tok(lax.ppermute(route, 'stage', to_next))
        x_fwd = lax.ppermute(x_acts[1, 0], 'stage', to_next)
        dy_all = gather_tok(d_out[0])
        x_all = gather_tok(x_bwd)
        xs, q, rg = gather_rows(route[:, 0:16], x_all, dy_all, capacity)
        dwcat, dwout, dxs = expert_backward(xs, q, wcat, wout)
        dwout = reduce_wgt(dwout)
        dwcat = reduce_wgt(dwcat)
        dx = reduce_tok(scatter_rows(rg, dxs, capacity)).astype(BF16)
        dx = lax.ppermute(dx, 'stage', to_prev)
        xf_all = gather_tok(x_fwd)
        xs_f, rg_f = gather_rows(route[:, 16:32], xf_all, None, capacity)
        c = expert_forward(rg_f, xs_f, wcat, wout, capacity)
        y = reduce_tok(scatter_rows(rg_f, c, capacity)).astype(BF16)
        dwcat = dwcat.astype(BF16)
        return (y[None], dx[None], dwcat[None, None, :, :hid], dwcat[None, None, :, hid:],
                dwout.astype(BF16)[None, None])

    tok_spec = P(None, 'stage', 'expert', None)
    w_spec = P('stage', 'expert', None, None)
    row_spec = P('stage', 'expert', None)
    return jax.shard_map(device_fn, mesh=mesh,
                         in_specs=(tok_spec, tok_spec, tok_spec, w_spec, w_spec, w_spec, row_spec),
                         out_specs=(row_spec, row_spec, w_spec, w_spec, w_spec), check_vma=False)
```

time: 884 us -> 497 us (0.56); the launches traced: 871 us -> 495 us
  local copies, waits for them, and re-layouts: 152 us -> 6.12 us
  waiting for transfers between devices: 472 us -> 359 us
  other arithmetic: 100 us -> 9.05 us
  matrix products: 84.1 us -> 0 us
  Pallas kernels: 0 us -> 80.5 us
  starting transfers between devices: 61.7 us -> 8.01 us
  blocking collectives: 0 us -> 19.1 us
  between operations: 1.52 us -> 13.9 us
    all_to_all x7 -> x0, waiting for transfers between devices: 433 us -> none  [the longest x5 310 us: dispatch(): received = lax.all_to_all(split_buf, 'expert', 0, 2, tiled=True)]
    reduce_scatter x0 -> x4, waiting for transfers between devices: none -> 226 us  [the longest x2 149 us: reduce_wgt(): lax.psum_scatter(arr, 'expert', axis_index_groups=wgt_groups, scatter_dim...]
    unnamed x52 -> x5, local copies, waits for them, and re-layouts: 125 us -> 2.46 us
    all_gather x0 -> x5, waiting for transfers between devices: none -> 104 us  [the longest x2 81.3 us: gather_wgt(): return lax.all_gather(arr, 'expert', axis_index_groups=wgt_groups, axis=0)]
    dot_general x15 -> x0, matrix products: 84.1 us -> none  [the longest x3 16.4 us: to_slots(): jnp.einsum('uec,ud->ecd', slot_hit, tok_rows, preferred_element_type=jnp....]
    unnamed x5 -> x0, other arithmetic: 83.4 us -> none
    pallas_call x0 -> x6, Pallas kernels: none -> 80.5 us  [the longest x2 27.7 us: gather_rows(): pl.pallas_call(functools.partial(gather_kernel, capacity, with_dy), grid=...]
    all_to_all x7 -> x0, starting transfers between devices: 56.7 us -> none  [the longest x5 39.8 us: dispatch(): received = lax.all_to_all(split_buf, 'expert', 0, 2, tiled=True)]
  transfers between devices with their start and end apart: 14 -> 13, of which waited for: 12 -> 11; matrix products, arithmetic and copies ran while one was open for 32% -> 3% of each run, Pallas kernels for 0% -> 16%
where the time goes in v1:
time: 497 us; the launch traced here: 495 us
  waiting for transfers between devices  359 us (72%)
  Pallas kernels  80.5 us (16%)
  blocking collectives  19.1 us (4%)
  between operations  13.9 us (3%)
  other arithmetic  9.05 us (2%)
  starting transfers between devices  8.01 us (2%)
  local copies, waits for them, and re-layouts  6.12 us (1%)
    reduce_scatter x2, waiting for transfers between devices, reduce_wgt(): lax.psum_scatter(arr, 'expert', axis_index_groups=wgt_groups, scatter_dim...  149 us
    all_gather x2, waiting for transfers between devices, gather_wgt(): return lax.all_gather(arr, 'expert', axis_index_groups=wgt_groups, axis=0)  81.3 us
    reduce_scatter x2, waiting for transfers between devices, reduce_tok(): lax.psum_scatter(arr, 'expert', axis_index_groups=tok_groups, scatter_dim...  76.6 us
    pallas_call x2, Pallas kernels, gather_rows(): pl.pallas_call(functools.partial(gather_kernel, capacity, with_dy), grid=...  27.7 us
    all_gather x3, waiting for transfers between devices, gather_tok(): return lax.all_gather(arr, 'expert', axis_index_groups=tok_groups, axis=0)  23.1 us
    pallas_call x1, Pallas kernels, expert_backward(): pl.pallas_call(backward_kernel, grid=(num_local,), in_specs=[row_block, r...  21.1 us
    pallas_call x2, Pallas kernels, scatter_rows(): pl.pallas_call(functools.partial(scatter_kernel, capacity), grid=(groups,...  20.1 us
    all_gather x1, blocking collectives, gather_tok(): return lax.all_gather(arr, 'expert', axis_index_groups=tok_groups, axis=0)  19.1 us
  transfers between devices with their start and end apart: 13, of which 11 were waited for; matrix products, arithmetic and copies ran while one was open for 3% of the time, Pallas kernels for 16%

profile of v1, /device:TPU:1, one launch (start us, length us, event | category | flops | bytes accessed | tf_op | source)
XLA Modules:
  0.0 495.3 jit_solution(15320358245769295872)
XLA Ops:
  9.2 2.1 collective-permute-start.2
  11.3 10.7 %collective-permute-done.2 = bf16[512,512]{1,0:T(8,128)(2,1)S(1)} collective-permute-done((bf16[512,512]{1,0:T(8,128)(2,1)S(1)}, bf16[512,512]{1,0:T(8,128)(2,1)S(1)}, u32[]{:S(2)}, u32[]{:S(2)}) %collective-permute-start.2) | collective-permute-done | bytes 524320 | tf_op jit(solution)/shard_map/ppermute | solution.py:212
  23.8 1.9 pad_maximum_fusion
  25.7 1.9 collective-permute-start.1
  27.6 10.8 %collective-permute-done.1 = bf16[512,512]{1,0:T(8,128)(2,1)S(1)} collective-permute-done((bf16[512,512]{1,0:T(8,128)(2,1)S(1)}, bf16[512,512]{1,0:T(8,128)(2,1)S(1)}, u32[]{:S(2)}, u32[]{:S(2)}) %collective-permute-start.1) | collective-permute-done | bytes 524320 | tf_op jit(solution)/shard_map/ppermute | solution.py:214
  41.9 3.7 collective-permute-done
  45.6 19.1 %all-gather = f32[256,512]{1,0:T(8,128)S(1)} all-gather(f32[32,512]{1,0:T(8,128)S(1)} %collective-permute-done), channel_id=2, replica_groups={{0,1,2,3,4,5,6,7},{8,9,10,11,12,13,14,15},{16,17,18,19,20,21,22,23},{24..., dimensions={0}, use_global_device_ids=true | all-gather | bytes 589824 | tf_op jit(solution)/shard_map/all_gather | solution.py:197
  65.6 19.1 %all-gather.19.cloned.1.call-done = bf16[4096,512]{1,0:T(8,128)(2,1)} async-done(((bf16[512,512]{1,0:T(8,128)(2,1)}), bf16[4096,512]{1,0:T(8,128)(2,1)}) %all-gather.19.cloned.1.call-update) | async-done | bytes 4194320 | tf_op jit(solution)/shard_map/all_gather | solution.py:197
  84.7 15.9 %gather_rows_b.1 = (bf16[8,768,512]{2,1,0:T(8,128)(2,1)}, bf16[8,768,512]{2,1,0:T(8,128)(2,1)}, f32[8,16,512]{2,1,0:T(8,128)}) custom-call(f32[8,16,512]{2,1,0:T(8,128)} %get-tuple-element.25.refs_0_, bf16[8,512,512]{2,1,0:T(8,128)(2,1)} %bitcast.47, bf16[8,512,512]{2,1,0:T(8,128)(2,1)} %all-gather.11.cloned.1.call-done.refs_2_), custom_call_target="tpu_custom_call" | custom-call | flops 6442450944 | bytes 16777216 | tf_op jit(solution)/shard_map/gather_rows_b/pallas_call | solution.py:78
  100.6 21.9 %all-gather.17.cloned.1.call-done = bf16[8,1,256,512]{3,2,1,0:T(8,128)(2,1)} async-done(((bf16[1,1,256,512]{3,2,1,0:T(8,128)(2,1)}), bf16[8,1,256,512]{3,2,1,0:T(8,128)(2,1)}) %all-gather.17.cloned.1.call-update) | async-done | bytes 2097168 | tf_op jit(solution)/shard_map/all_gather | solution.py:200
  122.5 59.4 %all-gather.15.cloned.1.call-done = bf16[4096,512]{1,0:T(8,128)(2,1)} async-done(((bf16[512,512]{1,0:T(8,128)(2,1)}), bf16[4096,512]{1,0:T(8,128)(2,1)}) %all-gather.15.cloned.1.call-update) | async-done | bytes 4194320 | tf_op jit(solution)/shard_map/all_gather | solution.py:200
  181.9 21.1 %expert_backward.1 = (f32[8,512,512]{2,1,0:T(8,128)}, f32[8,256,512]{2,1,0:T(8,128)}, bf16[8,768,512]{2,1,0:T(8,128)(2,1)}) custom-call(bf16[8,768,512]{2,1,0:T(8,128)(2,1)} %get-tuple-element.16.x_ref, bf16[8,768,512]{2,1,0:T(8,128)(2,1)} %get-tuple-element.17.q_ref, bf16[8,512,512]{2,1,0:T(8,128)(2,1)} %bitcast.38, bf16[8,256,512]{2,1,0:T(8,128)(2,1)} %bitcast.40), custom_call_target="tpu_custom_call" | custom-call | flops 12884901888 | bytes 39845888 | tf_op jit(solution)/shard_map/expert_backward/pallas_call | solution.py:114
  203.0 10.0 %scatter_rows.3 = f32[8,512,512]{2,1,0:T(8,128)} custom-call(f32[8,16,512]{2,1,0:T(8,128)} %get-tuple-element.15.rg_ref, bf16[8,768,512]{2,1,0:T(8,128)(2,1)} %get-tuple-element.18.c_ref), custom_call_target="tpu_custom_call" | custom-call | flops 3221225472 | bytes 16777216 | tf_op jit(solution)/shard_map/scatter_rows/pallas_call | solution.py:168
  213.8 4.1 all-gather.13.cloned.1.call-done
  217.9 11.8 %gather_rows_f.1 = (bf16[8,768,512]{2,1,0:T(8,128)(2,1)}, f32[8,16,512]{2,1,0:T(8,128)}) custom-call(f32[8,16,512]{2,1,0:T(8,128)} %get-tuple-element.26.refs_0_, bf16[8,512,512]{2,1,0:T(8,128)(2,1)} %bitcast.46), custom_call_target="tpu_custom_call" | custom-call | flops 3221225472 | bytes 16777216 | tf_op jit(solution)/shard_map/gather_rows_f/pallas_call | solution.py:78
  229.7 11.7 %expert_forward.1.c_ref = bf16[8,768,512]{2,1,0:T(8,128)(2,1)} custom-call(f32[8,16,512]{2,1,0:T(8,128)} %get-tuple-element.13.rg_ref, bf16[8,768,512]{2,1,0:T(8,128)(2,1)} %get-tuple-element.14.x_ref, bf16[8,512,512]{2,1,0:T(8,128)(2,1)} %bitcast.39, bf16[8,256,512]{2,1,0:T(8,128)(2,1)} %bitcast.41), custom_call_target="tpu_custom_call" | custom-call | flops 4831838208 | bytes 20971520 | tf_op jit(solution)/shard_map/expert_forward/pallas_call | solution.py:145
  241.4 10.1 %scatter_rows.2 = f32[8,512,512]{2,1,0:T(8,128)} custom-call(f32[8,16,512]{2,1,0:T(8,128)} %get-tuple-element.13.rg_ref, bf16[8,768,512]{2,1,0:T(8,128)(2,1)} %expert_forward.1.c_ref), custom_call_target="tpu_custom_call" | custom-call | flops 3221225472 | bytes 16777216 | tf_op jit(solution)/shard_map/scatter_rows/pallas_call | solution.py:168
  252.2 22.3 %reduce-scatter.7.cloned.1.call-done = f32[1,512,512]{2,1,0:T(8,128)} async-done(((f32[8,512,512]{2,1,0:T(8,128)}), f32[1,512,512]{2,1,0:T(8,128)}) %reduce-scatter.7.cloned.1.call-update) | async-done | bytes 1048592 | tf_op jit(solution)/shard_map/reduce_scatter | solution.py:203
  275.8 2.5 collective-permute-start.3
  278.2 54.1 %reduce-scatter.11.cloned.1.call-done = f32[1,256,512]{2,1,0:T(8,128)} async-done(((f32[8,256,512]{2,1,0:T(8,128)}), f32[1,256,512]{2,1,0:T(8,128)}) %reduce-scatter.11.cloned.1.call-update) | async-done | bytes 524304 | tf_op jit(solution)/shard_map/reduce_scatter | solution.py:206
  332.3 1.8 convert_bitcast_fusion.2
  334.1 54.3 %reduce-scatter.5.cloned.1.call-done = f32[1,512,512]{2,1,0:T(8,128)} async-done(((f32[8,512,512]{2,1,0:T(8,128)}), f32[1,512,512]{2,1,0:T(8,128)}) %reduce-scatter.5.cloned.1.call-update) | async-done | bytes 1048592 | tf_op jit(solution)/shard_map/reduce_scatter | solution.py:203
  388.4 2.1 convert_element_type.53
  390.5 95.4 %reduce-scatter.9.cloned.1.call-done = f32[1,512,512]{2,1,0:T(8,128)} async-done(((f32[8,512,512]{2,1,0:T(8,128)}), f32[1,512,512]{2,1,0:T(8,128)}) %reduce-scatter.9.cloned.1.call-update) | async-done | bytes 1048592 | tf_op jit(solution)/shard_map/reduce_scatter | solution.py:206
  (34 shorter events, 13.7 us)
Async XLA Ops:
  7.2 58.4 %all-gather.11.cloned.1.call-start = ((), (), s32[]{:S(2)}) async-start(), calls=%async_computation.5 | async-start | bytes 4718592 | tf_op jit(solution)/shard_map/all_gather | solution.py:197
  7.9 76.8 %all-gather.19.cloned.1.call-start = ((), (), s32[]{:S(2)}) async-start(), calls=%async_computation.12 | async-start | bytes 4718592 | tf_op jit(solution)/shard_map/all_gather | solution.py:197
  9.2 12.9 %collective-permute-start.2 = (bf16[512,512]{1,0:T(8,128)(2,1)S(1)}, bf16[512,512]{1,0:T(8,128)(2,1)S(1)}, u32[]{:S(2)}, u32[]{:S(2)}) collective-permute-start(bf16[512,512]{1,0:T(8,128)(2,1)S(1)} %get-tuple-element.21), channel_id=1, source_target_pairs={{0,64},{64,128},{128,192},{192,0},{1,65},{65,129},{129,193},{193,1... | collective-permute-start | bytes 1572872 | tf_op jit(solution)/shard_map/ppermute | solution.py:212
  22.1 0.9 copy-start.1
  23.0 99.5 %all-gather.17.cloned.1.call-start = ((), (), s32[]{:S(2)}) async-start(), calls=%async_computation.11 | async-start | bytes 2359296 | tf_op jit(solution)/shard_map/all_gather | solution.py:200
  23.7 158.2 %all-gather.15.cloned.1.call-start = ((), (), s32[]{:S(2)}) async-start(), calls=%async_computation.10 | async-start | bytes 4718592 | tf_op jit(solution)/shard_map/all_gather | solution.py:200
  25.6 192.3 %all-gather.13.cloned.1.call-start = ((), (), s32[]{:S(2)}) async-start(), calls=%async_computation.9 | async-start | bytes 4718592 | tf_op jit(solution)/shard_map/all_gather | solution.py:197
  25.7 12.8 %collective-permute-start.1 = (bf16[512,512]{1,0:T(8,128)(2,1)S(1)}, bf16[512,512]{1,0:T(8,128)(2,1)S(1)}, u32[]{:S(2)}, u32[]{:S(2)}) collective-permute-start(bf16[512,512]{1,0:T(8,128)(2,1)S(1)} %get-tuple-element.22), channel_id=1, source_target_pairs={{0,64},{64,128},{128,192},{192,0},{1,65},{65,129},{129,193},{193,1... | collective-permute-start | bytes 1572872 | tf_op jit(solution)/shard_map/ppermute | solution.py:214
  38.5 0.8 copy-start
  39.3 235.2 %reduce-scatter.7.cloned.1.call-start = ((), (), s32[]{:S(2)}) async-start(), calls=%async_computation.6 | async-start | bytes 9437184 | tf_op jit(solution)/shard_map/reduce_scatter | solution.py:203
  40.8 4.8 collective-permute-start
  213.0 119.3 %reduce-scatter.11.cloned.1.call-start = ((), (), s32[]{:S(2)}) async-start(), calls=%async_computation.8 | async-start | bytes 4718592 | tf_op jit(solution)/shard_map/reduce_scatter | solution.py:206
  213.8 174.6 %reduce-scatter.5.cloned.1.call-start = ((), (), s32[]{:S(2)}) async-start(), calls=%async_computation.4 | async-start | bytes 9437184 | tf_op jit(solution)/shard_map/reduce_scatter | solution.py:203
  251.5 234.4 %reduce-scatter.9.cloned.1.call-start = ((), (), s32[]{:S(2)}) async-start(), calls=%async_computation.7 | async-start | bytes 9437184 | tf_op jit(solution)/shard_map/reduce_scatter | solution.py:206
  275.8 212.2 %collective-permute-start.3 = (bf16[512,512]{1,0:T(8,128)(2,1)S(1)}, bf16[512,512]{1,0:T(8,128)(2,1)S(1)}, u32[]{:S(2)}, u32[]{:S(2)}) collective-permute-start(bf16[512,512]{1,0:T(8,128)(2,1)S(1)} %convert_bitcast_fusion.1), channel_id=1, source_target_pairs={{64,0},{128,64},{192,128},{0,192},{65,1},{129,65},{193,129},{1,193... | collective-permute-start | bytes 1572872 | tf_op jit(solution)/shard_map/ppermute | solution.py:222
Sparse Core Ops, SparseCore 0:
  9.8 38.5 all-gather.10
  50.3 34.3 all-gather.18
  86.5 35.9 all-gather.16
  124.7 57.1 all-gather.14
  184.2 33.6 all-gather.12
  220.3 54.1 reduce-scatter.6
  277.0 55.2 reduce-scatter.10
  334.9 53.4 reduce-scatter.4
  390.9 94.8 reduce-scatter.8

commit v2 on v1

v2 whole, which is shorter than its diff:
```python
import functools

import jax
import jax.numpy as jnp
from jax import lax
from jax.experimental import pallas as pl
from jax.experimental.pallas import tpu as pltpu
from jax.sharding import PartitionSpec as P

TG = 8
F32 = jnp.float32
BF16 = jnp.bfloat16
MESH = pl.DeviceIdType.MESH


def routing_rows(gates, ids, group_rank, num_local):
    tokens = ids.shape[1]
    taken, gate = [], []
    for k in range(num_local):
        hit = ids == group_rank + k * TG
        taken.append(jnp.sum(jnp.where(hit, 1.0, 0.0), axis=0, keepdims=True))
        gate.append(jnp.sum(jnp.where(hit, gates, 0.0), axis=0, keepdims=True))
    taken, gate = jnp.concatenate(taken, axis=0), jnp.concatenate(gate, axis=0)
    lane = lax.broadcasted_iota(jnp.int32, taken.shape, 1)
    count, shift = taken, 1
    while shift < tokens:
        count = count + jnp.where(lane >= shift, pltpu.roll(count, shift, 1), 0.0)
        shift *= 2
    return jnp.where(taken > 0.0, count - 1.0, -1.0), gate


def slot_mask(rank_row, capacity):
    slot = lax.broadcasted_iota(jnp.int32, (capacity, rank_row.shape[1]), 0).astype(F32)
    return slot == rank_row


def fill_onehot(hot_ref, rank, capacity):
    for k in range(rank.shape[0]):
        hit = slot_mask(rank[k:k + 1], capacity)
        hot_ref[k * capacity:(k + 1) * capacity, :] = jnp.where(hit, 1.0, 0.0).astype(BF16)


def gate_column(rank_row, gate_row, capacity):
    hit = slot_mask(rank_row, capacity)
    return jnp.sum(jnp.where(hit, gate_row, 0.0), axis=1, keepdims=True)


class Peers:
    def __init__(self, num_stages):
        stage, me = lax.axis_index('stage'), lax.axis_index('expert')
        self.rank = lax.rem(me, TG)
        self.base = me - self.rank
        self.stage = stage
        self.core = lax.rem(self.rank, 2)
        self.ypos = (self.rank - self.core) // 2
        self.own, self.up_slot = self.rank, self.slot(1)
        self.far_slot, self.down_slot = self.slot(2), self.slot(3)
        self.up = (stage, self.base + self.slot(1))
        self.down = (stage, self.base + self.slot(3))
        self.partner = (stage, self.base + self.slot(0, True))
        self.after = (lax.rem(stage + 1, num_stages), me)
        self.before = (lax.rem(stage + num_stages - 1, num_stages), me)

    def slot(self, offset, other_core=False):
        core = 1 - self.core if other_core else self.core
        return lax.rem(self.ypos + offset, 4) * 2 + core


def greet(devices):
    barrier = pltpu.get_barrier_semaphore()
    for device in devices:
        pl.semaphore_signal(barrier, inc=1, device_id=device, device_id_type=MESH)
    pl.semaphore_wait(barrier, len(devices))


def send(src, dst, send_sem, recv_sem, device):
    return pltpu.make_async_remote_copy(src_ref=src, dst_ref=dst, send_sem=send_sem, recv_sem=recv_sem,
                                        device_id=device, device_id_type=MESH)


class Spread:
    def __init__(self, peers, src, buf, send_sems, recv_sems):
        half = buf.shape[1] // 2
        p = peers

        def copy(i, ref, device, dst=None):
            return send(ref, ref if dst is None else dst, send_sems.at[i], recv_sems.at[i], device)

        own = buf.at[p.own]
        self.own_up = copy(0, src, p.up, own)
        self.own_down = copy(1, src, p.down, own)
        self.fwd_up = copy(2, buf.at[p.down_slot, pl.ds(0, half)], p.up)
        self.fwd_down = copy(3, buf.at[p.up_slot, pl.ds(half, half)], p.down)
        self.own_side = copy(4, src, p.partner, own)
        self.down_side = copy(5, buf.at[p.down_slot], p.partner)
        self.up_side = copy(6, buf.at[p.up_slot], p.partner)
        self.far_side = copy(7, buf.at[p.far_slot], p.partner)

    def start(self):
        self.own_up.start()
        self.own_down.start()
        self.own_side.start()

    def forward(self):
        self.own_up.wait_recv()
        self.fwd_up.start()
        self.down_side.start()
        self.own_down.wait_recv()
        self.fwd_down.start()
        self.up_side.start()

    def last(self):
        self.fwd_up.wait_recv()
        self.fwd_down.wait_recv()
        self.far_side.start()
        for copy in (self.own_side, self.down_side, self.up_side, self.far_side):
            copy.wait_recv()

    def finish(self):
        for copy in (self.own_up, self.own_down, self.fwd_up, self.fwd_down,
                     self.own_side, self.down_side, self.up_side, self.far_side):
            copy.wait_send()


def dispatch_kernel(num_stages, capacity, x_ref, ids_ref, gate_ref, dy_ref,
                    xs_ref, q_ref, xf_ref, rgb_ref, rgf_ref,
                    dy_buf, xb_buf, xf_buf, ids_buf, gate_buf, hot_ref, stage_ref,
                    send_sems, recv_sems, hop_send, hop_recv, local_sem, out_sems):
    p = Peers(num_stages)
    num_local = xs_ref.shape[0]
    keep = pltpu.make_async_copy(dy_ref, dy_buf.at[p.own], local_sem)
    keep.start()
    greet((p.up, p.down, p.partner, p.after, p.before))
    hops = []
    for i, (src, buf) in enumerate(((ids_ref, ids_buf), (gate_ref, gate_buf),
                                    (x_ref.at[0], xb_buf), (x_ref.at[1], xf_buf))):
        hops.append(send(src, buf.at[p.own], hop_send.at[i], hop_recv.at[i], p.after))
    spread = [Spread(p, src, buf, send_sems.at[i], recv_sems.at[i]) for i, (src, buf) in enumerate((
        (ids_buf.at[p.own], ids_buf), (gate_buf.at[p.own], gate_buf), (xb_buf.at[p.own], xb_buf),
        (xf_buf.at[p.own], xf_buf), (dy_ref, dy_buf)))]
    s_ids, s_gate, s_xb, s_xf, s_dy = spread
    hops[0].start()
    hops[1].start()
    hops[2].start()
    s_dy.start()
    hops[3].start()
    hops[0].wait_recv()
    s_ids.start()
    hops[1].wait_recv()
    s_gate.start()
    s_ids.forward()
    s_gate.forward()
    s_dy.forward()
    hops[2].wait_recv()
    s_xb.start()
    s_ids.last()
    s_gate.last()

    def route_step(s, carry):
        for mb, out in ((0, rgb_ref), (1, rgf_ref)):
            rank, gate = routing_rows(gate_buf[s, mb], ids_buf[s, mb], p.rank, num_local)
            out[s, 0:8] = rank
            out[s, 8:16] = gate
        fill_onehot(hot_ref.at[s], rgb_ref[s, 0:8], capacity)
        return carry

    lax.fori_loop(0, TG, route_step, 0)
    s_dy.last()
    keep.wait()

    def put(slot, s, out_ref):
        rows = pl.ds(pl.multiple_of(s * capacity, 16), capacity)
        return pltpu.make_async_copy(stage_ref.at[slot], out_ref.at[:, rows], out_sems.at[slot])

    def gather(buf, out_ref, lo, hi, gates):
        def step(s, carry):
            slot = lax.rem(s, 2)

            @pl.when(s >= lo + 2)
            def _():
                put(slot, s - 2, out_ref).wait()

            rows = jnp.dot(hot_ref[s], buf[s], preferred_element_type=F32)
            if gates is None:
                stage_ref[slot] = rows.astype(BF16).reshape(stage_ref.shape[1:])
            else:
                for k in range(num_local):
                    col = gate_column(gates[s, k:k + 1], gates[s, 8 + k:9 + k], capacity)
                    stage_ref[slot, k] = (col * rows[k * capacity:(k + 1) * capacity]).astype(BF16)
            put(slot, s, out_ref).start()
            return carry

        lax.fori_loop(lo, hi, step, 0)
        for s in (hi - 2, hi - 1):
            put(s % 2, s, out_ref).wait()

    gather(dy_buf, q_ref, 0, 4, rgb_ref)
    s_xb.forward()
    hops[3].wait_recv()
    s_xf.start()
    gather(dy_buf, q_ref, 4, 8, rgb_ref)
    s_xb.last()
    gather(xb_buf, xs_ref, 0, 8, None)
    s_xf.forward()

    def hot_step(s, carry):
        fill_onehot(hot_ref.at[s], rgf_ref[s, 0:8], capacity)
        return carry

    lax.fori_loop(0, TG, hot_step, 0)
    s_xf.last()
    gather(xf_buf, xf_ref, 0, 8, None)
    for s in spread:
        s.finish()
    for hop in hops:
        hop.wait_send()


def dispatch_rows(x_acts, ids, gates, dy, capacity, num_stages):
    tokens, width = dy.shape
    num_local = 8
    slot_shape = jax.ShapeDtypeStruct((num_local, TG * capacity, width), BF16)
    rg_shape = jax.ShapeDtypeStruct((TG, 16, tokens), F32)
    any_spec, vmem_spec = pl.BlockSpec(memory_space=pl.ANY), pl.BlockSpec(memory_space=pltpu.VMEM)
    return pl.pallas_call(
        functools.partial(dispatch_kernel, num_stages, capacity),
        in_specs=[any_spec] * 4,
        out_specs=[any_spec] * 3 + [vmem_spec] * 2,
        out_shape=[slot_shape] * 3 + [rg_shape] * 2,
        scratch_shapes=[
            pltpu.VMEM((TG, tokens, width), BF16), pltpu.VMEM((TG, tokens, width), BF16),
            pltpu.VMEM((TG, tokens, width), BF16), pltpu.VMEM((TG,) + ids.shape, jnp.int32),
            pltpu.VMEM((TG,) + gates.shape, F32), pltpu.VMEM((TG, num_local * capacity, tokens), BF16),
            pltpu.VMEM((2, num_local, capacity, width), BF16),
            pltpu.SemaphoreType.DMA((5, 8)), pltpu.SemaphoreType.DMA((5, 8)),
            pltpu.SemaphoreType.DMA((4,)), pltpu.SemaphoreType.DMA((4,)),
            pltpu.SemaphoreType.DMA, pltpu.SemaphoreType.DMA((2,))],
        compiler_params=pltpu.CompilerParams(collective_id=1, has_side_effects=True,
                                             vmem_limit_bytes=56 << 20),
        cost_estimate=pl.CostEstimate(flops=40 * 10 ** 9, bytes_accessed=40 << 20, transcendentals=0),
        name='dispatch_rows',
    )(x_acts, ids, gates, dy)


def backward_kernel(x_ref, q_ref, wall_ref, dw_ref, dx_ref, dab_ref):
    x, q = x_ref[0], q_ref[0]
    width, hid = x.shape[1], dab_ref.shape[1] // 2
    wcat, wout = wall_ref[0, :width], wall_ref[0, width:]
    pre = jnp.dot(x, wcat, preferred_element_type=F32)
    a, b = pre[:, :hid], pre[:, hid:]
    sig = jax.nn.sigmoid(a)
    act = a * sig
    h = (act * b).astype(BF16)
    dw_ref[0, width:] = lax.dot_general(h, q, (((0,), (0,)), ((), ())), preferred_element_type=F32)
    u = lax.dot_general(q, wout, (((1,), (1,)), ((), ())), preferred_element_type=F32)
    dab_ref[:, :hid] = (u * b * sig * (1.0 + a * (1.0 - sig))).astype(BF16)
    dab_ref[:, hid:] = (u * act).astype(BF16)
    dab = dab_ref[...]
    dw_ref[0, :width] = lax.dot_general(x, dab, (((0,), (0,)), ((), ())), preferred_element_type=F32)
    dx = lax.dot_general(dab, wcat, (((1,), (1,)), ((), ())), preferred_element_type=F32)
    dx_ref[0] = dx.astype(BF16)


def expert_backward(xs, q, wall, hid):
    num_local, rows, width = xs.shape
    row_block = pl.BlockSpec((1, rows, width), lambda e: (e, 0, 0))
    wgt_block = pl.BlockSpec((1,) + wall.shape[1:], lambda e: (e, 0, 0))
    return pl.pallas_call(
        backward_kernel,
        grid=(num_local,),
        in_specs=[row_block, row_block, wgt_block],
        out_specs=[wgt_block, row_block],
        out_shape=[jax.ShapeDtypeStruct(wall.shape, F32), jax.ShapeDtypeStruct(xs.shape, BF16)],
        scratch_shapes=[pltpu.VMEM((rows, 2 * hid), BF16)],
        cost_estimate=pl.CostEstimate(flops=16 * num_local * rows * width * hid, bytes_accessed=38 << 20,
                                      transcendentals=num_local * rows * hid),
        name='expert_backward',
    )(xs, q, wall)


def forward_kernel(capacity, rg_ref, x_ref, wall_ref, c_ref):
    e = pl.program_id(0)
    x = x_ref[0]
    width = x.shape[1]
    wcat, wout = wall_ref[0, :width], wall_ref[0, width:]
    hid = wout.shape[0]
    pre = jnp.dot(x, wcat, preferred_element_type=F32)
    a, b = pre[:, :hid], pre[:, hid:]
    h = (a * jax.nn.sigmoid(a) * b).astype(BF16)
    o = jnp.dot(h, wout, preferred_element_type=F32)
    for s in range(rg_ref.shape[0]):
        col = gate_column(rg_ref[s, pl.ds(e, 1)], rg_ref[s, pl.ds(8 + e, 1)], capacity)
        c_ref[0, s * capacity:(s + 1) * capacity] = (col * o[s * capacity:(s + 1) * capacity]).astype(BF16)


def expert_forward(rg, xs, wall, hid, capacity):
    num_local, rows, width = xs.shape
    row_block = pl.BlockSpec((1, rows, width), lambda e: (e, 0, 0))
    return pl.pallas_call(
        functools.partial(forward_kernel, capacity),
        grid=(num_local,),
        in_specs=[pl.BlockSpec(rg.shape, lambda e: (0, 0, 0)), row_block,
                  pl.BlockSpec((1,) + wall.shape[1:], lambda e: (e, 0, 0))],
        out_specs=row_block,
        out_shape=jax.ShapeDtypeStruct(xs.shape, BF16),
        cost_estimate=pl.CostEstimate(flops=6 * num_local * rows * width * hid, bytes_accessed=20 << 20,
                                      transcendentals=num_local * rows * hid),
        name='expert_forward',
    )(rg, xs, wall)


def combine_kernel(num_stages, capacity, rg_ref, c_ref, out_ref, hot_ref, side_out, side_in, acc, half_in,
                   up_in, down_in, send_sems, recv_sems):
    p = Peers(num_stages)
    half = acc.shape[1] // 2
    low, high = pl.ds(0, half), pl.ds(half, half)
    greet((p.up, p.down, p.partner))

    def partial_sum(slot):
        fill_onehot(hot_ref, rg_ref[slot, 0:8], capacity)
        start = pl.ds(pl.multiple_of(slot * capacity, 16), capacity)
        rows = c_ref[:, start].reshape(hot_ref.shape[0], c_ref.shape[2])
        return lax.dot_general(hot_ref[...], rows, (((0,), (0,)), ((), ())), preferred_element_type=F32)

    sides = [send(side_out.at[d], side_in.at[d], send_sems.at[d], recv_sems.at[d], p.partner) for d in range(4)]
    far_up = send(acc.at[2, low], half_in.at[0], send_sems.at[4], recv_sems.at[4], p.up)
    far_down = send(acc.at[2, high], half_in.at[1], send_sems.at[5], recv_sems.at[5], p.down)
    up_a = send(acc.at[1, high], up_in.at[high], send_sems.at[6], recv_sems.at[6], p.up)
    up_b = send(acc.at[1, low], up_in.at[low], send_sems.at[7], recv_sems.at[7], p.up)
    down_a = send(acc.at[3, low], down_in.at[low], send_sems.at[8], recv_sems.at[8], p.down)
    down_b = send(acc.at[3, high], down_in.at[high], send_sems.at[9], recv_sems.at[9], p.down)

    def both(d):
        side_out[d] = partial_sum(p.slot(d, True))
        sides[d].start()
        acc[d] = partial_sum(p.slot(d))

    def add_side(d):
        sides[d].wait_recv()
        acc[d] = acc[d] + side_in[d]

    both(2)
    add_side(2)
    far_up.start()
    far_down.start()
    both(1)
    add_side(1)
    up_a.start()
    both(3)
    add_side(3)
    down_a.start()
    both(0)
    add_side(0)
    far_up.wait_recv()
    acc[1, low] = acc[1, low] + half_in[0]
    up_b.start()
    far_down.wait_recv()
    acc[3, high] = acc[3, high] + half_in[1]
    down_b.start()
    up_a.wait_recv()
    up_b.wait_recv()
    down_a.wait_recv()
    down_b.wait_recv()
    out_ref[...] = (acc[0] + up_in[...] + down_in[...]).astype(BF16)
    for copy in sides + [far_up, far_down, up_a, up_b, down_a, down_b]:
        copy.wait_send()


def combine_rows(rg, slots, capacity, num_stages, collective_id):
    num_local, _, width = slots.shape
    tokens = rg.shape[2]
    vmem_spec = pl.BlockSpec(memory_space=pltpu.VMEM)
    return pl.pallas_call(
        functools.partial(combine_kernel, num_stages, capacity),
        in_specs=[vmem_spec, vmem_spec],
        out_specs=vmem_spec,
        out_shape=jax.ShapeDtypeStruct((tokens, width), BF16),
        scratch_shapes=[
            pltpu.VMEM((num_local * capacity, tokens), BF16),
            pltpu.VMEM((4, tokens, width), F32), pltpu.VMEM((4, tokens, width), F32),
            pltpu.VMEM((4, tokens, width), F32), pltpu.VMEM((2, tokens // 2, width), F32),
            pltpu.VMEM((tokens, width), F32), pltpu.VMEM((tokens, width), F32),
            pltpu.SemaphoreType.DMA((10,)), pltpu.SemaphoreType.DMA((10,))],
        compiler_params=pltpu.CompilerParams(collective_id=collective_id, has_side_effects=True,
                                             vmem_limit_bytes=56 << 20),
        cost_estimate=pl.CostEstimate(flops=20 * 10 ** 9, bytes_accessed=8 << 20, transcendentals=0),
        name='combine_rows_%d' % collective_id,
    )(rg, slots)


def solution(mesh):
    group_size = mesh.shape['expert']
    num_stages = mesh.shape['stage']
    to_prev = [((i + 1) % num_stages, i) for i in range(num_stages)]
    rows_of = group_size // TG
    wgt_groups = [[z * TG + r for z in range(rows_of)] for r in range(TG)]

    def device_fn(x_acts, expert_ids, gate_wts, w_in, w_up, w_out, d_out):
        tokens, width = x_acts.shape[2], x_acts.shape[3]
        hid = w_in.shape[3]
        capacity = 96

        def gather_wgt(arr):
            return lax.all_gather(arr, 'expert', axis_index_groups=wgt_groups, axis=0)

        def reduce_wgt(arr):
            return lax.psum_scatter(arr, 'expert', axis_index_groups=wgt_groups, scatter_dimension=0, tiled=False)

        wall = jnp.concatenate([jnp.concatenate([w_in[0, 0], w_up[0, 0]], axis=1), w_out[0, 0]], axis=0)
        wall = gather_wgt(wall)
        ids = jnp.swapaxes(expert_ids[:, 0], 1, 2)
        gates = jnp.swapaxes(gate_wts[:, 0], 1, 2)
        xs, q, xs_f, rg, rg_f = dispatch_rows(x_acts[:, 0], ids, gates, d_out[0], capacity, num_stages)
        dwall, dxs = expert_backward(xs, q, wall, hid)
        xs_f, dxs = lax.optimization_barrier((xs_f, dxs))
        dwall = reduce_wgt(dwall)
        dx = combine_rows(rg, dxs, capacity, num_stages, 2)
        dx = lax.ppermute(dx, 'stage', to_prev)
        c = expert_forward(rg_f, xs_f, wall, hid, capacity)
        y = combine_rows(rg_f, c, capacity, num_stages, 3)
        dwall = dwall.astype(BF16)
        return (y[None], dx[None], dwall[None, None, :width, :hid], dwall[None, None, :width, hid:],
                dwall[None, None, width:])

    tok_spec = P(None, 'stage', 'expert', None)
    w_spec = P('stage', 'expert', None, None)
    row_spec = P('stage', 'expert', None)
    return jax.shard_map(device_fn, mesh=mesh,
                         in_specs=(tok_spec, tok_spec, tok_spec, w_spec, w_spec, w_spec, row_spec),
                         out_specs=(row_spec, row_spec, w_spec, w_spec, w_spec), check_vma=False)
```

time: 497 us -> 255 us (0.51)
  waiting for transfers between devices: 359 us -> 32.4 us
  Pallas kernels: 80.5 us -> 198 us
  blocking collectives: 19.1 us -> 0 us
  starting transfers between devices: 8.01 us -> 2.75 us
    reduce_scatter x2 -> x1, waiting for transfers between devices: 149 us -> 27.5 us  [reduce_wgt(): lax.psum_scatter(arr, 'expert', axis_index_groups=wgt_groups, scatter_dim...]
    pallas_call x4 -> x3, Pallas kernels: 47.8 us -> 165 us  [the longest x2 91.5 us: combine_rows(): pl.pallas_call(functools.partial(combine_kernel, num_stages, capacity), i...]
    reduce_scatter x2 -> x0, waiting for transfers between devices: 76.6 us -> none  [reduce_tok(): lax.psum_scatter(arr, 'expert', axis_index_groups=tok_groups, scatter_dim...]
    all_gather x2 -> x1, waiting for transfers between devices: 81.3 us -> 4.93 us  [gather_wgt(): return lax.all_gather(arr, 'expert', axis_index_groups=wgt_groups, axis=0)]
    ppermute x3 -> x0, waiting for transfers between devices: 25.3 us -> none  [the longest x1 10.8 us: device_fn(): x_fwd = lax.ppermute(x_acts[1, 0], 'stage', to_next)]
    all_gather x3 -> x0, waiting for transfers between devices: 23.1 us -> none  [gather_tok(): return lax.all_gather(arr, 'expert', axis_index_groups=tok_groups, axis=0)]
    all_gather x1 -> x0, blocking collectives: 19.1 us -> none  [gather_tok(): return lax.all_gather(arr, 'expert', axis_index_groups=tok_groups, axis=0)]
    ppermute x3 -> x0, starting transfers between devices: 5.16 us -> none  [the longest x1 2.11 us: device_fn(): x_bwd = lax.ppermute(x_acts[0, 0], 'stage', to_next)]
  transfers between devices with their start and end apart: 13 -> 3, of which waited for: 11 -> 2; matrix products, arithmetic and copies ran while one was open for 3% -> 0% of each run, Pallas kernels for 16% -> 69%
where the time goes in v2:
time: 255 us
  Pallas kernels  198 us (78%)
  waiting for transfers between devices  32.4 us (13%)
  between operations  14.1 us (6%)
  other arithmetic  5.06 us (2%)
  local copies, waits for them, and re-layouts  3.13 us (1%)
  starting transfers between devices  2.75 us (1%)
    pallas_call x2, Pallas kernels, combine_rows(): pl.pallas_call(functools.partial(combine_kernel, num_stages, capacity), i...  91.5 us
    pallas_call x1, Pallas kernels, dispatch_rows(): pl.pallas_call(functools.partial(dispatch_kernel, num_stages, capacity),...  73.4 us
    reduce_scatter x1, waiting for transfers between devices, reduce_wgt(): lax.psum_scatter(arr, 'expert', axis_index_groups=wgt_groups, scatter_dim...  27.5 us
    pallas_call x1, Pallas kernels, expert_backward(): pl.pallas_call(backward_kernel, grid=(num_local,), in_specs=[row_block, r...  21.1 us
    pallas_call x1, Pallas kernels, expert_forward(): pl.pallas_call(functools.partial(forward_kernel, capacity), grid=(num_loc...  11.6 us
  transfers between devices with their start and end apart: 3, of which 2 were waited for; matrix products, arithmetic and copies ran while one was open for 0% of the time, Pallas kernels for 69%

profile of v2, /device:TPU:1, one launch (start us, length us, event | category | flops | bytes accessed | tf_op | source)
XLA Modules:
  0.0 255.0 jit_solution(4481649352592625786)
XLA Ops:
  7.2 0.0 all-gather.3.cloned.1.call-start
  7.2 2.1 pad_maximum_fusion
  9.3 0.0 all-gather.3.cloned.1.call-update
  9.3 0.0 reduce-scatter.2.cloned.1.call-start
  9.3 73.4 %dispatch_rows.1 = (bf16[8,768,512]{2,1,0:T(8,128)(2,1)}, bf16[8,768,512]{2,1,0:T(8,128)(2,1)}, bf16[8,768,512]{2,1,0:T(8,128)(2,1)}, f32[8,16,512]{2,1,0:T(8,128)}, f32[8,16,512]{2,1,0:T(8,128)}) custom-call(bf16[2,512,512]{2,1,0:T(8,128)(2,1)} %bitcast.29, s32[2,8,512]{2,1,0:T(8,128)} %bitcast.31, f32[2,8,512]{2,1,0:T(8,128)} %bitcast.32, ...), custom_call_target="tpu_custom_call" | custom-call | flops 40000000000 | bytes 41943040 | tf_op jit(solution)/shard_map/dispatch_rows/pallas_call | solution.py:225
  82.7 4.9 %all-gather.3.cloned.1.call-done = bf16[6144,512]{1,0:T(8,128)(2,1)} async-done(((bf16[768,512]{1,0:T(8,128)(2,1)}), bf16[6144,512]{1,0:T(8,128)(2,1)}) %all-gather.3.cloned.1.call-update) | async-done | bytes 6291472 | tf_op jit(solution)/shard_map/all_gather | solution.py:404
  87.7 21.1 %expert_backward.1 = (f32[8,768,512]{2,1,0:T(8,128)}, bf16[8,768,512]{2,1,0:T(8,128)(2,1)}) custom-call(bf16[8,768,512]{2,1,0:T(8,128)(2,1)} %get-tuple-element.16.x_ref, bf16[8,768,512]{2,1,0:T(8,128)(2,1)} %get-tuple-element.17.q_ref, bf16[8,768,512]{2,1,0:T(8,128)(2,1)} %bitcast.22), custom_call_target="tpu_custom_call" | custom-call | flops 12884901888 | bytes 39845888 | tf_op jit(solution)/shard_map/expert_backward/pallas_call | solution.py:268
  108.7 0.0 reduce-scatter.2.cloned.1.call-update
  108.8 46.2 %combine_rows_2.1 = bf16[512,512]{1,0:T(8,128)(2,1)} custom-call(f32[8,16,512]{2,1,0:T(8,128)} %get-tuple-element.20.rg_ref, bf16[8,768,512]{2,1,0:T(8,128)(2,1)} %get-tuple-element.21.c_ref), custom_call_target="tpu_custom_call" | custom-call | flops 20000000000 | bytes 8388608 | tf_op jit(solution)/shard_map/combine_rows_2/pallas_call | solution.py:373
  154.9 2.7 %collective-permute-start = (bf16[512,512]{1,0:T(8,128)(2,1)}, bf16[512,512]{1,0:T(8,128)(2,1)S(1)}, u32[]{:S(2)}, u32[]{:S(2)}) collective-permute-start(bf16[512,512]{1,0:T(8,128)(2,1)} %combine_rows_2.1), channel_id=1, source_target_pairs={{64,0},{128,64},{192,128},{0,192},{65,1},{129,65},{193,129},{1,193... | collective-permute-start | bytes 1572872 | tf_op jit(solution)/shard_map/ppermute | solution.py:418
  157.6 11.6 %expert_forward.1.c_ref = bf16[8,768,512]{2,1,0:T(8,128)(2,1)} custom-call(f32[8,16,512]{2,1,0:T(8,128)} %get-tuple-element.14.rg_ref, bf16[8,768,512]{2,1,0:T(8,128)(2,1)} %get-tuple-element.19.x_ref, bf16[8,768,512]{2,1,0:T(8,128)(2,1)} %bitcast.23), custom_call_target="tpu_custom_call" | custom-call | flops 4831838208 | bytes 20971520 | tf_op jit(solution)/shard_map/expert_forward/pallas_call | solution.py:299
  169.2 45.3 %combine_rows_3.1 = bf16[512,512]{1,0:T(8,128)(2,1)} custom-call(f32[8,16,512]{2,1,0:T(8,128)} %get-tuple-element.14.rg_ref, bf16[8,768,512]{2,1,0:T(8,128)(2,1)} %expert_forward.1.c_ref), custom_call_target="tpu_custom_call" | custom-call | flops 20000000000 | bytes 8388608 | tf_op jit(solution)/shard_map/combine_rows_3/pallas_call | solution.py:373
  214.6 0.0 copy-start
  214.6 0.0 collective-permute-done
  214.6 27.5 %reduce-scatter.2.cloned.1.call-done = f32[1,768,512]{2,1,0:T(8,128)} async-done(((f32[8,768,512]{2,1,0:T(8,128)}), f32[1,768,512]{2,1,0:T(8,128)}) %reduce-scatter.2.cloned.1.call-update) | async-done | bytes 1572880 | tf_op jit(solution)/shard_map/reduce_scatter | solution.py:407
  242.0 1.5 convert_element_type.6
  243.6 0.7 slice_bitcast_fusion
  244.3 1.5 convert_bitcast_fusion
  245.8 0.8 slice_bitcast_fusion.1
  246.6 0.0 copy-done
  246.6 0.8 copy.14
  247.4 0.8 copy.15
Async XLA Ops:
  7.2 80.5 %all-gather.3.cloned.1.call-start = ((), (), s32[]{:S(2)}) async-start(), calls=%async_computation.2 | async-start | bytes 7077888 | tf_op jit(solution)/shard_map/all_gather | solution.py:404
  9.3 232.8 %reduce-scatter.2.cloned.1.call-start = ((), (), s32[]{:S(2)}) async-start(), calls=%async_computation.1 | async-start | bytes 14155776 | tf_op jit(solution)/shard_map/reduce_scatter | solution.py:407
  154.9 59.7 %collective-permute-start = (bf16[512,512]{1,0:T(8,128)(2,1)}, bf16[512,512]{1,0:T(8,128)(2,1)S(1)}, u32[]{:S(2)}, u32[]{:S(2)}) collective-permute-start(bf16[512,512]{1,0:T(8,128)(2,1)} %combine_rows_2.1), channel_id=1, source_target_pairs={{64,0},{128,64},{192,128},{0,192},{65,1},{129,65},{193,129},{1,193... | collective-permute-start | bytes 1572872 | tf_op jit(solution)/shard_map/ppermute | solution.py:418
  214.6 32.1 %copy-start = (bf16[512,512]{1,0:T(8,128)(2,1)S(1)}, bf16[512,512]{1,0:T(8,128)(2,1)}, u32[]{:S(2)}) copy-start(bf16[512,512]{1,0:T(8,128)(2,1)} %combine_rows_3.1) | copy-start | bytes 1572868
Sparse Core Ops, SparseCore 0:
  9.8 77.8 all-gather.2
  108.9 133.1 reduce-scatter.1

commit v3 on v2

--- a/solution.py
+++ b/solution.py
@@ -46,11 +46,14 @@
 
 
 class Peers:
-    def __init__(self, num_stages):
+    def __init__(self, num_stages, group_size=64):
         stage, me = lax.axis_index('stage'), lax.axis_index('expert')
         self.rank = lax.rem(me, TG)
         self.base = me - self.rank
-        self.stage = stage
+        self.zpos = self.base // TG
+        self.z_size = group_size // TG
+        self.z_up = (stage, self.z_slot(1) * TG + self.rank)
+        self.z_down = (stage, self.z_slot(-1) * TG + self.rank)
         self.core = lax.rem(self.rank, 2)
         self.ypos = (self.rank - self.core) // 2
         self.own, self.up_slot = self.rank, self.slot(1)
@@ -61,6 +64,9 @@
         self.after = (lax.rem(stage + 1, num_stages), me)
         self.before = (lax.rem(stage + num_stages - 1, num_stages), me)
 
+    def z_slot(self, offset):
+        return lax.rem(self.zpos + offset + self.z_size, self.z_size)
+
     def slot(self, offset, other_core=False):
         core = 1 - self.core if other_core else self.core
         return lax.rem(self.ypos + offset, 4) * 2 + core
@@ -122,15 +128,70 @@
             copy.wait_send()
 
 
-def dispatch_kernel(num_stages, capacity, x_ref, ids_ref, gate_ref, dy_ref,
-                    xs_ref, q_ref, xf_ref, rgb_ref, rgf_ref,
-                    dy_buf, xb_buf, xf_buf, ids_buf, gate_buf, hot_ref, stage_ref,
-                    send_sems, recv_sems, hop_send, hop_recv, local_sem, out_sems):
+class WeightRing:
+    def __init__(self, p, buf, send_sems, recv_sems):
+        self.rows = buf.shape[1] // 4
+        self.copies = []
+        for way, device in ((0, p.z_up), (1, p.z_down)):
+            way_copies = []
+            for i in range(14):
+                step, pos = divmod(i, 4)
+                piece = (pos + 2 * way) % 4
+                slot = p.z_slot(-step if way == 0 else step)
+                ref = buf.at[slot, pl.ds(piece * self.rows, self.rows)]
+                way_copies.append(send(ref, ref, send_sems.at[way, i], recv_sems.at[way, i], device))
+            self.copies.append(way_copies)
+
+    def start(self):
+        for pos in range(4):
+            for way in range(2):
+                self.copies[way][pos].start()
+
+    def event(self, i):
+        for way in range(2):
+            self.copies[way][i].wait_recv()
+            if i + 4 < 14:
+                self.copies[way][i + 4].start()
+
+    def finish(self):
+        for way in range(2):
+            for copy in self.copies[way]:
+                copy.wait_send()
+
+
+def expert_step(x, q, wcat, wout, dw_ref, dx_ref, dab_ref):
+    width, hid = wcat.shape[0], wout.shape[0]
+    pre = jnp.dot(x, wcat, preferred_element_type=F32)
+    a, b = pre[:, :hid], pre[:, hid:]
+    sig = jax.nn.sigmoid(a)
+    act = a * sig
+    h = (act * b).astype(BF16)
+    dw_ref[width:] = lax.dot_general(h, q, (((0,), (0,)), ((), ())), preferred_element_type=F32)
+    u = lax.dot_general(q, wout, (((1,), (1,)), ((), ())), preferred_element_type=F32)
+    dab_ref[:, :hid] = (u * b * sig * (1.0 + a * (1.0 - sig))).astype(BF16)
+    dab_ref[:, hid:] = (u * act).astype(BF16)
+    dab = dab_ref[...]
+    dw_ref[:width] = lax.dot_general(x, dab, (((0,), (0,)), ((), ())), preferred_element_type=F32)
+    dx = lax.dot_general(dab, wcat, (((1,), (1,)), ((), ())), preferred_element_type=F32)
+    dx_ref[...] = dx.astype(BF16)
+
+
+def dispatch_kernel(num_stages, capacity, x_ref, ids_ref, gate_ref, dy_ref, wi_ref, wu_ref, wo_ref,
+                    dw_ref, dxs_ref, xf_ref, wall_ref, rgb_ref, rgf_ref,
+                    dy_buf, xb_buf, xf_buf, ids_buf, gate_buf, hot_ref, xs_buf, q_buf, wall_buf, dw_buf, dab_ref,
+                    send_sems, recv_sems, hop_send, hop_recv, z_send, z_recv, local_sems, dw_sems, dx_sems):
     p = Peers(num_stages)
-    num_local = xs_ref.shape[0]
-    keep = pltpu.make_async_copy(dy_ref, dy_buf.at[p.own], local_sem)
-    keep.start()
-    greet((p.up, p.down, p.partner, p.after, p.before))
+    num_local = xs_buf.shape[0]
+    width, hid = wi_ref.shape
+    block = wall_buf.at[p.z_slot(0)]
+    keep = [pltpu.make_async_copy(wi_ref, block.at[pl.ds(0, width), pl.ds(0, hid)], local_sems.at[0]),
+            pltpu.make_async_copy(wu_ref, block.at[pl.ds(0, width), pl.ds(hid, hid)], local_sems.at[1]),
+            pltpu.make_async_copy(wo_ref, block.at[pl.ds(width, hid)], local_sems.at[2])]
+    keep_dy = pltpu.make_async_copy(dy_ref, dy_buf.at[p.own], local_sems.at[3])
+    for copy in keep:
+        copy.start()
+    keep_dy.start()
+    greet((p.up, p.down, p.partner, p.after, p.before, p.z_up, p.z_down))
     hops = []
     for i, (src, buf) in enumerate(((ids_ref, ids_buf), (gate_ref, gate_buf),
                                     (x_ref.at[0], xb_buf), (x_ref.at[1], xf_buf))):
@@ -139,20 +200,27 @@
         (ids_buf.at[p.own], ids_buf), (gate_buf.at[p.own], gate_buf), (xb_buf.at[p.own], xb_buf),
         (xf_buf.at[p.own], xf_buf), (dy_ref, dy_buf)))]
     s_ids, s_gate, s_xb, s_xf, s_dy = spread
+    ring = WeightRing(p, wall_buf, z_send, z_recv)
     hops[0].start()
     hops[1].start()
     hops[2].start()
     s_dy.start()
+    for copy in keep:
+        copy.wait()
+    ring.start()
     hops[3].start()
     hops[0].wait_recv()
     s_ids.start()
     hops[1].wait_recv()
     s_gate.start()
+    ring.event(0)
+    ring.event(1)
     s_ids.forward()
     s_gate.forward()
     s_dy.forward()
     hops[2].wait_recv()
     s_xb.start()
+    ring.event(2)
     s_ids.last()
     s_gate.last()
 
@@ -164,118 +232,160 @@
         fill_onehot(hot_ref.at[s], rgb_ref[s, 0:8], capacity)
         return carry
 
-    lax.fori_loop(0, TG, route_step, 0)
+    def rows_of(s):
+        return pl.ds(pl.multiple_of(s * capacity, 16), capacity)
+
+    def dy_step(s, carry):
+        rows = jnp.dot(hot_ref[s], dy_buf[s], preferred_element_type=F32)
+        for k in range(num_local):
+            col = gate_column(rgb_ref[s, k:k + 1], rgb_ref[s, 8 + k:9 + k], capacity)
+            q_buf[k, rows_of(s)] = (col * rows[k * capacity:(k + 1) * capacity]).astype(BF16)
+        return carry
+
+    def x_step(s, carry):
+        rows = jnp.dot(hot_ref[s], xb_buf[s], preferred_element_type=F32).astype(BF16)
+        for k in range(num_local):
+            xs_buf[k, rows_of(s)] = rows[k * capacity:(k + 1) * capacity]
+        return carry
+
+    half = TG // 2
+    lax.fori_loop(0, half, route_step, 0)
+    ring.event(3)
+    lax.fori_loop(half, TG, route_step, 0)
     s_dy.last()
-    keep.wait()
-
-    def put(slot, s, out_ref):
-        rows = pl.ds(pl.multiple_of(s * capacity, 16), capacity)
-        return pltpu.make_async_copy(stage_ref.at[slot], out_ref.at[:, rows], out_sems.at[slot])
-
-    def gather(buf, out_ref, lo, hi, gates):
-        def step(s, carry):
-            slot = lax.rem(s, 2)
-
-            @pl.when(s >= lo + 2)
-            def _():
-                put(slot, s - 2, out_ref).wait()
-
-            rows = jnp.dot(hot_ref[s], buf[s], preferred_element_type=F32)
-            if gates is None:
-                stage_ref[slot] = rows.astype(BF16).reshape(stage_ref.shape[1:])
-            else:
-                for k in range(num_local):
-                    col = gate_column(gates[s, k:k + 1], gates[s, 8 + k:9 + k], capacity)
-                    stage_ref[slot, k] = (col * rows[k * capacity:(k + 1) * capacity]).astype(BF16)
-            put(slot, s, out_ref).start()
-            return carry
-
-        lax.fori_loop(lo, hi, step, 0)
-        for s in (hi - 2, hi - 1):
-            put(s % 2, s, out_ref).wait()
-
-    gather(dy_buf, q_ref, 0, 4, rgb_ref)
+    keep_dy.wait()
+    ring.event(4)
+    lax.fori_loop(0, half, dy_step, 0)
+    ring.event(5)
+    lax.fori_loop(half, TG, dy_step, 0)
+    ring.event(6)
     s_xb.forward()
     hops[3].wait_recv()
     s_xf.start()
-    gather(dy_buf, q_ref, 4, 8, rgb_ref)
+    ring.event(7)
     s_xb.last()
-    gather(xb_buf, xs_ref, 0, 8, None)
-    s_xf.forward()
-
-    def hot_step(s, carry):
-        fill_onehot(hot_ref.at[s], rgf_ref[s, 0:8], capacity)
+    ring.event(8)
+    lax.fori_loop(0, half, x_step, 0)
+    ring.event(9)
+    lax.fori_loop(half, TG, x_step, 0)
+    ring.event(10)
+
+    def expert_of(i):
+        return p.z_slot((1 - 2 * lax.rem(i, 2)) * ((i + 1) // 2))
+
+    def put_dw(i):
+        slot = lax.rem(i, 2)
+        return pltpu.make_async_copy(dw_buf.at[slot], dw_ref.at[expert_of(i)], dw_sems.at[slot])
+
+    def put_dx(i):
+        e = expert_of(i)
+        return pltpu.make_async_copy(q_buf.at[e], dxs_ref.at[e], dx_sems.at[i])
+
+    put_xf = pltpu.make_async_copy(xf_buf, xf_ref, local_sems.at[0])
+    put_wall = pltpu.make_async_copy(wall_buf, wall_ref, local_sems.at[1])
+
+    def backward_step(i, carry):
+        @pl.when(i == 2)
+        def _():
+            ring.event(11)
+
+        @pl.when(i == 3)
+        def _():
+            s_xf.forward()
+
+        @pl.when(i == 4)
+        def _():
+            ring.event(12)
+
+        @pl.when(i == 6)
+        def _():
+            s_xf.last()
+            put_xf.start()
+
+        @pl.when(i == 7)
+        def _():
+            ring.event(13)
+            put_wall.start()
+
+        @pl.when(i >= 2)
+        def _():
+            put_dw(i - 2).wait()
+
+        e = expert_of(i)
+        expert_step(xs_buf[e], q_buf[e], wall_buf[e, :width], wall_buf[e, width:], dw_buf.at[lax.rem(i, 2)],
+                    q_buf.at[e], dab_ref)
+        put_dw(i).start()
+        put_dx(i).start()
         return carry
 
-    lax.fori_loop(0, TG, hot_step, 0)
-    s_xf.last()
-    gather(xf_buf, xf_ref, 0, 8, None)
+    lax.fori_loop(0, num_local, backward_step, 0)
+    put_xf.wait()
+    put_wall.wait()
+    for i in range(num_local):
+        put_dx(jnp.int32(i)).wait()
+    put_dw(jnp.int32(num_local - 2)).wait()
+    put_dw(jnp.int32(num_local - 1)).wait()
     for s in spread:
         s.finish()
     for hop in hops:
         hop.wait_send()
-
-
-def dispatch_rows(x_acts, ids, gates, dy, capacity, num_stages):
+    ring.finish()
+
+
+def dispatch_rows(x_acts, ids, gates, dy, w_in, w_up, w_out, capacity, num_stages):
     tokens, width = dy.shape
+    hid = w_in.shape[1]
     num_local = 8
     slot_shape = jax.ShapeDtypeStruct((num_local, TG * capacity, width), BF16)
     rg_shape = jax.ShapeDtypeStruct((TG, 16, tokens), F32)
+    wall_size = (num_local, width + hid, width)
     any_spec, vmem_spec = pl.BlockSpec(memory_space=pl.ANY), pl.BlockSpec(memory_space=pltpu.VMEM)
+    tok_buf = pltpu.VMEM((TG, tokens, width), BF16)
+    slot_buf = pltpu.VMEM((num_local, TG * capacity, width), BF16)
     return pl.pallas_call(
         functools.partial(dispatch_kernel, num_stages, capacity),
-        in_specs=[any_spec] * 4,
-        out_specs=[any_spec] * 3 + [vmem_spec] * 2,
-        out_shape=[slot_shape] * 3 + [rg_shape] * 2,
+        in_specs=[any_spec] * 7,
+        out_specs=[any_spec] * 4 + [vmem_spec] * 2,
+        out_shape=[jax.ShapeDtypeStruct(wall_size, F32), slot_shape,
+                   jax.ShapeDtypeStruct((TG, tokens, width), BF16), jax.ShapeDtypeStruct(wall_size, BF16),
+                   rg_shape, rg_shape],
         scratch_shapes=[
-            pltpu.VMEM((TG, tokens, width), BF16), pltpu.VMEM((TG, tokens, width), BF16),
-            pltpu.VMEM((TG, tokens, width), BF16), pltpu.VMEM((TG,) + ids.shape, jnp.int32),
+            tok_buf, tok_buf, tok_buf, pltpu.VMEM((TG,) + ids.shape, jnp.int32),
             pltpu.VMEM((TG,) + gates.shape, F32), pltpu.VMEM((TG, num_local * capacity, tokens), BF16),
-            pltpu.VMEM((2, num_local, capacity, width), BF16),
+            slot_buf, slot_buf, pltpu.VMEM(wall_size, BF16), pltpu.VMEM((2,) + wall_size[1:], F32),
+            pltpu.VMEM((TG * capacity, 2 * hid), BF16),
             pltpu.SemaphoreType.DMA((5, 8)), pltpu.SemaphoreType.DMA((5, 8)),
             pltpu.SemaphoreType.DMA((4,)), pltpu.SemaphoreType.DMA((4,)),
-            pltpu.SemaphoreType.DMA, pltpu.SemaphoreType.DMA((2,))],
+            pltpu.SemaphoreType.DMA((2, 14)), pltpu.SemaphoreType.DMA((2, 14)),
+            pltpu.SemaphoreType.DMA((4,)), pltpu.SemaphoreType.DMA((2,)), pltpu.SemaphoreType.DMA((num_local,))],
         compiler_params=pltpu.CompilerParams(collective_id=1, has_side_effects=True,
-                                             vmem_limit_bytes=56 << 20),
+                                             vmem_limit_bytes=63 << 20),
         cost_estimate=pl.CostEstimate(flops=40 * 10 ** 9, bytes_accessed=40 << 20, transcendentals=0),
         name='dispatch_rows',
-    )(x_acts, ids, gates, dy)
-
-
-def backward_kernel(x_ref, q_ref, wall_ref, dw_ref, dx_ref, dab_ref):
-    x, q = x_ref[0], q_ref[0]
-    width, hid = x.shape[1], dab_ref.shape[1] // 2
-    wcat, wout = wall_ref[0, :width], wall_ref[0, width:]
-    pre = jnp.dot(x, wcat, preferred_element_type=F32)
-    a, b = pre[:, :hid], pre[:, hid:]
-    sig = jax.nn.sigmoid(a)
-    act = a * sig
-    h = (act * b).astype(BF16)
-    dw_ref[0, width:] = lax.dot_general(h, q, (((0,), (0,)), ((), ())), preferred_element_type=F32)
-    u = lax.dot_general(q, wout, (((1,), (1,)), ((), ())), preferred_element_type=F32)
-    dab_ref[:, :hid] = (u * b * sig * (1.0 + a * (1.0 - sig))).astype(BF16)
-    dab_ref[:, hid:] = (u * act).astype(BF16)
-    dab = dab_ref[...]
-    dw_ref[0, :width] = lax.dot_general(x, dab, (((0,), (0,)), ((), ())), preferred_element_type=F32)
-    dx = lax.dot_general(dab, wcat, (((1,), (1,)), ((), ())), preferred_element_type=F32)
-    dx_ref[0] = dx.astype(BF16)
-
-
-def expert_backward(xs, q, wall, hid):
-    num_local, rows, width = xs.shape
-    row_block = pl.BlockSpec((1, rows, width), lambda e: (e, 0, 0))
-    wgt_block = pl.BlockSpec((1,) + wall.shape[1:], lambda e: (e, 0, 0))
+    )(x_acts, ids, gates, dy, w_in, w_up, w_out)
+
+
+def gather_kernel(capacity, rg_ref, x_ref, xs_ref, hot_ref):
+    fill_onehot(hot_ref, rg_ref[0, 0:8], capacity)
+    rows = jnp.dot(hot_ref[...], x_ref[0], preferred_element_type=F32)
+    xs_ref[...] = rows.astype(BF16).reshape(xs_ref.shape)
+
+
+def gather_rows(rg, x_all, capacity):
+    groups, tokens, width = x_all.shape
+    num_local = 8
     return pl.pallas_call(
-        backward_kernel,
-        grid=(num_local,),
-        in_specs=[row_block, row_block, wgt_block],
-        out_specs=[wgt_block, row_block],
-        out_shape=[jax.ShapeDtypeStruct(wall.shape, F32), jax.ShapeDtypeStruct(xs.shape, BF16)],
-        scratch_shapes=[pltpu.VMEM((rows, 2 * hid), BF16)],
-        cost_estimate=pl.CostEstimate(flops=16 * num_local * rows * width * hid, bytes_accessed=38 << 20,
-                                      transcendentals=num_local * rows * hid),
-        name='expert_backward',
-    )(xs, q, wall)
+        functools.partial(gather_kernel, capacity),
+        grid=(groups,),
+        in_specs=[pl.BlockSpec((1, 16, tokens), lambda s: (s, 0, 0)),
+                  pl.BlockSpec((1, tokens, width), lambda s: (s, 0, 0))],
+        out_specs=pl.BlockSpec((num_local, capacity, width), lambda s: (0, s, 0)),
+        out_shape=jax.ShapeDtypeStruct((num_local, groups * capacity, width), BF16),
+        scratch_shapes=[pltpu.VMEM((num_local * capacity, tokens), BF16)],
+        cost_estimate=pl.CostEstimate(flops=2 * groups * num_local * capacity * tokens * width,
+                                      bytes_accessed=10 << 20, transcendentals=0),
+        name='gather_rows',
+    )(rg, x_all)
 
 
 def forward_kernel(capacity, rg_ref, x_ref, wall_ref, c_ref):
@@ -400,22 +510,18 @@
         hid = w_in.shape[3]
         capacity = 96
 
-        def gather_wgt(arr):
-            return lax.all_gather(arr, 'expert', axis_index_groups=wgt_groups, axis=0)
-
         def reduce_wgt(arr):
             return lax.psum_scatter(arr, 'expert', axis_index_groups=wgt_groups, scatter_dimension=0, tiled=False)
 
-        wall = jnp.concatenate([jnp.concatenate([w_in[0, 0], w_up[0, 0]], axis=1), w_out[0, 0]], axis=0)
-        wall = gather_wgt(wall)
         ids = jnp.swapaxes(expert_ids[:, 0], 1, 2)
         gates = jnp.swapaxes(gate_wts[:, 0], 1, 2)
-        xs, q, xs_f, rg, rg_f = dispatch_rows(x_acts[:, 0], ids, gates, d_out[0], capacity, num_stages)
-        dwall, dxs = expert_backward(xs, q, wall, hid)
-        xs_f, dxs = lax.optimization_barrier((xs_f, dxs))
+        dwall, dxs, xf_all, wall, rg, rg_f = dispatch_rows(
+            x_acts[:, 0], ids, gates, d_out[0], w_in[0, 0], w_up[0, 0], w_out[0, 0], capacity, num_stages)
         dwall = reduce_wgt(dwall)
         dx = combine_rows(rg, dxs, capacity, num_stages, 2)
+        xf_all, dx = lax.optimization_barrier((xf_all, dx))
         dx = lax.ppermute(dx, 'stage', to_prev)
+        xs_f = gather_rows(rg_f, xf_all, capacity)
         c = expert_forward(rg_f, xs_f, wall, hid, capacity)
         y = combine_rows(rg_f, c, capacity, num_stages, 3)
         dwall = dwall.astype(BF16)

time: 255 us -> 234 us (0.918)
  waiting for transfers between devices: 32.4 us -> 19.4 us
  Pallas kernels: 198 us -> 194 us
    pallas_call x1, Pallas kernels: 21.1 us -> 9.04 us  [gather_rows(): pl.pallas_call(functools.partial(gather_kernel, capacity), grid=(groups,)...]
    pallas_call x1, Pallas kernels: 73.4 us -> 82.2 us  [dispatch_rows(): pl.pallas_call(functools.partial(dispatch_kernel, num_stages, capacity),...]
    reduce_scatter x1, waiting for transfers between devices: 27.5 us -> 19.4 us  [reduce_wgt(): lax.psum_scatter(arr, 'expert', axis_index_groups=wgt_groups, scatter_dim...]
    all_gather x1 -> x0, waiting for transfers between devices: 4.93 us -> none  [gather_wgt(): return lax.all_gather(arr, 'expert', axis_index_groups=wgt_groups, axis=0)]
  transfers between devices with their start and end apart: 3 -> 2, of which waited for: 2 -> 1; matrix products, arithmetic and copies ran while one was open for 0% -> 0% of each run, Pallas kernels for 69% -> 48%
where the time goes in v3:
time: 234 us
  Pallas kernels  194 us (83%)
  waiting for transfers between devices  19.4 us (8%)
  between operations  14.1 us (6%)
  local copies, waits for them, and re-layouts  3.13 us (1%)
  other arithmetic  3.01 us (1%)
    pallas_call x2, Pallas kernels, combine_rows(): pl.pallas_call(functools.partial(combine_kernel, num_stages, capacity), i...  90.9 us
    pallas_call x1, Pallas kernels, dispatch_rows(): pl.pallas_call(functools.partial(dispatch_kernel, num_stages, capacity),...  82.2 us
    reduce_scatter x1, waiting for transfers between devices, reduce_wgt(): lax.psum_scatter(arr, 'expert', axis_index_groups=wgt_groups, scatter_dim...  19.4 us
    pallas_call x1, Pallas kernels, expert_forward(): pl.pallas_call(functools.partial(forward_kernel, capacity), grid=(num_loc...  11.6 us
    pallas_call x1, Pallas kernels, gather_rows(): pl.pallas_call(functools.partial(gather_kernel, capacity), grid=(groups,)...  9.04 us
  transfers between devices with their start and end apart: 2, of which 1 were waited for; matrix products, arithmetic and copies ran while one was open for 0% of the time, Pallas kernels for 48%

profile of v3, /device:TPU:1, one launch (start us, length us, event | category | flops | bytes accessed | tf_op | source)
XLA Modules:
  0.0 233.8 jit_solution(12395021611326262403)
XLA Ops:
  7.2 0.0 reduce-scatter.2.cloned.1.call-start
  7.2 82.2 %dispatch_rows.1 = (f32[8,768,512]{2,1,0:T(8,128)}, bf16[8,768,512]{2,1,0:T(8,128)(2,1)}, bf16[8,512,512]{2,1,0:T(8,128)(2,1)}, bf16[8,768,512]{2,1,0:T(8,128)(2...) custom-call(bf16[2,512,512]{2,1,0:T(8,128)(2,1)} %bitcast.23, s32[2,8,512]{2,1,0:T(8,128)} %bitcast.28, ...), custom_call_target="tpu_custom_call" | custom-call | flops 40000000000 | bytes 41943040 | tf_op jit(solution)/shard_map/dispatch_rows/pallas_call | solution.py:345
  89.5 0.0 reduce-scatter.2.cloned.1.call-update
  89.5 44.4 %combine_rows_2.1 = bf16[512,512]{1,0:T(8,128)(2,1)} custom-call(f32[8,16,512]{2,1,0:T(8,128)} %get-tuple-element.15.rg_ref, bf16[8,768,512]{2,1,0:T(8,128)(2,1)} %get-tuple-element.16.c_ref), custom_call_target="tpu_custom_call" | custom-call | flops 20000000000 | bytes 8388608 | tf_op jit(solution)/shard_map/combine_rows_2/pallas_call | solution.py:483
  133.9 0.3 collective-permute-start
  134.2 9.0 %gather_rows.1.x_ref = bf16[8,768,512]{2,1,0:T(8,128)(2,1)} custom-call(f32[8,16,512]{2,1,0:T(8,128)} %get-tuple-element.13.rg_ref, bf16[8,512,512]{2,1,0:T(8,128)(2,1)} %get-tuple-element.17.x_ref), custom_call_target="tpu_custom_call" | custom-call | flops 3221225472 | bytes 10485760 | tf_op jit(solution)/shard_map/gather_rows/pallas_call | solution.py:377
  143.2 11.6 %expert_forward.1.c_ref = bf16[8,768,512]{2,1,0:T(8,128)(2,1)} custom-call(f32[8,16,512]{2,1,0:T(8,128)} %get-tuple-element.13.rg_ref, bf16[8,768,512]{2,1,0:T(8,128)(2,1)} %gather_rows.1.x_ref, bf16[8,768,512]{2,1,0:T(8,128)(2,1)} %get-tuple-element.18.wall_ref), custom_call_target="tpu_custom_call" | custom-call | flops 4831838208 | bytes 20971520 | tf_op jit(solution)/shard_map/expert_forward/pallas_call | solution.py:409
  154.9 46.5 %combine_rows_3.1 = bf16[512,512]{1,0:T(8,128)(2,1)} custom-call(f32[8,16,512]{2,1,0:T(8,128)} %get-tuple-element.13.rg_ref, bf16[8,768,512]{2,1,0:T(8,128)(2,1)} %expert_forward.1.c_ref), custom_call_target="tpu_custom_call" | custom-call | flops 20000000000 | bytes 8388608 | tf_op jit(solution)/shard_map/combine_rows_3/pallas_call | solution.py:483
  201.4 0.0 copy-start
  201.4 0.0 collective-permute-done
  201.4 19.4 %reduce-scatter.2.cloned.1.call-done = f32[1,768,512]{2,1,0:T(8,128)} async-done(((f32[8,768,512]{2,1,0:T(8,128)}), f32[1,768,512]{2,1,0:T(8,128)}) %reduce-scatter.2.cloned.1.call-update) | async-done | bytes 1572880 | tf_op jit(solution)/shard_map/reduce_scatter | solution.py:514
  220.8 1.5 convert_element_type.6
  222.3 0.7 slice_bitcast_fusion
  223.0 1.5 convert_bitcast_fusion
  224.5 0.8 slice_bitcast_fusion.1
  225.4 0.0 copy-done
  225.4 0.8 copy.14
  226.2 0.8 copy.15
Async XLA Ops:
  7.2 213.6 %reduce-scatter.2.cloned.1.call-start = ((), (), s32[]{:S(2)}) async-start(), calls=%async_computation.1 | async-start | bytes 14155776 | tf_op jit(solution)/shard_map/reduce_scatter | solution.py:514
  133.9 67.4 %collective-permute-start = (bf16[512,512]{1,0:T(8,128)(2,1)}, bf16[512,512]{1,0:T(8,128)(2,1)S(1)}, u32[]{:S(2)}, u32[]{:S(2)}) collective-permute-start(bf16[512,512]{1,0:T(8,128)(2,1)} %combine_rows_2.1), channel_id=1, source_target_pairs={{64,0},{128,64},{192,128},{0,192},{65,1},{129,65},{193,129},{1,193... | collective-permute-start | bytes 1572872 | tf_op jit(solution)/shard_map/ppermute | solution.py:523
  201.4 24.0 %copy-start = (bf16[512,512]{1,0:T(8,128)(2,1)S(1)}, bf16[512,512]{1,0:T(8,128)(2,1)}, u32[]{:S(2)}) copy-start(bf16[512,512]{1,0:T(8,128)(2,1)} %combine_rows_3.1) | copy-start | bytes 1572868
Sparse Core Ops, SparseCore 0:
  89.6 131.1 reduce-scatter.1

commit v4 on v3

--- a/solution.py
+++ b/solution.py
@@ -365,168 +365,288 @@
     )(x_acts, ids, gates, dy, w_in, w_up, w_out)
 
 
-def gather_kernel(capacity, rg_ref, x_ref, xs_ref, hot_ref):
-    fill_onehot(hot_ref, rg_ref[0, 0:8], capacity)
-    rows = jnp.dot(hot_ref[...], x_ref[0], preferred_element_type=F32)
-    xs_ref[...] = rows.astype(BF16).reshape(xs_ref.shape)
-
-
-def gather_rows(rg, x_all, capacity):
-    groups, tokens, width = x_all.shape
-    num_local = 8
+class GradRing:
+    def __init__(self, p, part, inbox, send_sems, recv_sems):
+        self.part, self.inbox = part, inbox
+        self.rows = part.shape[1] // 4
+        self.copies, self.target = [], []
+        self.home = p.z_slot(0)
+        for way, device in ((0, p.z_up), (1, p.z_down)):
+            way_copies, way_target = [], []
+            for i in range(14):
+                step, pos = divmod(i + 2, 4)
+                piece = (pos + 2 - 2 * way) % 4
+                slot = p.z_slot(4 - step if way == 0 else step - 4)
+                src = part.at[slot, pl.ds(piece * self.rows, self.rows)]
+                dst = inbox.at[way, pl.ds(i * self.rows, self.rows)]
+                way_copies.append(send(src, dst, send_sems.at[way, i], recv_sems.at[way, i], device))
+                way_target.append((slot, piece))
+            self.copies.append(way_copies)
+            self.target.append(way_target)
+
+    def start(self, lo, hi):
+        for i in range(lo, hi):
+            for way in range(2):
+                self.copies[way][i].start()
+
+    def event(self, i):
+        for way in range(2):
+            self.copies[way][i].wait_recv()
+            if i + 4 < 14:
+                slot, piece = self.target[way][i + 4]
+            else:
+                slot, piece = self.home, (i - 10 + 2 - 2 * way) % 4
+            rows = pl.ds(piece * self.rows, self.rows)
+            self.part[slot, rows] = self.part[slot, rows] + self.inbox[way, pl.ds(i * self.rows, self.rows)]
+            if i + 4 < 14:
+                self.copies[way][i + 4].start()
+
+    def finish(self):
+        for way in range(2):
+            for copy in self.copies[way]:
+                copy.wait_send()
+
+
+class Combine:
+    def __init__(self, p, partial_sum, side_out, side_in, acc, half_in, up_in, down_in, send_sems, recv_sems):
+        half = acc.shape[1] // 2
+        self.low, self.high = pl.ds(0, half), pl.ds(half, half)
+        low, high = self.low, self.high
+        self.p, self.partial_sum = p, partial_sum
+        self.side_out, self.side_in, self.acc, self.half_in = side_out, side_in, acc, half_in
+        self.up_in, self.down_in = up_in, down_in
+
+        def copy(i, src, dst, device):
+            return send(src, dst, send_sems.at[i], recv_sems.at[i], device)
+
+        self.sides = [copy(d, side_out.at[d], side_in.at[d], p.partner) for d in range(4)]
+        self.far_up = copy(4, acc.at[2, low], half_in.at[0], p.up)
+        self.far_down = copy(5, acc.at[2, high], half_in.at[1], p.down)
+        self.up_a = copy(6, acc.at[1, high], up_in.at[high], p.up)
+        self.up_b = copy(7, acc.at[1, low], up_in.at[low], p.up)
+        self.down_a = copy(8, acc.at[3, low], down_in.at[low], p.down)
+        self.down_b = copy(9, acc.at[3, high], down_in.at[high], p.down)
+
+    def both(self, d):
+        self.side_out[d] = self.partial_sum(self.p.slot(d, True))
+        self.sides[d].start()
+        self.acc[d] = self.partial_sum(self.p.slot(d))
+
+    def add_side(self, d):
+        self.sides[d].wait_recv()
+        self.acc[d] = self.acc[d] + self.side_in[d]
+
+    def start_far(self):
+        self.far_up.start()
+        self.far_down.start()
+
+    def add_far(self):
+        low, high, acc = self.low, self.high, self.acc
+        self.far_up.wait_recv()
+        acc[1, low] = acc[1, low] + self.half_in[0]
+        self.up_b.start()
+        self.far_down.wait_recv()
+        acc[3, high] = acc[3, high] + self.half_in[1]
+        self.down_b.start()
+
+    def total(self):
+        for copy in (self.up_a, self.up_b, self.down_a, self.down_b):
+            copy.wait_recv()
+        return (self.acc[0] + self.up_in[...] + self.down_in[...]).astype(BF16)
+
+    def finish(self):
+        for copy in self.sides + [self.far_up, self.far_down, self.up_a, self.up_b, self.down_a, self.down_b]:
+            copy.wait_send()
+
+
+def finish_kernel(num_stages, capacity, dw_ref, dxs_ref, xf_ref, wall_ref, rgb_ref, rgf_ref, out_ref,
+                  part, inbox, slots, hot_ref, xf_buf, w_buf, side_out, side_in, acc, half_in, up_in, down_in,
+                  stage_dx, stage_y, stage_dw, z_send, z_recv, dx_send, dx_recv, y_send, y_recv, hop_send, hop_recv,
+                  load_sems, slot_sem, xf_sems, w_sems, out_sems, credit):
+    p = Peers(num_stages)
+    num_local = slots.shape[0]
+    tokens, width = stage_y.shape
+    order = (4, 3, -3, 2, -2, 1, -1, 0)
+    loads = []
+    for i, off in enumerate(order):
+        slot = p.z_slot(off)
+        loads.append(pltpu.make_async_copy(dw_ref.at[slot], part.at[slot], load_sems.at[i]))
+    load_slots = pltpu.make_async_copy(dxs_ref, slots, slot_sem)
+    for load in loads[:3]:
+        load.start()
+    load_slots.start()
+    for load in loads[3:]:
+        load.start()
+    greet((p.up, p.down, p.partner, p.after, p.before, p.z_up, p.z_down))
+    ring = GradRing(p, part, inbox, z_send, z_recv)
+    loads[0].wait()
+    ring.start(0, 2)
+    loads[1].wait()
+    loads[2].wait()
+    ring.start(2, 4)
+    load_slots.wait()
+
+    def rows_of(s):
+        return pl.ds(pl.multiple_of(s * capacity, 16), capacity)
+
+    def partial_sum(rg_ref):
+        def compute(s):
+            fill_onehot(hot_ref, rg_ref[s, 0:8], capacity)
+            rows = slots[:, rows_of(s)].reshape(hot_ref.shape[0], width)
+            return lax.dot_general(hot_ref[...], rows, (((0,), (0,)), ((), ())), preferred_element_type=F32)
+        return compute
+
+    shared = (side_out, side_in, acc, half_in, up_in, down_in)
+    dx_sum = Combine(p, partial_sum(rgb_ref), *shared, dx_send, dx_recv)
+    y_sum = Combine(p, partial_sum(rgf_ref), *shared, y_send, y_recv)
+
+    def load_xf(s):
+        slot = lax.rem(s, 2)
+        return pltpu.make_async_copy(xf_ref.at[s], xf_buf.at[slot], xf_sems.at[slot])
+
+    def load_w(e):
+        slot = lax.rem(e, 2)
+        return pltpu.make_async_copy(wall_ref.at[e], w_buf.at[slot], w_sems.at[slot])
+
+    def gather_step(s, carry):
+        @pl.when(s < TG - 1)
+        def _():
+            load_xf(s + 1).start()
+
+        load_xf(s).wait()
+        fill_onehot(hot_ref, rgf_ref[s, 0:8], capacity)
+        rows = jnp.dot(hot_ref[...], xf_buf[lax.rem(s, 2)], preferred_element_type=F32).astype(BF16)
+        for k in range(num_local):
+            slots[k, rows_of(s)] = rows[k * capacity:(k + 1) * capacity]
+        return carry
+
+    def forward_step(e, carry):
+        @pl.when(e < num_local - 1)
+        def _():
+            load_w(e + 1).start()
+
+        load_w(e).wait()
+        slot = lax.rem(e, 2)
+        wcat, wout = w_buf[slot, :width], w_buf[slot, width:]
+        hid = wout.shape[0]
+        pre = jnp.dot(slots[e], wcat, preferred_element_type=F32)
+        a, b = pre[:, :hid], pre[:, hid:]
+        h = (a * jax.nn.sigmoid(a) * b).astype(BF16)
+        o = jnp.dot(h, wout, preferred_element_type=F32)
+        for s in range(TG):
+            col = gate_column(rgf_ref[s, pl.ds(e, 1)], rgf_ref[s, pl.ds(8 + e, 1)], capacity)
+            slots[e, s * capacity:(s + 1) * capacity] = (col * o[s * capacity:(s + 1) * capacity]).astype(BF16)
+        return carry
+
+    load_xf(jnp.int32(0)).start()
+    load_w(jnp.int32(0)).start()
+    dx_sum.both(2)
+    dx_sum.add_side(2)
+    dx_sum.start_far()
+    dx_sum.both(1)
+    dx_sum.add_side(1)
+    dx_sum.up_a.start()
+    dx_sum.both(3)
+    dx_sum.add_side(3)
+    dx_sum.down_a.start()
+    dx_sum.both(0)
+    dx_sum.add_side(0)
+    pl.semaphore_signal(credit.at[2], inc=1, device_id=p.partner, device_id_type=MESH)
+    for load in loads[3:]:
+        load.wait()
+    ring.event(0)
+    lax.fori_loop(0, 3, gather_step, 0)
+    dx_sum.add_far()
+    ring.event(1)
+    lax.fori_loop(3, TG, gather_step, 0)
+    ring.event(2)
+    lax.fori_loop(0, 5, forward_step, 0)
+    ring.event(3)
+    lax.fori_loop(5, num_local, forward_step, 0)
+    stage_dx[...] = dx_sum.total()
+    hop = send(stage_dx, out_ref.at[pl.ds(tokens, tokens)], hop_send, hop_recv, p.before)
+    hop.start()
+    pl.semaphore_signal(credit.at[1], inc=1, device_id=p.up, device_id_type=MESH)
+    pl.semaphore_signal(credit.at[0], inc=1, device_id=p.down, device_id_type=MESH)
+    dx_sum.finish()
+    pl.semaphore_wait(credit.at[2], 1)
+    y_sum.both(2)
+    y_sum.add_side(2)
+    pl.semaphore_wait(credit.at[0], 1)
+    pl.semaphore_wait(credit.at[1], 1)
+    y_sum.start_far()
+    ring.event(4)
+    y_sum.both(1)
+    y_sum.add_side(1)
+    y_sum.up_a.start()
+    y_sum.both(3)
+    y_sum.add_side(3)
+    y_sum.down_a.start()
+    y_sum.both(0)
+    y_sum.add_side(0)
+    ring.event(5)
+    y_sum.add_far()
+    ring.event(6)
+    ring.event(7)
+    ring.event(8)
+    stage_y[...] = y_sum.total()
+    put_y = pltpu.make_async_copy(stage_y, out_ref.at[pl.ds(0, tokens)], out_sems.at[0])
+    put_y.start()
+    for i in range(9, 14):
+        ring.event(i)
+    stage_dw[...] = part[ring.home].astype(BF16)
+    put_dw = pltpu.make_async_copy(stage_dw, out_ref.at[pl.ds(2 * tokens, part.shape[1])], out_sems.at[1])
+    put_dw.start()
+    put_y.wait()
+    hop.wait()
+    y_sum.finish()
+    ring.finish()
+    put_dw.wait()
+
+
+def finish_rows(dw, dxs, xf_all, wall, rg_b, rg_f, capacity, num_stages):
+    num_local, _, width = dxs.shape
+    tokens = rg_b.shape[2]
+    any_spec, vmem_spec = pl.BlockSpec(memory_space=pl.ANY), pl.BlockSpec(memory_space=pltpu.VMEM)
+    dma, quad = pltpu.SemaphoreType.DMA, pltpu.VMEM((4, tokens, width), F32)
+    one = pltpu.VMEM((tokens, width), F32)
     return pl.pallas_call(
-        functools.partial(gather_kernel, capacity),
-        grid=(groups,),
-        in_specs=[pl.BlockSpec((1, 16, tokens), lambda s: (s, 0, 0)),
-                  pl.BlockSpec((1, tokens, width), lambda s: (s, 0, 0))],
-        out_specs=pl.BlockSpec((num_local, capacity, width), lambda s: (0, s, 0)),
-        out_shape=jax.ShapeDtypeStruct((num_local, groups * capacity, width), BF16),
-        scratch_shapes=[pltpu.VMEM((num_local * capacity, tokens), BF16)],
-        cost_estimate=pl.CostEstimate(flops=2 * groups * num_local * capacity * tokens * width,
-                                      bytes_accessed=10 << 20, transcendentals=0),
-        name='gather_rows',
-    )(rg, x_all)
-
-
-def forward_kernel(capacity, rg_ref, x_ref, wall_ref, c_ref):
-    e = pl.program_id(0)
-    x = x_ref[0]
-    width = x.shape[1]
-    wcat, wout = wall_ref[0, :width], wall_ref[0, width:]
-    hid = wout.shape[0]
-    pre = jnp.dot(x, wcat, preferred_element_type=F32)
-    a, b = pre[:, :hid], pre[:, hid:]
-    h = (a * jax.nn.sigmoid(a) * b).astype(BF16)
-    o = jnp.dot(h, wout, preferred_element_type=F32)
-    for s in range(rg_ref.shape[0]):
-        col = gate_column(rg_ref[s, pl.ds(e, 1)], rg_ref[s, pl.ds(8 + e, 1)], capacity)
-        c_ref[0, s * capacity:(s + 1) * capacity] = (col * o[s * capacity:(s + 1) * capacity]).astype(BF16)
-
-
-def expert_forward(rg, xs, wall, hid, capacity):
-    num_local, rows, width = xs.shape
-    row_block = pl.BlockSpec((1, rows, width), lambda e: (e, 0, 0))
-    return pl.pallas_call(
-        functools.partial(forward_kernel, capacity),
-        grid=(num_local,),
-        in_specs=[pl.BlockSpec(rg.shape, lambda e: (0, 0, 0)), row_block,
-                  pl.BlockSpec((1,) + wall.shape[1:], lambda e: (e, 0, 0))],
-        out_specs=row_block,
-        out_shape=jax.ShapeDtypeStruct(xs.shape, BF16),
-        cost_estimate=pl.CostEstimate(flops=6 * num_local * rows * width * hid, bytes_accessed=20 << 20,
-                                      transcendentals=num_local * rows * hid),
-        name='expert_forward',
-    )(rg, xs, wall)
-
-
-def combine_kernel(num_stages, capacity, rg_ref, c_ref, out_ref, hot_ref, side_out, side_in, acc, half_in,
-                   up_in, down_in, send_sems, recv_sems):
-    p = Peers(num_stages)
-    half = acc.shape[1] // 2
-    low, high = pl.ds(0, half), pl.ds(half, half)
-    greet((p.up, p.down, p.partner))
-
-    def partial_sum(slot):
-        fill_onehot(hot_ref, rg_ref[slot, 0:8], capacity)
-        start = pl.ds(pl.multiple_of(slot * capacity, 16), capacity)
-        rows = c_ref[:, start].reshape(hot_ref.shape[0], c_ref.shape[2])
-        return lax.dot_general(hot_ref[...], rows, (((0,), (0,)), ((), ())), preferred_element_type=F32)
-
-    sides = [send(side_out.at[d], side_in.at[d], send_sems.at[d], recv_sems.at[d], p.partner) for d in range(4)]
-    far_up = send(acc.at[2, low], half_in.at[0], send_sems.at[4], recv_sems.at[4], p.up)
-    far_down = send(acc.at[2, high], half_in.at[1], send_sems.at[5], recv_sems.at[5], p.down)
-    up_a = send(acc.at[1, high], up_in.at[high], send_sems.at[6], recv_sems.at[6], p.up)
-    up_b = send(acc.at[1, low], up_in.at[low], send_sems.at[7], recv_sems.at[7], p.up)
-    down_a = send(acc.at[3, low], down_in.at[low], send_sems.at[8], recv_sems.at[8], p.down)
-    down_b = send(acc.at[3, high], down_in.at[high], send_sems.at[9], recv_sems.at[9], p.down)
-
-    def both(d):
-        side_out[d] = partial_sum(p.slot(d, True))
-        sides[d].start()
-        acc[d] = partial_sum(p.slot(d))
-
-    def add_side(d):
-        sides[d].wait_recv()
-        acc[d] = acc[d] + side_in[d]
-
-    both(2)
-    add_side(2)
-    far_up.start()
-    far_down.start()
-    both(1)
-    add_side(1)
-    up_a.start()
-    both(3)
-    add_side(3)
-    down_a.start()
-    both(0)
-    add_side(0)
-    far_up.wait_recv()
-    acc[1, low] = acc[1, low] + half_in[0]
-    up_b.start()
-    far_down.wait_recv()
-    acc[3, high] = acc[3, high] + half_in[1]
-    down_b.start()
-    up_a.wait_recv()
-    up_b.wait_recv()
-    down_a.wait_recv()
-    down_b.wait_recv()
-    out_ref[...] = (acc[0] + up_in[...] + down_in[...]).astype(BF16)
-    for copy in sides + [far_up, far_down, up_a, up_b, down_a, down_b]:
-        copy.wait_send()
-
-
-def combine_rows(rg, slots, capacity, num_stages, collective_id):
-    num_local, _, width = slots.shape
-    tokens = rg.shape[2]
-    vmem_spec = pl.BlockSpec(memory_space=pltpu.VMEM)
-    return pl.pallas_call(
-        functools.partial(combine_kernel, num_stages, capacity),
-        in_specs=[vmem_spec, vmem_spec],
-        out_specs=vmem_spec,
-        out_shape=jax.ShapeDtypeStruct((tokens, width), BF16),
+        functools.partial(finish_kernel, num_stages, capacity),
+        in_specs=[any_spec] * 4 + [vmem_spec] * 2,
+        out_specs=any_spec,
+        out_shape=jax.ShapeDtypeStruct((2 * tokens + dw.shape[1], width), BF16),
         scratch_shapes=[
-            pltpu.VMEM((num_local * capacity, tokens), BF16),
-            pltpu.VMEM((4, tokens, width), F32), pltpu.VMEM((4, tokens, width), F32),
-            pltpu.VMEM((4, tokens, width), F32), pltpu.VMEM((2, tokens // 2, width), F32),
-            pltpu.VMEM((tokens, width), F32), pltpu.VMEM((tokens, width), F32),
-            pltpu.SemaphoreType.DMA((10,)), pltpu.SemaphoreType.DMA((10,))],
-        compiler_params=pltpu.CompilerParams(collective_id=collective_id, has_side_effects=True,
-                                             vmem_limit_bytes=56 << 20),
-        cost_estimate=pl.CostEstimate(flops=20 * 10 ** 9, bytes_accessed=8 << 20, transcendentals=0),
-        name='combine_rows_%d' % collective_id,
-    )(rg, slots)
+            pltpu.VMEM(dw.shape, F32), pltpu.VMEM((2, 14 * (dw.shape[1] // 4), width), F32),
+            pltpu.VMEM(dxs.shape, BF16), pltpu.VMEM((num_local * capacity, tokens), BF16),
+            pltpu.VMEM((2, tokens, width), BF16), pltpu.VMEM((2,) + wall.shape[1:], BF16),
+            quad, quad, quad, pltpu.VMEM((2, tokens // 2, width), F32), one, one,
+            pltpu.VMEM((tokens, width), BF16), pltpu.VMEM((tokens, width), BF16),
+            pltpu.VMEM(dw.shape[1:], BF16),
+            dma((2, 14)), dma((2, 14)), dma((10,)), dma((10,)), dma((10,)), dma((10,)), dma, dma,
+            dma((8,)), dma, dma((2,)), dma((2,)), dma((2,)), pltpu.SemaphoreType.REGULAR((3,))],
+        compiler_params=pltpu.CompilerParams(collective_id=2, has_side_effects=True,
+                                             vmem_limit_bytes=63 << 20),
+        cost_estimate=pl.CostEstimate(flops=60 * 10 ** 9, bytes_accessed=40 << 20, transcendentals=0),
+        name='finish_rows',
+    )(dw, dxs, xf_all, wall, rg_b, rg_f)
 
 
 def solution(mesh):
-    group_size = mesh.shape['expert']
     num_stages = mesh.shape['stage']
-    to_prev = [((i + 1) % num_stages, i) for i in range(num_stages)]
-    rows_of = group_size // TG
-    wgt_groups = [[z * TG + r for z in range(rows_of)] for r in range(TG)]
 
     def device_fn(x_acts, expert_ids, gate_wts, w_in, w_up, w_out, d_out):
         tokens, width = x_acts.shape[2], x_acts.shape[3]
         hid = w_in.shape[3]
         capacity = 96
 
-        def reduce_wgt(arr):
-            return lax.psum_scatter(arr, 'expert', axis_index_groups=wgt_groups, scatter_dimension=0, tiled=False)
-
         ids = jnp.swapaxes(expert_ids[:, 0], 1, 2)
         gates = jnp.swapaxes(gate_wts[:, 0], 1, 2)
         dwall, dxs, xf_all, wall, rg, rg_f = dispatch_rows(
             x_acts[:, 0], ids, gates, d_out[0], w_in[0, 0], w_up[0, 0], w_out[0, 0], capacity, num_stages)
-        dwall = reduce_wgt(dwall)
-        dx = combine_rows(rg, dxs, capacity, num_stages, 2)
-        xf_all, dx = lax.optimization_barrier((xf_all, dx))
-        dx = lax.ppermute(dx, 'stage', to_prev)
-        xs_f = gather_rows(rg_f, xf_all, capacity)
-        c = expert_forward(rg_f, xs_f, wall, hid, capacity)
-        y = combine_rows(rg_f, c, capacity, num_stages, 3)
-        dwall = dwall.astype(BF16)
-        return (y[None], dx[None], dwall[None, None, :width, :hid], dwall[None, None, :width, hid:],
-                dwall[None, None, width:])
+        out = finish_rows(dwall, dxs, xf_all, wall, rg, rg_f, capacity, num_stages)
+        y, dx, dw = out[:tokens], out[tokens:2 * tokens], out[2 * tokens:]
+        return (y[None], dx[None], dw[None, None, :width, :hid], dw[None, None, :width, hid:],
+                dw[None, None, width:])
 
     tok_spec = P(None, 'stage', 'expert', None)
     w_spec = P('stage', 'expert', None, None)

time: 234 us -> 215 us (0.919)
  waiting for transfers between devices: 19.4 us -> 0 us
  Pallas kernels: 194 us -> 208 us
  between operations: 14.1 us -> 0.65 us
  other arithmetic: 3.01 us -> 0 us
  local copies, waits for them, and re-layouts: 3.13 us -> 5.75 us
    reduce_scatter x1 -> x0, waiting for transfers between devices: 19.4 us -> none  [reduce_wgt(): lax.psum_scatter(arr, 'expert', axis_index_groups=wgt_groups, scatter_dim...]
    pallas_call x4 -> x1, Pallas kernels: 112 us -> 126 us  [finish_rows(): pl.pallas_call(functools.partial(finish_kernel, num_stages, capacity), in...]
    broadcast_in_dim x2 -> x3, local copies, waits for them, and re-layouts: 1.54 us -> 5.75 us  [the longest x1 2.23 us: device_fn(): dx[None]]
    convert_element_type x2 -> x0, other arithmetic: 3.01 us -> none  [device_fn(): dwall = dwall.astype(BF16)]
  transfers between devices with their start and end apart: 2 -> 0, of which waited for: 1 -> 0; matrix products, arithmetic and copies ran while one was open for 0% -> 0% of each run, Pallas kernels for 48% -> 0%
where the time goes in v4:
time: 215 us
  Pallas kernels  208 us (97%)
  local copies, waits for them, and re-layouts  5.75 us (3%)
    pallas_call x1, Pallas kernels, finish_rows(): pl.pallas_call(functools.partial(finish_kernel, num_stages, capacity), in...  126 us
    pallas_call x1, Pallas kernels, dispatch_rows(): pl.pallas_call(functools.partial(dispatch_kernel, num_stages, capacity),...  82.3 us

profile of v4, /device:TPU:1, one launch (start us, length us, event | category | flops | bytes accessed | tf_op | source)
XLA Modules:
  0.0 214.9 jit_solution(4356523406805793847)
XLA Ops:
  0.6 82.3 %dispatch_rows.1 = (f32[8,768,512]{2,1,0:T(8,128)}, bf16[8,768,512]{2,1,0:T(8,128)(2,1)}, bf16[8,512,512]{2,1,0:T(8,128)(2,1)}, bf16[8,768,512]{2,1,0:T(8,128)(2...) custom-call(bf16[2,512,512]{2,1,0:T(8,128)(2,1)} %bitcast.21, s32[2,8,512]{2,1,0:T(8,128)} %bitcast.26, ...), custom_call_target="tpu_custom_call" | custom-call | flops 40000000000 | bytes 41943040 | tf_op jit(solution)/shard_map/dispatch_rows/pallas_call | solution.py:345
  82.9 126.2 %finish_rows.1 = bf16[1792,512]{1,0:T(8,128)(2,1)} custom-call(f32[8,768,512]{2,1,0:T(8,128)} %get-tuple-element.11.dw_ref, bf16[8,768,512]{2,1,0:T(8,128)(2,1)} %get-tuple-element.12.dxs_ref, bf16[8,512,512]{2,1,0:T(8,128)(2,1)} %get-tuple-element.13.xf_ref, bf16[8,768,512]{2,1,0:T(8,128)(2,1)} %get-tuple-element.14.wall_ref, ...), custom_call_target="tpu_custom_call" | custom-call | flops 60000002048 | bytes 41943040 | tf_op jit(solution)/shard_map/finish_rows/pallas_call | solution.py:613
  209.1 1.7 slice_bitcast_fusion.2
  210.8 1.9 slice_bitcast_fusion.3
  212.7 2.2 %slice_bitcast_fusion = (bf16[1,512,512]{2,1,0:T(8,128)(2,1)}, bf16[1,512,512]{2,1,0:T(8,128)(2,1)}) fusion(bf16[1792,512]{1,0:T(8,128)(2,1)} %finish_rows.1), kind=kLoop, calls=%fused_computation | loop fusion | bytes 2097152 | tf_op jit(solution)/shard_map/broadcast_in_dim | solution.py:648

commit v5 on v4

--- a/solution.py
+++ b/solution.py
@@ -11,6 +11,7 @@
 F32 = jnp.float32
 BF16 = jnp.bfloat16
 MESH = pl.DeviceIdType.MESH
+EARLY = 5
 
 
 def routing_rows(gates, ids, group_rank, num_local):
@@ -67,6 +68,14 @@
     def z_slot(self, offset):
         return lax.rem(self.zpos + offset + self.z_size, self.z_size)
 
+    def expert(self, i):
+        return self.z_slot((1 - 2 * lax.rem(i, 2)) * ((i + 1) // 2))
+
+    def arrival(self, j):
+        h = j // 2
+        offset = h + h // 2 - 2 * (h // 3)
+        return lax.rem(self.ypos + offset, 4) * 2 + lax.rem(self.core + lax.rem(j, 2), 2)
+
     def slot(self, offset, other_core=False):
         core = 1 - self.core if other_core else self.core
         return lax.rem(self.ypos + offset, 4) * 2 + core
@@ -115,12 +124,15 @@
         self.fwd_down.start()
         self.up_side.start()
 
+    def near(self):
+        for copy in (self.own_side, self.down_side, self.up_side):
+            copy.wait_recv()
+
     def last(self):
         self.fwd_up.wait_recv()
         self.fwd_down.wait_recv()
         self.far_side.start()
-        for copy in (self.own_side, self.down_side, self.up_side, self.far_side):
-            copy.wait_recv()
+        self.far_side.wait_recv()
 
     def finish(self):
         for copy in (self.own_up, self.own_down, self.fwd_up, self.fwd_down,
@@ -177,9 +189,10 @@
 
 
 def dispatch_kernel(num_stages, capacity, x_ref, ids_ref, gate_ref, dy_ref, wi_ref, wu_ref, wo_ref,
-                    dw_ref, dxs_ref, xf_ref, wall_ref, rgb_ref, rgf_ref,
+                    dw_ref, dxs_ref, xs_ref, xf_ref, wall_ref, rgb_ref, rgf_ref,
                     dy_buf, xb_buf, xf_buf, ids_buf, gate_buf, hot_ref, xs_buf, q_buf, wall_buf, dw_buf, dab_ref,
-                    send_sems, recv_sems, hop_send, hop_recv, z_send, z_recv, local_sems, dw_sems, dx_sems):
+                    send_sems, recv_sems, hop_send, hop_recv, z_send, z_recv, local_sems, dw_sems, dx_sems,
+                    xs_sems, wall_sems):
     p = Peers(num_stages)
     num_local = xs_buf.shape[0]
     width, hid = wi_ref.shape
@@ -208,6 +221,12 @@
     for copy in keep:
         copy.wait()
     ring.start()
+
+    def put_wall(i):
+        e = p.expert(jnp.int32(i))
+        return pltpu.make_async_copy(wall_buf.at[e], wall_ref.at[e], wall_sems.at[i])
+
+    put_wall(0).start()
     hops[3].start()
     hops[0].wait_recv()
     s_ids.start()
@@ -221,6 +240,8 @@
     hops[2].wait_recv()
     s_xb.start()
     ring.event(2)
+    s_ids.near()
+    s_gate.near()
     s_ids.last()
     s_gate.last()
 
@@ -242,7 +263,8 @@
             q_buf[k, rows_of(s)] = (col * rows[k * capacity:(k + 1) * capacity]).astype(BF16)
         return carry
 
-    def x_step(s, carry):
+    def x_step(j, carry):
+        s = p.arrival(j)
         rows = jnp.dot(hot_ref[s], xb_buf[s], preferred_element_type=F32).astype(BF16)
         for k in range(num_local):
             xs_buf[k, rows_of(s)] = rows[k * capacity:(k + 1) * capacity]
@@ -251,27 +273,30 @@
     half = TG // 2
     lax.fori_loop(0, half, route_step, 0)
     ring.event(3)
+    put_wall(1).start()
+    put_wall(2).start()
     lax.fori_loop(half, TG, route_step, 0)
+    s_dy.near()
     s_dy.last()
     keep_dy.wait()
     ring.event(4)
     lax.fori_loop(0, half, dy_step, 0)
     ring.event(5)
-    lax.fori_loop(half, TG, dy_step, 0)
-    ring.event(6)
     s_xb.forward()
     hops[3].wait_recv()
     s_xf.start()
+    ring.event(6)
+    lax.fori_loop(half, TG, dy_step, 0)
     ring.event(7)
+    put_wall(3).start()
+    put_wall(4).start()
+    s_xb.near()
+    lax.fori_loop(0, 6, x_step, 0)
+    ring.event(8)
     s_xb.last()
-    ring.event(8)
-    lax.fori_loop(0, half, x_step, 0)
+    lax.fori_loop(6, TG, x_step, 0)
     ring.event(9)
-    lax.fori_loop(half, TG, x_step, 0)
-    ring.event(10)
-
-    def expert_of(i):
-        return p.z_slot((1 - 2 * lax.rem(i, 2)) * ((i + 1) // 2))
+    expert_of = p.expert
 
     def put_dw(i):
         slot = lax.rem(i, 2)
@@ -281,31 +306,29 @@
         e = expert_of(i)
         return pltpu.make_async_copy(q_buf.at[e], dxs_ref.at[e], dx_sems.at[i])
 
+    def put_xs(i):
+        return pltpu.make_async_copy(xs_buf.at[expert_of(jnp.int32(i))], xs_ref.at[7 - i], xs_sems.at[7 - i])
+
     put_xf = pltpu.make_async_copy(xf_buf, xf_ref, local_sems.at[0])
-    put_wall = pltpu.make_async_copy(wall_buf, wall_ref, local_sems.at[1])
+    for i in range(EARLY, num_local):
+        put_xs(i).start()
+        put_dx(jnp.int32(i)).start()
 
     def backward_step(i, carry):
+        @pl.when(i == 1)
+        def _():
+            ring.event(10)
+
         @pl.when(i == 2)
         def _():
+            s_xf.forward()
             ring.event(11)
-
-        @pl.when(i == 3)
-        def _():
-            s_xf.forward()
+            put_wall(5).start()
+            put_wall(6).start()
 
         @pl.when(i == 4)
         def _():
             ring.event(12)
-
-        @pl.when(i == 6)
-        def _():
-            s_xf.last()
-            put_xf.start()
-
-        @pl.when(i == 7)
-        def _():
-            ring.event(13)
-            put_wall.start()
 
         @pl.when(i >= 2)
         def _():
@@ -318,18 +341,26 @@
         put_dx(i).start()
         return carry
 
-    lax.fori_loop(0, num_local, backward_step, 0)
-    put_xf.wait()
-    put_wall.wait()
+    lax.fori_loop(0, EARLY, backward_step, 0)
+    s_xf.near()
+    s_xf.last()
+    put_xf.start()
+    ring.event(13)
+    put_wall(7).start()
+    for i in range(EARLY, num_local):
+        put_xs(i).wait()
     for i in range(num_local):
         put_dx(jnp.int32(i)).wait()
-    put_dw(jnp.int32(num_local - 2)).wait()
-    put_dw(jnp.int32(num_local - 1)).wait()
+    put_dw(jnp.int32(EARLY - 2)).wait()
+    put_dw(jnp.int32(EARLY - 1)).wait()
     for s in spread:
         s.finish()
     for hop in hops:
         hop.wait_send()
     ring.finish()
+    put_xf.wait()
+    for i in range(num_local):
+        put_wall(i).wait()
 
 
 def dispatch_rows(x_acts, ids, gates, dy, w_in, w_up, w_out, capacity, num_stages):
@@ -345,8 +376,9 @@
     return pl.pallas_call(
         functools.partial(dispatch_kernel, num_stages, capacity),
         in_specs=[any_spec] * 7,
-        out_specs=[any_spec] * 4 + [vmem_spec] * 2,
+        out_specs=[any_spec] * 5 + [vmem_spec] * 2,
         out_shape=[jax.ShapeDtypeStruct(wall_size, F32), slot_shape,
+                   jax.ShapeDtypeStruct((num_local - EARLY,) + slot_shape.shape[1:], BF16),
                    jax.ShapeDtypeStruct((TG, tokens, width), BF16), jax.ShapeDtypeStruct(wall_size, BF16),
                    rg_shape, rg_shape],
         scratch_shapes=[
@@ -357,7 +389,8 @@
             pltpu.SemaphoreType.DMA((5, 8)), pltpu.SemaphoreType.DMA((5, 8)),
             pltpu.SemaphoreType.DMA((4,)), pltpu.SemaphoreType.DMA((4,)),
             pltpu.SemaphoreType.DMA((2, 14)), pltpu.SemaphoreType.DMA((2, 14)),
-            pltpu.SemaphoreType.DMA((4,)), pltpu.SemaphoreType.DMA((2,)), pltpu.SemaphoreType.DMA((num_local,))],
+            pltpu.SemaphoreType.DMA((4,)), pltpu.SemaphoreType.DMA((2,)), pltpu.SemaphoreType.DMA((num_local,)),
+            pltpu.SemaphoreType.DMA((num_local - EARLY,)), pltpu.SemaphoreType.DMA((num_local,))],
         compiler_params=pltpu.CompilerParams(collective_id=1, has_side_effects=True,
                                              vmem_limit_bytes=63 << 20),
         cost_estimate=pl.CostEstimate(flops=40 * 10 ** 9, bytes_accessed=40 << 20, transcendentals=0),
@@ -459,32 +492,61 @@
             copy.wait_send()
 
 
-def finish_kernel(num_stages, capacity, dw_ref, dxs_ref, xf_ref, wall_ref, rgb_ref, rgf_ref, out_ref,
-                  part, inbox, slots, hot_ref, xf_buf, w_buf, side_out, side_in, acc, half_in, up_in, down_in,
+def finish_kernel(num_stages, capacity, dw_ref, dxs_ref, xs_ref, xf_ref, wall_ref, rgb_ref, rgf_ref, out_ref,
+                  x_buf, dab_ref, part, inbox, slots, hot_ref, xf_buf, w_buf, side_out, side_in, acc, half_in, up_in, down_in,
                   stage_dx, stage_y, stage_dw, z_send, z_recv, dx_send, dx_recv, y_send, y_recv, hop_send, hop_recv,
-                  load_sems, slot_sem, xf_sems, w_sems, out_sems, credit):
+                  load_sems, slot_sems, x_sems, xf_sems, w_sems, out_sems, credit):
     p = Peers(num_stages)
     num_local = slots.shape[0]
     tokens, width = stage_y.shape
-    order = (4, 3, -3, 2, -2, 1, -1, 0)
-    loads = []
-    for i, off in enumerate(order):
-        slot = p.z_slot(off)
-        loads.append(pltpu.make_async_copy(dw_ref.at[slot], part.at[slot], load_sems.at[i]))
-    load_slots = pltpu.make_async_copy(dxs_ref, slots, slot_sem)
-    for load in loads[:3]:
-        load.start()
-    load_slots.start()
-    for load in loads[3:]:
-        load.start()
+    late = num_local - EARLY
+
+    def load_late(i):
+        slot, e = lax.rem(i, 2), p.expert(7 - i)
+        return (pltpu.make_async_copy(wall_ref.at[e], w_buf.at[slot], w_sems.at[slot]),
+                pltpu.make_async_copy(xs_ref.at[i], x_buf.at[slot], x_sems.at[slot]))
+
+    def load_slot(i):
+        e = p.expert(7 - i)
+        return pltpu.make_async_copy(dxs_ref.at[e], slots.at[e], slot_sems.at[i])
+
+    def load_dw(i):
+        e = p.expert(jnp.int32(i))
+        return pltpu.make_async_copy(dw_ref.at[e], part.at[e], load_sems.at[i])
+
+    for i in range(2):
+        load_slot(jnp.int32(i)).start()
+        for load in load_late(jnp.int32(i)):
+            load.start()
+    for i in range(2, num_local):
+        load_slot(jnp.int32(i)).start()
+    for i in range(EARLY):
+        load_dw(EARLY - 1 - i).start()
     greet((p.up, p.down, p.partner, p.after, p.before, p.z_up, p.z_down))
     ring = GradRing(p, part, inbox, z_send, z_recv)
-    loads[0].wait()
-    ring.start(0, 2)
-    loads[1].wait()
-    loads[2].wait()
+
+    def late_step(i, carry):
+        for load in load_late(i):
+            load.wait()
+        load_slot(i).wait()
+        slot, e = lax.rem(i, 2), p.expert(7 - i)
+        expert_step(x_buf[slot], slots[e], w_buf[slot, :width], w_buf[slot, width:], part.at[e], slots.at[e], dab_ref)
+
+        @pl.when(i == 0)
+        def _():
+            ring.start(0, 2)
+
+        @pl.when(i + 2 < late)
+        def _():
+            for load in load_late(i + 2):
+                load.start()
+
+        return carry
+
+    lax.fori_loop(0, late, late_step, 0)
     ring.start(2, 4)
-    load_slots.wait()
+    for i in range(late, num_local):
+        load_slot(jnp.int32(i)).wait()
 
     def rows_of(s):
         return pl.ds(pl.multiple_of(s * capacity, 16), capacity)
@@ -552,8 +614,8 @@
     dx_sum.both(0)
     dx_sum.add_side(0)
     pl.semaphore_signal(credit.at[2], inc=1, device_id=p.partner, device_id_type=MESH)
-    for load in loads[3:]:
-        load.wait()
+    for i in range(EARLY):
+        load_dw(i).wait()
     ring.event(0)
     lax.fori_loop(0, 3, gather_step, 0)
     dx_sum.add_far()
@@ -604,7 +666,7 @@
     put_dw.wait()
 
 
-def finish_rows(dw, dxs, xf_all, wall, rg_b, rg_f, capacity, num_stages):
+def finish_rows(dw, dxs, xs_late, xf_all, wall, rg_b, rg_f, capacity, num_stages):
     num_local, _, width = dxs.shape
     tokens = rg_b.shape[2]
     any_spec, vmem_spec = pl.BlockSpec(memory_space=pl.ANY), pl.BlockSpec(memory_space=pltpu.VMEM)
@@ -612,10 +674,11 @@
     one = pltpu.VMEM((tokens, width), F32)
     return pl.pallas_call(
         functools.partial(finish_kernel, num_stages, capacity),
-        in_specs=[any_spec] * 4 + [vmem_spec] * 2,
+        in_specs=[any_spec] * 5 + [vmem_spec] * 2,
         out_specs=any_spec,
         out_shape=jax.ShapeDtypeStruct((2 * tokens + dw.shape[1], width), BF16),
         scratch_shapes=[
+            pltpu.VMEM((2,) + dxs.shape[1:], BF16), pltpu.VMEM((dxs.shape[1], width), BF16),
             pltpu.VMEM(dw.shape, F32), pltpu.VMEM((2, 14 * (dw.shape[1] // 4), width), F32),
             pltpu.VMEM(dxs.shape, BF16), pltpu.VMEM((num_local * capacity, tokens), BF16),
             pltpu.VMEM((2, tokens, width), BF16), pltpu.VMEM((2,) + wall.shape[1:], BF16),
@@ -623,12 +686,47 @@
             pltpu.VMEM((tokens, width), BF16), pltpu.VMEM((tokens, width), BF16),
             pltpu.VMEM(dw.shape[1:], BF16),
             dma((2, 14)), dma((2, 14)), dma((10,)), dma((10,)), dma((10,)), dma((10,)), dma, dma,
-            dma((8,)), dma, dma((2,)), dma((2,)), dma((2,)), pltpu.SemaphoreType.REGULAR((3,))],
+            dma((EARLY,)), dma((num_local,)), dma((2,)), dma((2,)), dma((2,)), dma((2,)),
+            pltpu.SemaphoreType.REGULAR((3,))],
         compiler_params=pltpu.CompilerParams(collective_id=2, has_side_effects=True,
                                              vmem_limit_bytes=63 << 20),
         cost_estimate=pl.CostEstimate(flops=60 * 10 ** 9, bytes_accessed=40 << 20, transcendentals=0),
         name='finish_rows',
-    )(dw, dxs, xf_all, wall, rg_b, rg_f)
+    )(dw, dxs, xs_late, xf_all, wall, rg_b, rg_f)
+
+
+def split_kernel(out_ref, y_ref, dx_ref, wi_ref, wu_ref, wo_ref, buf, in_sems, out_sems):
+    tokens, (width, hid) = y_ref.shape[0], wi_ref.shape
+    first = 2 * tokens
+    spans = ((0, tokens), (tokens, tokens), (first, width), (first + width, hid))
+    loads = [pltpu.make_async_copy(out_ref.at[pl.ds(lo, size)], buf.at[pl.ds(lo, size)], in_sems.at[i])
+             for i, (lo, size) in enumerate(spans)]
+    for load in loads:
+        load.start()
+    stores = []
+    targets = (((0, tokens), (0, width), y_ref), ((tokens, tokens), (0, width), dx_ref),
+               ((first, width), (0, hid), wi_ref), ((first, width), (hid, hid), wu_ref),
+               ((first + width, hid), (0, width), wo_ref))
+    for i, (rows, cols, ref) in enumerate(targets):
+        if i != 3:
+            loads[min(i, 2) if i < 3 else 3].wait()
+        stores.append(pltpu.make_async_copy(buf.at[pl.ds(*rows), pl.ds(*cols)], ref, out_sems.at[i]))
+        stores[-1].start()
+    for store in stores:
+        store.wait()
+
+
+def split_rows(out, tokens, width, hid):
+    any_spec = pl.BlockSpec(memory_space=pl.ANY)
+    shapes = ((tokens, width), (tokens, width), (width, hid), (width, hid), (hid, width))
+    return pl.pallas_call(
+        split_kernel,
+        in_specs=[any_spec],
+        out_specs=[any_spec] * 5,
+        out_shape=[jax.ShapeDtypeStruct(shape, BF16) for shape in shapes],
+        scratch_shapes=[pltpu.VMEM(out.shape, BF16), pltpu.SemaphoreType.DMA((4,)), pltpu.SemaphoreType.DMA((5,))],
+        name='split_rows',
+    )(out)
 
 
 def solution(mesh):
@@ -641,12 +739,11 @@
 
         ids = jnp.swapaxes(expert_ids[:, 0], 1, 2)
         gates = jnp.swapaxes(gate_wts[:, 0], 1, 2)
-        dwall, dxs, xf_all, wall, rg, rg_f = dispatch_rows(
+        dwall, dxs, xs_late, xf_all, wall, rg, rg_f = dispatch_rows(
             x_acts[:, 0], ids, gates, d_out[0], w_in[0, 0], w_up[0, 0], w_out[0, 0], capacity, num_stages)
-        out = finish_rows(dwall, dxs, xf_all, wall, rg, rg_f, capacity, num_stages)
-        y, dx, dw = out[:tokens], out[tokens:2 * tokens], out[2 * tokens:]
-        return (y[None], dx[None], dw[None, None, :width, :hid], dw[None, None, :width, hid:],
-                dw[None, None, width:])
+        out = finish_rows(dwall, dxs, xs_late, xf_all, wall, rg, rg_f, capacity, num_stages)
+        y, dx, dw_in, dw_up, dw_out = split_rows(out, tokens, width, hid)
+        return y[None], dx[None], dw_in[None, None], dw_up[None, None], dw_out[None, None]
 
     tok_spec = P(None, 'stage', 'expert', None)
     w_spec = P('stage', 'expert', None, None)

time: 215 us -> 208 us (0.967)
  local copies, waits for them, and re-layouts: 5.75 us -> 0 us
    pallas_call x1, Pallas kernels: 82.3 us -> 75.6 us  [dispatch_rows(): pl.pallas_call(functools.partial(dispatch_kernel, num_stages, capacity),...]
    broadcast_in_dim x3 -> x0, local copies, waits for them, and re-layouts: 5.75 us -> none  [the longest x1 2.23 us: device_fn(): dx[None]]
    pallas_call x1, Pallas kernels: 126 us -> 129 us  [finish_rows(): pl.pallas_call(functools.partial(finish_kernel, num_stages, capacity), in...]
    pallas_call x0 -> x1, Pallas kernels: none -> 2.34 us  [split_rows(): pl.pallas_call(split_kernel, in_specs=[any_spec], out_specs=[any_spec] *...]
where the time goes in v5:
time: 208 us; the launch traced here: 207 us
  Pallas kernels  206 us (99%)
    pallas_call x1, Pallas kernels, finish_rows(): pl.pallas_call(functools.partial(finish_kernel, num_stages, capacity), in...  129 us
    pallas_call x1, Pallas kernels, dispatch_rows(): pl.pallas_call(functools.partial(dispatch_kernel, num_stages, capacity),...  75.6 us

profile of v5, /device:TPU:1, one launch (start us, length us, event | category | flops | bytes accessed | tf_op | source)
XLA Modules:
  0.0 207.3 jit_solution(10886748872643693423)
XLA Ops:
  0.6 75.6 %dispatch_rows.1 = (f32[8,768,512]{2,1,0:T(8,128)}, bf16[8,768,512]{2,1,0:T(8,128)(2,1)}, bf16[3,768,512]{2,1,0:T(8,128)(2,1)}, bf16[8,512,512]{2,1,0:T(8,128)(2...) custom-call(bf16[2,512,512]{2,1,0:T(8,128)(2,1)} %bitcast.16, ...), custom_call_target="tpu_custom_call" | custom-call | flops 40000000000 | bytes 41943040 | tf_op jit(solution)/shard_map/dispatch_rows/pallas_call | solution.py:376
  76.2 128.5 %finish_rows.1.out_ref = bf16[1792,512]{1,0:T(8,128)(2,1)} custom-call(f32[8,768,512]{2,1,0:T(8,128)} %get-tuple-element.17.dw_ref, bf16[8,768,512]{2,1,0:T(8,128)(2,1)} %get-tuple-element.18.dxs_ref, bf16[3,768,512]{2,1,0:T(8,128)(2,1)} %get-tuple-element.19.xs_ref, bf16[8,512,512]{2,1,0:T(8,128)(2,1)} %get-tuple-element.20.xf_ref, ...), custom_call_target="tpu_custom_call" | custom-call | flops 60000002048 | bytes 41943040 | tf_op jit(solution)/shard_map/finish_rows/pallas_call | solution.py:675
  204.8 2.3 %split_rows.1 = (bf16[512,512]{1,0:T(8,128)(2,1)}, bf16[512,512]{1,0:T(8,128)(2,1)}, bf16[512,256]{1,0:T(8,128)(2,1)}, bf16[512,256]{1,0:T(8,128)(2,1)}, bf16[256,512]{1,0:T(8,128)(2,1)}) custom-call(bf16[1792,512]{1,0:T(8,128)(2,1)} %finish_rows.1.out_ref), custom_call_target="tpu_custom_call" | custom-call | tf_op jit(solution)/shard_map/split_rows/pallas_call | solution.py:722

commit v6 on v5

--- a/solution.py
+++ b/solution.py
@@ -11,7 +11,8 @@
 F32 = jnp.float32
 BF16 = jnp.bfloat16
 MESH = pl.DeviceIdType.MESH
-EARLY = 5
+EARLY = (2, 3, 4, 5, 6)
+LATE = (7, 1, 0)
 
 
 def routing_rows(gates, ids, group_rank, num_local):
@@ -189,10 +190,10 @@
 
 
 def dispatch_kernel(num_stages, capacity, x_ref, ids_ref, gate_ref, dy_ref, wi_ref, wu_ref, wo_ref,
-                    dw_ref, dxs_ref, xs_ref, xf_ref, wall_ref, rgb_ref, rgf_ref,
-                    dy_buf, xb_buf, xf_buf, ids_buf, gate_buf, hot_ref, xs_buf, q_buf, wall_buf, dw_buf, dab_ref,
+                    dw_ref, dxs_ref, xs_ref, xf_ref, wall_ref, rg_ref, ids_out, gate_out,
+                    rgb_ref, dy_buf, xb_buf, xf_buf, ids_buf, gate_buf, hot_ref, xs_buf, q_buf, wall_buf, dw_buf, dab_ref,
                     send_sems, recv_sems, hop_send, hop_recv, z_send, z_recv, local_sems, dw_sems, dx_sems,
-                    xs_sems, wall_sems):
+                    xs_sems, wall_sems, xf_sems, rg_sems):
     p = Peers(num_stages)
     num_local = xs_buf.shape[0]
     width, hid = wi_ref.shape
@@ -246,10 +247,9 @@
     s_gate.last()
 
     def route_step(s, carry):
-        for mb, out in ((0, rgb_ref), (1, rgf_ref)):
-            rank, gate = routing_rows(gate_buf[s, mb], ids_buf[s, mb], p.rank, num_local)
-            out[s, 0:8] = rank
-            out[s, 8:16] = gate
+        rank, gate = routing_rows(gate_buf[s, 0], ids_buf[s, 0], p.rank, num_local)
+        rgb_ref[s, 0:8] = rank
+        rgb_ref[s, 8:16] = gate
         fill_onehot(hot_ref.at[s], rgb_ref[s, 0:8], capacity)
         return carry
 
@@ -276,6 +276,11 @@
     put_wall(1).start()
     put_wall(2).start()
     lax.fori_loop(half, TG, route_step, 0)
+    put_rg = [pltpu.make_async_copy(rgb_ref, rg_ref, rg_sems.at[0]),
+              pltpu.make_async_copy(ids_buf.at[:, 1], ids_out, rg_sems.at[1]),
+              pltpu.make_async_copy(gate_buf.at[:, 1], gate_out, rg_sems.at[2])]
+    for copy in put_rg:
+        copy.start()
     s_dy.near()
     s_dy.last()
     keep_dy.wait()
@@ -306,31 +311,40 @@
         e = expert_of(i)
         return pltpu.make_async_copy(q_buf.at[e], dxs_ref.at[e], dx_sems.at[i])
 
-    def put_xs(i):
-        return pltpu.make_async_copy(xs_buf.at[expert_of(jnp.int32(i))], xs_ref.at[7 - i], xs_sems.at[7 - i])
-
-    put_xf = pltpu.make_async_copy(xf_buf, xf_ref, local_sems.at[0])
-    for i in range(EARLY, num_local):
-        put_xs(i).start()
-        put_dx(jnp.int32(i)).start()
+    def put_xs(n):
+        return pltpu.make_async_copy(xs_buf.at[expert_of(jnp.int32(LATE[n]))], xs_ref.at[n], xs_sems.at[n])
+
+    def put_xf(j):
+        s = p.arrival(jnp.int32(j))
+        return pltpu.make_async_copy(xf_buf.at[s], xf_ref.at[s], xf_sems.at[j])
+
+    for n in range(len(LATE)):
+        put_xs(n).start()
+        put_dx(jnp.int32(LATE[n])).start()
 
     def backward_step(i, carry):
-        @pl.when(i == 1)
+        @pl.when(i == 3)
         def _():
             ring.event(10)
 
-        @pl.when(i == 2)
+        @pl.when(i == 4)
         def _():
             s_xf.forward()
+
+        @pl.when(i == 5)
+        def _():
             ring.event(11)
             put_wall(5).start()
             put_wall(6).start()
 
-        @pl.when(i == 4)
+        @pl.when(i == 6)
         def _():
+            s_xf.near()
+            for j in range(6):
+                put_xf(j).start()
             ring.event(12)
 
-        @pl.when(i >= 2)
+        @pl.when(i >= EARLY[0] + 2)
         def _():
             put_dw(i - 2).wait()
 
@@ -341,26 +355,28 @@
         put_dx(i).start()
         return carry
 
-    lax.fori_loop(0, EARLY, backward_step, 0)
-    s_xf.near()
+    lax.fori_loop(EARLY[0], EARLY[-1] + 1, backward_step, 0)
     s_xf.last()
-    put_xf.start()
+    for j in (6, 7):
+        put_xf(j).start()
     ring.event(13)
     put_wall(7).start()
-    for i in range(EARLY, num_local):
-        put_xs(i).wait()
+    for n in range(len(LATE)):
+        put_xs(n).wait()
     for i in range(num_local):
         put_dx(jnp.int32(i)).wait()
-    put_dw(jnp.int32(EARLY - 2)).wait()
-    put_dw(jnp.int32(EARLY - 1)).wait()
+    put_dw(jnp.int32(EARLY[-2])).wait()
+    put_dw(jnp.int32(EARLY[-1])).wait()
     for s in spread:
         s.finish()
     for hop in hops:
         hop.wait_send()
     ring.finish()
-    put_xf.wait()
     for i in range(num_local):
+        put_xf(i).wait()
         put_wall(i).wait()
+    for copy in put_rg:
+        copy.wait()
 
 
 def dispatch_rows(x_acts, ids, gates, dy, w_in, w_up, w_out, capacity, num_stages):
@@ -370,19 +386,20 @@
     slot_shape = jax.ShapeDtypeStruct((num_local, TG * capacity, width), BF16)
     rg_shape = jax.ShapeDtypeStruct((TG, 16, tokens), F32)
     wall_size = (num_local, width + hid, width)
-    any_spec, vmem_spec = pl.BlockSpec(memory_space=pl.ANY), pl.BlockSpec(memory_space=pltpu.VMEM)
+    any_spec = pl.BlockSpec(memory_space=pl.ANY)
     tok_buf = pltpu.VMEM((TG, tokens, width), BF16)
     slot_buf = pltpu.VMEM((num_local, TG * capacity, width), BF16)
     return pl.pallas_call(
         functools.partial(dispatch_kernel, num_stages, capacity),
         in_specs=[any_spec] * 7,
-        out_specs=[any_spec] * 5 + [vmem_spec] * 2,
+        out_specs=[any_spec] * 8,
         out_shape=[jax.ShapeDtypeStruct(wall_size, F32), slot_shape,
-                   jax.ShapeDtypeStruct((num_local - EARLY,) + slot_shape.shape[1:], BF16),
+                   jax.ShapeDtypeStruct((len(LATE),) + slot_shape.shape[1:], BF16),
                    jax.ShapeDtypeStruct((TG, tokens, width), BF16), jax.ShapeDtypeStruct(wall_size, BF16),
-                   rg_shape, rg_shape],
+                   rg_shape, jax.ShapeDtypeStruct((TG,) + ids.shape[1:], jnp.int32),
+                   jax.ShapeDtypeStruct((TG,) + ids.shape[1:], F32)],
         scratch_shapes=[
-            tok_buf, tok_buf, tok_buf, pltpu.VMEM((TG,) + ids.shape, jnp.int32),
+            pltpu.VMEM(rg_shape.shape, F32), tok_buf, tok_buf, tok_buf, pltpu.VMEM((TG,) + ids.shape, jnp.int32),
             pltpu.VMEM((TG,) + gates.shape, F32), pltpu.VMEM((TG, num_local * capacity, tokens), BF16),
             slot_buf, slot_buf, pltpu.VMEM(wall_size, BF16), pltpu.VMEM((2,) + wall_size[1:], F32),
             pltpu.VMEM((TG * capacity, 2 * hid), BF16),
@@ -390,7 +407,8 @@
             pltpu.SemaphoreType.DMA((4,)), pltpu.SemaphoreType.DMA((4,)),
             pltpu.SemaphoreType.DMA((2, 14)), pltpu.SemaphoreType.DMA((2, 14)),
             pltpu.SemaphoreType.DMA((4,)), pltpu.SemaphoreType.DMA((2,)), pltpu.SemaphoreType.DMA((num_local,)),
-            pltpu.SemaphoreType.DMA((num_local - EARLY,)), pltpu.SemaphoreType.DMA((num_local,))],
+            pltpu.SemaphoreType.DMA((len(LATE),)), pltpu.SemaphoreType.DMA((num_local,)),
+            pltpu.SemaphoreType.DMA((TG,)), pltpu.SemaphoreType.DMA((3,))],
         compiler_params=pltpu.CompilerParams(collective_id=1, has_side_effects=True,
                                              vmem_limit_bytes=63 << 20),
         cost_estimate=pl.CostEstimate(flops=40 * 10 ** 9, bytes_accessed=40 << 20, transcendentals=0),
@@ -422,7 +440,8 @@
             for way in range(2):
                 self.copies[way][i].start()
 
-    def event(self, i):
+    def event(self, k):
+        i = (2, 3, 0, 1, 6, 7, 4, 5, 10, 11, 8, 9, 12, 13)[k]
         for way in range(2):
             self.copies[way][i].wait_recv()
             if i + 4 < 14:
@@ -492,61 +511,70 @@
             copy.wait_send()
 
 
-def finish_kernel(num_stages, capacity, dw_ref, dxs_ref, xs_ref, xf_ref, wall_ref, rgb_ref, rgf_ref, out_ref,
-                  x_buf, dab_ref, part, inbox, slots, hot_ref, xf_buf, w_buf, side_out, side_in, acc, half_in, up_in, down_in,
+def finish_kernel(num_stages, capacity, dw_ref, dxs_ref, xs_ref, xf_ref, wall_ref, rg_hbm, ids_hbm, gate_hbm, out_ref,
+                  rgb_ref, rgf_ref, ids_buf, gate_buf, x_buf, dab_ref, part, inbox, slots, hot_ref, xf_buf, w_buf, side_out, side_in, acc, half_in, up_in, down_in,
                   stage_dx, stage_y, stage_dw, z_send, z_recv, dx_send, dx_recv, y_send, y_recv, hop_send, hop_recv,
-                  load_sems, slot_sems, x_sems, xf_sems, w_sems, out_sems, credit):
+                  load_sems, slot_sems, x_sems, xf_sems, w_sems, out_sems, rg_sems, credit):
     p = Peers(num_stages)
     num_local = slots.shape[0]
     tokens, width = stage_y.shape
-    late = num_local - EARLY
+    def late_number(i):
+        return 2 - i + 5 * (1 - (i + 1) // 2)
 
     def load_late(i):
-        slot, e = lax.rem(i, 2), p.expert(7 - i)
+        slot, e = lax.rem(i, 2), p.expert(late_number(i))
         return (pltpu.make_async_copy(wall_ref.at[e], w_buf.at[slot], w_sems.at[slot]),
-                pltpu.make_async_copy(xs_ref.at[i], x_buf.at[slot], x_sems.at[slot]))
+                pltpu.make_async_copy(xs_ref.at[i], x_buf.at[slot], x_sems.at[slot]),
+                pltpu.make_async_copy(dxs_ref.at[e], slots.at[e], slot_sems.at[i]))
 
     def load_slot(i):
-        e = p.expert(7 - i)
-        return pltpu.make_async_copy(dxs_ref.at[e], slots.at[e], slot_sems.at[i])
+        e = p.expert(jnp.int32(i))
+        return pltpu.make_async_copy(dxs_ref.at[e], slots.at[e], slot_sems.at[i + 1])
 
     def load_dw(i):
         e = p.expert(jnp.int32(i))
         return pltpu.make_async_copy(dw_ref.at[e], part.at[e], load_sems.at[i])
 
+    load_rg = [pltpu.make_async_copy(rg_hbm, rgb_ref, rg_sems.at[0]),
+               pltpu.make_async_copy(ids_hbm, ids_buf, rg_sems.at[1]),
+               pltpu.make_async_copy(gate_hbm, gate_buf, rg_sems.at[2])]
+    load_dw(5).start()
+    load_dw(6).start()
     for i in range(2):
-        load_slot(jnp.int32(i)).start()
         for load in load_late(jnp.int32(i)):
             load.start()
-    for i in range(2, num_local):
-        load_slot(jnp.int32(i)).start()
-    for i in range(EARLY):
-        load_dw(EARLY - 1 - i).start()
+    for load in load_rg:
+        load.start()
+    for i in EARLY:
+        load_slot(i).start()
+    for i in EARLY[:-2]:
+        load_dw(i).start()
     greet((p.up, p.down, p.partner, p.after, p.before, p.z_up, p.z_down))
     ring = GradRing(p, part, inbox, z_send, z_recv)
+
+    load_dw(5).wait()
+    load_dw(6).wait()
+    ring.start(2, 4)
 
     def late_step(i, carry):
         for load in load_late(i):
             load.wait()
-        load_slot(i).wait()
-        slot, e = lax.rem(i, 2), p.expert(7 - i)
+        slot, e = lax.rem(i, 2), p.expert(late_number(i))
         expert_step(x_buf[slot], slots[e], w_buf[slot, :width], w_buf[slot, width:], part.at[e], slots.at[e], dab_ref)
 
         @pl.when(i == 0)
         def _():
             ring.start(0, 2)
-
-        @pl.when(i + 2 < late)
-        def _():
             for load in load_late(i + 2):
                 load.start()
 
         return carry
 
-    lax.fori_loop(0, late, late_step, 0)
-    ring.start(2, 4)
-    for i in range(late, num_local):
-        load_slot(jnp.int32(i)).wait()
+    lax.fori_loop(0, len(LATE), late_step, 0)
+    for load in load_rg:
+        load.wait()
+    for i in EARLY:
+        load_slot(i).wait()
 
     def rows_of(s):
         return pl.ds(pl.multiple_of(s * capacity, 16), capacity)
@@ -569,6 +597,12 @@
     def load_w(e):
         slot = lax.rem(e, 2)
         return pltpu.make_async_copy(wall_ref.at[e], w_buf.at[slot], w_sems.at[slot])
+
+    def route_step(s, carry):
+        rank, gate = routing_rows(gate_buf[s], ids_buf[s], p.rank, num_local)
+        rgf_ref[s, 0:8] = rank
+        rgf_ref[s, 8:16] = gate
+        return carry
 
     def gather_step(s, carry):
         @pl.when(s < TG - 1)
@@ -614,9 +648,10 @@
     dx_sum.both(0)
     dx_sum.add_side(0)
     pl.semaphore_signal(credit.at[2], inc=1, device_id=p.partner, device_id_type=MESH)
-    for i in range(EARLY):
+    for i in EARLY[:-2]:
         load_dw(i).wait()
     ring.event(0)
+    lax.fori_loop(0, TG, route_step, 0)
     lax.fori_loop(0, 3, gather_step, 0)
     dx_sum.add_far()
     ring.event(1)
@@ -654,31 +689,40 @@
     stage_y[...] = y_sum.total()
     put_y = pltpu.make_async_copy(stage_y, out_ref.at[pl.ds(0, tokens)], out_sems.at[0])
     put_y.start()
-    for i in range(9, 14):
+    for i in range(9, 12):
         ring.event(i)
-    stage_dw[...] = part[ring.home].astype(BF16)
-    put_dw = pltpu.make_async_copy(stage_dw, out_ref.at[pl.ds(2 * tokens, part.shape[1])], out_sems.at[1])
-    put_dw.start()
+    puts = []
+    for i in range(2):
+        ring.event(12 + i)
+        for piece in (i, i + 2):
+            rows = pl.ds(piece * ring.rows, ring.rows)
+            stage_dw[rows] = part[ring.home, rows].astype(BF16)
+            puts.append(pltpu.make_async_copy(
+                stage_dw.at[rows], out_ref.at[pl.ds(2 * tokens + piece * ring.rows, ring.rows)],
+                out_sems.at[1 + piece]))
+            puts[-1].start()
     put_y.wait()
     hop.wait()
     y_sum.finish()
     ring.finish()
-    put_dw.wait()
-
-
-def finish_rows(dw, dxs, xs_late, xf_all, wall, rg_b, rg_f, capacity, num_stages):
+    for put in puts:
+        put.wait()
+
+
+def finish_rows(dw, dxs, xs_late, xf_all, wall, rg, ids, gates, capacity, num_stages):
     num_local, _, width = dxs.shape
-    tokens = rg_b.shape[2]
-    any_spec, vmem_spec = pl.BlockSpec(memory_space=pl.ANY), pl.BlockSpec(memory_space=pltpu.VMEM)
+    tokens = rg.shape[2]
+    any_spec = pl.BlockSpec(memory_space=pl.ANY)
     dma, quad = pltpu.SemaphoreType.DMA, pltpu.VMEM((4, tokens, width), F32)
     one = pltpu.VMEM((tokens, width), F32)
     return pl.pallas_call(
         functools.partial(finish_kernel, num_stages, capacity),
-        in_specs=[any_spec] * 5 + [vmem_spec] * 2,
+        in_specs=[any_spec] * 8,
         out_specs=any_spec,
         out_shape=jax.ShapeDtypeStruct((2 * tokens + dw.shape[1], width), BF16),
         scratch_shapes=[
-            pltpu.VMEM((2,) + dxs.shape[1:], BF16), pltpu.VMEM((dxs.shape[1], width), BF16),
+            pltpu.VMEM(rg.shape, F32), pltpu.VMEM(rg.shape, F32), pltpu.VMEM(ids.shape, jnp.int32),
+            pltpu.VMEM(gates.shape, F32), pltpu.VMEM((2,) + dxs.shape[1:], BF16), pltpu.VMEM((dxs.shape[1], width), BF16),
             pltpu.VMEM(dw.shape, F32), pltpu.VMEM((2, 14 * (dw.shape[1] // 4), width), F32),
             pltpu.VMEM(dxs.shape, BF16), pltpu.VMEM((num_local * capacity, tokens), BF16),
             pltpu.VMEM((2, tokens, width), BF16), pltpu.VMEM((2,) + wall.shape[1:], BF16),
@@ -686,13 +730,13 @@
             pltpu.VMEM((tokens, width), BF16), pltpu.VMEM((tokens, width), BF16),
             pltpu.VMEM(dw.shape[1:], BF16),
             dma((2, 14)), dma((2, 14)), dma((10,)), dma((10,)), dma((10,)), dma((10,)), dma, dma,
-            dma((EARLY,)), dma((num_local,)), dma((2,)), dma((2,)), dma((2,)), dma((2,)),
-            pltpu.SemaphoreType.REGULAR((3,))],
+            dma((num_local,)), dma((num_local,)), dma((2,)), dma((2,)), dma((2,)), dma((5,)),
+            dma((3,)), pltpu.SemaphoreType.REGULAR((3,))],
         compiler_params=pltpu.CompilerParams(collective_id=2, has_side_effects=True,
                                              vmem_limit_bytes=63 << 20),
         cost_estimate=pl.CostEstimate(flops=60 * 10 ** 9, bytes_accessed=40 << 20, transcendentals=0),
         name='finish_rows',
-    )(dw, dxs, xs_late, xf_all, wall, rg_b, rg_f)
+    )(dw, dxs, xs_late, xf_all, wall, rg, ids, gates)
 
 
 def split_kernel(out_ref, y_ref, dx_ref, wi_ref, wu_ref, wo_ref, buf, in_sems, out_sems):
@@ -739,9 +783,9 @@
 
         ids = jnp.swapaxes(expert_ids[:, 0], 1, 2)
         gates = jnp.swapaxes(gate_wts[:, 0], 1, 2)
-        dwall, dxs, xs_late, xf_all, wall, rg, rg_f = dispatch_rows(
+        dwall, dxs, xs_late, xf_all, wall, rg, ids, gates = dispatch_rows(
             x_acts[:, 0], ids, gates, d_out[0], w_in[0, 0], w_up[0, 0], w_out[0, 0], capacity, num_stages)
-        out = finish_rows(dwall, dxs, xs_late, xf_all, wall, rg, rg_f, capacity, num_stages)
+        out = finish_rows(dwall, dxs, xs_late, xf_all, wall, rg, ids, gates, capacity, num_stages)
         y, dx, dw_in, dw_up, dw_out = split_rows(out, tokens, width, hid)
         return y[None], dx[None], dw_in[None, None], dw_up[None, None], dw_out[None, None]
 

time: 208 us -> 201 us (0.966)
  Pallas kernels: 206 us -> 200 us
    pallas_call x1, Pallas kernels: 129 us -> 124 us  [finish_rows(): pl.pallas_call(functools.partial(finish_kernel, num_stages, capacity), in...]
    pallas_call x1, Pallas kernels: 75.6 us -> 73.5 us  [dispatch_rows(): pl.pallas_call(functools.partial(dispatch_kernel, num_stages, capacity),...]
where the time goes in v6:
time: 201 us
  Pallas kernels  200 us (100%)
    pallas_call x1, Pallas kernels, finish_rows(): pl.pallas_call(functools.partial(finish_kernel, num_stages, capacity), in...  124 us
    pallas_call x1, Pallas kernels, dispatch_rows(): pl.pallas_call(functools.partial(dispatch_kernel, num_stages, capacity),...  73.5 us

profile of v6, /device:TPU:1, one launch (start us, length us, event | category | flops | bytes accessed | tf_op | source)
XLA Modules:
  0.0 200.5 jit_solution(4966967172175810747)
XLA Ops:
  0.6 73.5 %dispatch_rows.1 = (f32[8,768,512]{2,1,0:T(8,128)}, bf16[8,768,512]{2,1,0:T(8,128)(2,1)}, bf16[3,768,512]{2,1,0:T(8,128)(2,1)}, bf16[8,512,512]{2,1,0:T(8,128)(2...) custom-call(bf16[2,512,512]{2,1,0:T(8,128)(2,1)} %bitcast.16, ...), custom_call_target="tpu_custom_call" | custom-call | flops 40000000000 | bytes 41943040 | tf_op jit(solution)/shard_map/dispatch_rows/pallas_call | solution.py:392
  74.1 123.9 %finish_rows.1.out_ref = bf16[1792,512]{1,0:T(8,128)(2,1)} custom-call(f32[8,768,512]{2,1,0:T(8,128)} %get-tuple-element.18.dw_ref, bf16[8,768,512]{2,1,0:T(8,128)(2,1)} %get-tuple-element.19.dxs_ref, bf16[3,768,512]{2,1,0:T(8,128)(2,1)} %get-tuple-element.20.xs_ref, bf16[8,512,512]{2,1,0:T(8,128)(2,1)} %get-tuple-element.21.xf_ref, ...), custom_call_target="tpu_custom_call" | custom-call | flops 60000002048 | bytes 41943040 | tf_op jit(solution)/shard_map/finish_rows/pallas_call | solution.py:718
  198.0 2.3 %split_rows.1 = (bf16[512,512]{1,0:T(8,128)(2,1)}, bf16[512,512]{1,0:T(8,128)(2,1)}, bf16[512,256]{1,0:T(8,128)(2,1)}, bf16[512,256]{1,0:T(8,128)(2,1)}, bf16[256,512]{1,0:T(8,128)(2,1)}) custom-call(bf16[1792,512]{1,0:T(8,128)(2,1)} %finish_rows.1.out_ref), custom_call_target="tpu_custom_call" | custom-call | tf_op jit(solution)/shard_map/split_rows/pallas_call | solution.py:766

commit v7 on v6

--- a/solution.py
+++ b/solution.py
@@ -513,11 +513,11 @@
 
 def finish_kernel(num_stages, capacity, dw_ref, dxs_ref, xs_ref, xf_ref, wall_ref, rg_hbm, ids_hbm, gate_hbm, out_ref,
                   rgb_ref, rgf_ref, ids_buf, gate_buf, x_buf, dab_ref, part, inbox, slots, hot_ref, xf_buf, w_buf, side_out, side_in, acc, half_in, up_in, down_in,
-                  stage_dx, stage_y, stage_dw, z_send, z_recv, dx_send, dx_recv, y_send, y_recv, hop_send, hop_recv,
-                  load_sems, slot_sems, x_sems, xf_sems, w_sems, out_sems, rg_sems, credit):
+                  stage_dx, land_dx, z_send, z_recv, dx_send, dx_recv, y_send, y_recv, hop_send, hop_recv,
+                  load_sems, slot_sems, x_sems, xf_sems, w_sems, rg_sems, credit):
     p = Peers(num_stages)
     num_local = slots.shape[0]
-    tokens, width = stage_y.shape
+    tokens, width = stage_dx.shape
     def late_number(i):
         return 2 - i + 5 * (1 - (i + 1) // 2)
 
@@ -661,7 +661,7 @@
     ring.event(3)
     lax.fori_loop(5, num_local, forward_step, 0)
     stage_dx[...] = dx_sum.total()
-    hop = send(stage_dx, out_ref.at[pl.ds(tokens, tokens)], hop_send, hop_recv, p.before)
+    hop = send(stage_dx, land_dx, hop_send, hop_recv, p.before)
     hop.start()
     pl.semaphore_signal(credit.at[1], inc=1, device_id=p.up, device_id_type=MESH)
     pl.semaphore_signal(credit.at[0], inc=1, device_id=p.down, device_id_type=MESH)
@@ -686,27 +686,18 @@
     ring.event(6)
     ring.event(7)
     ring.event(8)
-    stage_y[...] = y_sum.total()
-    put_y = pltpu.make_async_copy(stage_y, out_ref.at[pl.ds(0, tokens)], out_sems.at[0])
-    put_y.start()
+    out_ref[:tokens] = y_sum.total()
     for i in range(9, 12):
         ring.event(i)
-    puts = []
+    hop.wait()
+    out_ref[tokens:2 * tokens] = land_dx[...]
     for i in range(2):
         ring.event(12 + i)
         for piece in (i, i + 2):
             rows = pl.ds(piece * ring.rows, ring.rows)
-            stage_dw[rows] = part[ring.home, rows].astype(BF16)
-            puts.append(pltpu.make_async_copy(
-                stage_dw.at[rows], out_ref.at[pl.ds(2 * tokens + piece * ring.rows, ring.rows)],
-                out_sems.at[1 + piece]))
-            puts[-1].start()
-    put_y.wait()
-    hop.wait()
+            out_ref[pl.ds(2 * tokens + piece * ring.rows, ring.rows)] = part[ring.home, rows].astype(BF16)
     y_sum.finish()
     ring.finish()
-    for put in puts:
-        put.wait()
 
 
 def finish_rows(dw, dxs, xs_late, xf_all, wall, rg, ids, gates, capacity, num_stages):
@@ -718,8 +709,8 @@
     return pl.pallas_call(
         functools.partial(finish_kernel, num_stages, capacity),
         in_specs=[any_spec] * 8,
-        out_specs=any_spec,
-        out_shape=jax.ShapeDtypeStruct((2 * tokens + dw.shape[1], width), BF16),
+        out_specs=pl.BlockSpec(memory_space=pltpu.VMEM),
+        out_shape=pltpu.VMEM((2 * tokens + dw.shape[1], width), BF16),
         scratch_shapes=[
             pltpu.VMEM(rg.shape, F32), pltpu.VMEM(rg.shape, F32), pltpu.VMEM(ids.shape, jnp.int32),
             pltpu.VMEM(gates.shape, F32), pltpu.VMEM((2,) + dxs.shape[1:], BF16), pltpu.VMEM((dxs.shape[1], width), BF16),
@@ -728,47 +719,39 @@
             pltpu.VMEM((2, tokens, width), BF16), pltpu.VMEM((2,) + wall.shape[1:], BF16),
             quad, quad, quad, pltpu.VMEM((2, tokens // 2, width), F32), one, one,
             pltpu.VMEM((tokens, width), BF16), pltpu.VMEM((tokens, width), BF16),
-            pltpu.VMEM(dw.shape[1:], BF16),
             dma((2, 14)), dma((2, 14)), dma((10,)), dma((10,)), dma((10,)), dma((10,)), dma, dma,
-            dma((num_local,)), dma((num_local,)), dma((2,)), dma((2,)), dma((2,)), dma((5,)),
+            dma((num_local,)), dma((num_local,)), dma((2,)), dma((2,)), dma((2,)),
             dma((3,)), pltpu.SemaphoreType.REGULAR((3,))],
         compiler_params=pltpu.CompilerParams(collective_id=2, has_side_effects=True,
-                                             vmem_limit_bytes=63 << 20),
+                                             vmem_limit_bytes=61 << 20),
         cost_estimate=pl.CostEstimate(flops=60 * 10 ** 9, bytes_accessed=40 << 20, transcendentals=0),
         name='finish_rows',
     )(dw, dxs, xs_late, xf_all, wall, rg, ids, gates)
 
 
-def split_kernel(out_ref, y_ref, dx_ref, wi_ref, wu_ref, wo_ref, buf, in_sems, out_sems):
+def split_kernel(out_ref, y_ref, dx_ref, wi_ref, wu_ref, wo_ref, out_sems):
     tokens, (width, hid) = y_ref.shape[0], wi_ref.shape
     first = 2 * tokens
-    spans = ((0, tokens), (tokens, tokens), (first, width), (first + width, hid))
-    loads = [pltpu.make_async_copy(out_ref.at[pl.ds(lo, size)], buf.at[pl.ds(lo, size)], in_sems.at[i])
-             for i, (lo, size) in enumerate(spans)]
-    for load in loads:
-        load.start()
-    stores = []
     targets = (((0, tokens), (0, width), y_ref), ((tokens, tokens), (0, width), dx_ref),
                ((first, width), (0, hid), wi_ref), ((first, width), (hid, hid), wu_ref),
                ((first + width, hid), (0, width), wo_ref))
+    stores = []
     for i, (rows, cols, ref) in enumerate(targets):
-        if i != 3:
-            loads[min(i, 2) if i < 3 else 3].wait()
-        stores.append(pltpu.make_async_copy(buf.at[pl.ds(*rows), pl.ds(*cols)], ref, out_sems.at[i]))
+        stores.append(pltpu.make_async_copy(out_ref.at[pl.ds(*rows), pl.ds(*cols)], ref, out_sems.at[i]))
         stores[-1].start()
     for store in stores:
         store.wait()
 
 
 def split_rows(out, tokens, width, hid):
-    any_spec = pl.BlockSpec(memory_space=pl.ANY)
     shapes = ((tokens, width), (tokens, width), (width, hid), (width, hid), (hid, width))
     return pl.pallas_call(
         split_kernel,
-        in_specs=[any_spec],
-        out_specs=[any_spec] * 5,
+        in_specs=[pl.BlockSpec(memory_space=pltpu.VMEM)],
+        out_specs=[pl.BlockSpec(memory_space=pl.ANY)] * 5,
         out_shape=[jax.ShapeDtypeStruct(shape, BF16) for shape in shapes],
-        scratch_shapes=[pltpu.VMEM(out.shape, BF16), pltpu.SemaphoreType.DMA((4,)), pltpu.SemaphoreType.DMA((5,))],
+        scratch_shapes=[pltpu.SemaphoreType.DMA((5,))],
+        compiler_params=pltpu.CompilerParams(vmem_limit_bytes=32 << 20),
         name='split_rows',
     )(out)
 

time: 201 us -> 199 us (0.990)
  no operation moved by 1% of the time
where the time goes in v7:
time: 199 us
  Pallas kernels  198 us (99%)
    pallas_call x1, Pallas kernels, finish_rows(): pl.pallas_call(functools.partial(finish_kernel, num_stages, capacity), in...  123 us
    pallas_call x1, Pallas kernels, dispatch_rows(): pl.pallas_call(functools.partial(dispatch_kernel, num_stages, capacity),...  73.5 us

profile of v7, /device:TPU:1, one launch (start us, length us, event | category | flops | bytes accessed | tf_op | source)
XLA Modules:
  0.0 198.7 jit_solution(15249268757080111902)
XLA Ops:
  0.6 73.5 %dispatch_rows.1 = (f32[8,768,512]{2,1,0:T(8,128)}, bf16[8,768,512]{2,1,0:T(8,128)(2,1)}, bf16[3,768,512]{2,1,0:T(8,128)(2,1)}, bf16[8,512,512]{2,1,0:T(8,128)(2...) custom-call(bf16[2,512,512]{2,1,0:T(8,128)(2,1)} %bitcast.16, ...), custom_call_target="tpu_custom_call" | custom-call | flops 40000000000 | bytes 41943040 | tf_op jit(solution)/shard_map/dispatch_rows/pallas_call | solution.py:392
  74.1 123.1 %finish_rows.1.out_ref = bf16[1792,512]{1,0:T(8,128)(2,1)S(1)} custom-call(f32[8,768,512]{2,1,0:T(8,128)} %get-tuple-element.18.dw_ref, bf16[8,768,512]{2,1,0:T(8,128)(2,1)} %get-tuple-element.19.dxs_ref, bf16[3,768,512]{2,1,0:T(8,128)(2,1)} %get-tuple-element.20.xs_ref, bf16[8,512,512]{2,1,0:T(8,128)(2,1)} %get-tuple-element.21.xf_ref, ...), custom_call_target="tpu_custom_call" | custom-call | flops 60000002048 | bytes 41943040 | tf_op jit(solution)/shard_map/finish_rows/pallas_call | solution.py:709
  197.2 1.3 split_rows.1

commit v8 on v7

--- a/solution.py
+++ b/solution.py
@@ -538,8 +538,16 @@
     load_rg = [pltpu.make_async_copy(rg_hbm, rgb_ref, rg_sems.at[0]),
                pltpu.make_async_copy(ids_hbm, ids_buf, rg_sems.at[1]),
                pltpu.make_async_copy(gate_hbm, gate_buf, rg_sems.at[2])]
-    load_dw(5).start()
-    load_dw(6).start()
+    half = part.shape[1] // 2
+
+    def load_half(i, lo, sem):
+        e, rows = p.expert(jnp.int32(i)), pl.ds(lo, half)
+        return pltpu.make_async_copy(dw_ref.at[e, rows], part.at[e, rows], load_sems.at[sem])
+
+    first_halves = (load_half(6, half, 6), load_half(5, 0, 5))
+    second_halves = (load_half(6, 0, 1), load_half(5, half, 0))
+    for load in first_halves:
+        load.start()
     for i in range(2):
         for load in load_late(jnp.int32(i)):
             load.start()
@@ -547,13 +555,15 @@
         load.start()
     for i in EARLY:
         load_slot(i).start()
+    for load in second_halves:
+        load.start()
     for i in EARLY[:-2]:
         load_dw(i).start()
     greet((p.up, p.down, p.partner, p.after, p.before, p.z_up, p.z_down))
     ring = GradRing(p, part, inbox, z_send, z_recv)
 
-    load_dw(5).wait()
-    load_dw(6).wait()
+    for load in first_halves:
+        load.wait()
     ring.start(2, 4)
 
     def late_step(i, carry):
@@ -648,6 +658,8 @@
     dx_sum.both(0)
     dx_sum.add_side(0)
     pl.semaphore_signal(credit.at[2], inc=1, device_id=p.partner, device_id_type=MESH)
+    for load in second_halves:
+        load.wait()
     for i in EARLY[:-2]:
         load_dw(i).wait()
     ring.event(0)

time: 199 us -> 199 us (level)
  no operation moved by 1% of the time
where the time goes in v8:
time: 199 us
  Pallas kernels  198 us (99%)
    pallas_call x1, Pallas kernels, finish_rows(): pl.pallas_call(functools.partial(finish_kernel, num_stages, capacity), in...  123 us
    pallas_call x1, Pallas kernels, dispatch_rows(): pl.pallas_call(functools.partial(dispatch_kernel, num_stages, capacity),...  73.5 us

profile of v8, /device:TPU:1, one launch (start us, length us, event | category | flops | bytes accessed | tf_op | source)
XLA Modules:
  0.0 198.7 jit_solution(13984636532106995817)
XLA Ops:
  0.6 73.5 %dispatch_rows.1 = (f32[8,768,512]{2,1,0:T(8,128)}, bf16[8,768,512]{2,1,0:T(8,128)(2,1)}, bf16[3,768,512]{2,1,0:T(8,128)(2,1)}, bf16[8,512,512]{2,1,0:T(8,128)(2...) custom-call(bf16[2,512,512]{2,1,0:T(8,128)(2,1)} %bitcast.16, ...), custom_call_target="tpu_custom_call" | custom-call | flops 40000000000 | bytes 41943040 | tf_op jit(solution)/shard_map/dispatch_rows/pallas_call | solution.py:392
  74.1 123.1 %finish_rows.1.out_ref = bf16[1792,512]{1,0:T(8,128)(2,1)S(1)} custom-call(f32[8,768,512]{2,1,0:T(8,128)} %get-tuple-element.18.dw_ref, bf16[8,768,512]{2,1,0:T(8,128)(2,1)} %get-tuple-element.19.dxs_ref, bf16[3,768,512]{2,1,0:T(8,128)(2,1)} %get-tuple-element.20.xs_ref, bf16[8,512,512]{2,1,0:T(8,128)(2,1)} %get-tuple-element.21.xf_ref, ...), custom_call_target="tpu_custom_call" | custom-call | flops 60000002048 | bytes 41943040 | tf_op jit(solution)/shard_map/finish_rows/pallas_call | solution.py:721
  197.3 1.3 split_rows.1
